TPU v7x, 32 devices: a whole 2x2x4 slice. The times are simulated.
32 devices in a mesh: wide: 8 (over z, y), narrow: 4 (over x, core).
Axes of the slice: x: 2, y: 2, z: 4, core: 2. Of those that a mesh axis runs over, the one named last changes fastest.
Arguments:
- rhs: float32 [3, 32, 32, 128], P(None, 'wide', 'narrow'), may hold values from -12 to 12
- start: float32 [3, 32, 32, 128], P(None, 'wide', 'narrow'), may hold values from -2 to 2
- trans: float32 [3, 32, 32, 128], P(None, 'wide', 'narrow'), may hold values from 0.2 to 2
- accum: float32 [32, 32, 128], P('wide', 'narrow'), may hold values from 2 to 8
- coupling: float32 [3, 3, 32, 32, 128], P(None, None, 'wide', 'narrow'), may hold values from -0.3 to 0.3
- well_cells: int32 [8, 4, 64], P('wide', 'narrow'), may hold values from 0 to 4095
- well_index: float32 [8, 4, 64], P('wide', 'narrow'), may hold values from 1 to 20
- agg_map: int32 [32, 32, 128], P('wide', 'narrow'), may hold values from 0 to 31
- tile_factors: bfloat16 [48, 48, 128, 128], P('wide', 'narrow')
- coarse_inverse: float32 [1024, 1024], P(('wide', 'narrow')), as said below
Outputs:
- iterate: float32 [3, 32, 32, 128], P(None, 'wide', 'narrow')
- residual: float32 [3, 32, 32, 128], P(None, 'wide', 'narrow')
Inputs may be any that keep to these rules, and one draw needn't show every extreme that they name: well_cells names, for each device's 64 connections, one of that device's own 4 * 8 * 128 cells, counted by pair, then column, then position in the tile; connections may share a cell. agg_map names one of the 32 aggregates of the device that owns the cell. coarse_inverse is symmetric.
All inputs are finite; a program needn't handle non-finite values.
Results may differ from a plain program's by a relative error of at most 0.00095.
Values sent between devices are 32-bit elements; how exact they have to be, the bound alone decides.
No kernel may reach another device: no remote copies, remote signals or barrier semaphores. Data moves between devices by JAX's collectives and lax.ppermute only.
A program may use at most 64 MiB of HBM per device.

v0:
```python
import jax
import jax.numpy as jnp
from jax import lax
from jax.sharding import PartitionSpec as P

AGG_LOC = 32
SWEEPS = 3
INNER = 3


best_precision = lax.Precision.HIGHEST


def padded(cells, sides, width):
    for axis, dim in sides:
        count = lax.axis_size(axis)
        head = lax.slice_in_dim(cells, 0, width, axis=dim)
        tail = lax.slice_in_dim(cells, cells.shape[dim] - width, cells.shape[dim], axis=dim)
        cells = jnp.concatenate(
            [
                lax.ppermute(tail, axis, [(i, (i + 1) % count) for i in range(count)]),
                cells,
                lax.ppermute(head, axis, [((i + 1) % count, i) for i in range(count)]),
            ],
            axis=dim,
        )
    return cells


def neighbour(values, along, offset):
    along = along % values.ndim
    length = values.shape[along]
    padding = [(0, 0)] * values.ndim
    if offset > 0:
        padding[along] = (0, offset)
        return lax.slice_in_dim(jnp.pad(values, padding), offset, offset + length, axis=along)
    padding[along] = (-offset, 0)
    return lax.slice_in_dim(jnp.pad(values, padding), 0, length, axis=along)


def east_of(values):
    middle = values.shape[-1] // 2
    from_next = neighbour(values, -3, 1)[..., :middle]
    return jnp.concatenate([values[..., middle:], from_next], axis=-1)


def west_of(values):
    middle = values.shape[-1] // 2
    from_prev = neighbour(values, -3, -1)[..., middle:]
    return jnp.concatenate([from_prev, values[..., :middle]], axis=-1)


def prepare(trans, accum_w):
    middle = trans.shape[-1] // 2
    layer_no = lax.broadcasted_iota(jnp.int32, accum_w.shape, accum_w.ndim - 1) % middle
    trans_x = trans[0]
    trans_y = trans[1]
    trans_z = jnp.where(layer_no < middle - 1, trans[2], 0.0)
    face_sum = trans_x + west_of(trans_x) + trans_y + neighbour(trans_y, -2, -1)
    face_sum = face_sum + trans_z + neighbour(trans_z, -1, -1)
    return (trans_x, trans_y, trans_z, accum_w + face_sum)


def operate(values, trans_x, trans_y, trans_z, centre, coupling):
    mixing = jnp.sum(coupling * values[None], axis=1)
    inflow = trans_x * east_of(values) + west_of(trans_x) * west_of(values)
    inflow = inflow + trans_y * neighbour(values, -2, 1)
    inflow = inflow + neighbour(trans_y, -2, -1) * neighbour(values, -2, -1)
    inflow = inflow + trans_z * neighbour(values, -1, 1)
    inflow = inflow + neighbour(trans_z, -1, -1) * neighbour(values, -1, -1)
    return centre * values + mixing - inflow


def tile_apply(values, inverse_diag, factors):
    scaled = (inverse_diag * values).astype(jnp.bfloat16)
    return jnp.einsum("cpyj,pykj->cpyk", scaled, factors, preferred_element_type=jnp.float32)


def local_solve(misfit, coeffs, inverse_diag, factors):
    trans_x, trans_y, trans_z, centre, coupling = coeffs
    update = tile_apply(misfit, inverse_diag, factors)
    for _ in range(INNER - 1):
        applied = operate(update, trans_x, trans_y, trans_z, centre, coupling)
        update = update + tile_apply(misfit - applied, inverse_diag, factors)
    return update


def per_device(
    rhs,
    start,
    trans,
    accum,
    coupling,
    well_cells,
    well_index,
    agg_map,
    tile_factors,
    coarse_inverse,
):
    phases = rhs.shape[0]
    accum_flat = accum.reshape(-1).at[well_cells.reshape(-1)].add(well_index.reshape(-1))
    accum_w = accum_flat.reshape(accum.shape)
    stacked = jnp.concatenate(
        [trans, accum_w[None], coupling.reshape((phases * phases,) + accum.shape)], axis=0
    )
    stacked = jnp.concatenate([stacked, rhs], axis=0)
    rim_wide = padded(stacked, (("wide", 1),), 2)
    rim_full = padded(rim_wide, (("narrow", 2),), 3)
    trans_x, trans_y, trans_z, centre = prepare(rim_full[0:3], rim_full[3])
    coupling_full = rim_full[4:13].reshape((phases, phases) + rim_full.shape[1:])
    full_set = (trans_x, trans_y, trans_z, centre, coupling_full)
    ext_set = tuple((member[..., 1:-1, 1:-1, :] for member in full_set))
    diag_part = jnp.stack([ext_set[4][member, member] for member in range(phases)])
    inverse_diag = 1.0 / (ext_set[3][None] + diag_part)

    def extended_fn(current):
        rim_x = padded(current, (("wide", 1),), 2)
        rim_xy = padded(rim_x, (("narrow", 2),), 3)
        applied = operate(rim_xy, full_set[0], full_set[1], full_set[2], full_set[3], full_set[4])
        extended = (rim_full[13:] - applied)[..., 1:-1, 1:-1, :]
        return (extended, extended[..., 1:-1, 2:-2, :])

    groups = jnp.arange(AGG_LOC, dtype=jnp.int32)
    member_of = (groups[:, None] == agg_map.reshape(1, -1)).astype(jnp.float32)
    current = start
    for _ in range(SWEEPS):
        extended, owned_misfit = extended_fn(current)
        coarse_rhs = jnp.dot(member_of, owned_misfit[0].reshape(-1), precision=best_precision)
        coarse_all = lax.all_gather(coarse_rhs, ("wide", "narrow"), axis=0, tiled=True)
        coarse_sol = jnp.dot(coarse_inverse, coarse_all, precision=best_precision)
        update = local_solve(extended, ext_set, inverse_diag, tile_factors)[..., 1:-1, 2:-2, :]
        lifted = jnp.dot(coarse_sol, member_of, precision=best_precision).reshape(accum.shape)
        current = current + update.at[0].add(lifted)
    final_misfit = extended_fn(current)[1]
    return (current, final_misfit)


def solution(mesh):
    return jax.shard_map(
        per_device,
        mesh=mesh,
        in_specs=(
            P(None, "wide", "narrow", None),
            P(None, "wide", "narrow", None),
            P(None, "wide", "narrow", None),
            P("wide", "narrow", None),
            P(None, None, "wide", "narrow", None),
            P("wide", "narrow", None),
            P("wide", "narrow", None),
            P("wide", "narrow", None),
            P("wide", "narrow", None, None),
            P(("wide", "narrow"), None),
        ),
        out_specs=(P(None, "wide", "narrow", None), P(None, "wide", "narrow", None)),
        check_vma=False,
    )
```

profile of v0, /device:TPU:0, one launch (start us, length us, event | category | flops | bytes accessed | tf_op | source)
XLA Modules:
  0.0 226.2 jit_solution(8377544734950382462)
XLA Ops:
  1.5 1.0 copy.180
  4.9 1.0 scatter_fusion
  6.7 3.0 %collective-permute-start = (f32[16,2,8,128]{3,0,2,1:T(8,128)}, f32[16,2,8,128]{3,0,2,1:T(8,128)S(1)}, u32[]{:S(2)}, u32[]{:S(2)}) collective-permute-start(f32[16,2,8,128]{3,0,2,1:T(8,128)} %get-tuple-element.64), channel_id=1, source_target_pairs={{0,4},{4,8},{8,12},{12,16},{16,20},{20,24},{24,28},{28,0},{1,5},{5... | collective-permute-start | bytes 393224 | tf_op jit(solution)/shard_map/ppermute | solution.py:21
  9.7 3.0 %collective-permute-start.1 = (f32[16,2,8,128]{3,0,2,1:T(8,128)S(1)}, f32[16,2,8,128]{3,0,2,1:T(8,128)S(1)}, u32[]{:S(2)}, u32[]{:S(2)}) collective-permute-start(f32[16,2,8,128]{3,0,2,1:T(8,128)S(1)} %get-tuple-element.65), channel_id=1, source_target_pairs={{4,0},{8,4},{12,8},{16,12},{20,16},{24,20},{28,24},{0,28},{5,1},{9... | collective-permute-start | bytes 393224 | tf_op jit(solution)/shard_map/ppermute | solution.py:23
  12.9 4.8 %collective-permute-start.5 = (f32[3,2,8,128]{3,0,2,1:T(4,128)S(1)}, f32[3,2,8,128]{3,0,2,1:T(4,128)S(1)}, u32[]{:S(2)}, u32[]{:S(2)}) collective-permute-start(f32[3,2,8,128]{3,0,2,1:T(4,128)S(1)} %copy.305), channel_id=1, source_target_pairs={{4,0},{8,4},{12,8},{16,12},{20,16},{24,20},{28,24},{0,28},{5,1},{9... | collective-permute-start | bytes 73736 | tf_op jit(solution)/shard_map/ppermute | solution.py:23
  17.6 1.8 collective-permute-done.4
  19.6 1.7 collective-permute-start.7
  21.3 1.8 collective-permute-done.6
  23.3 1.8 collective-permute-start.2
  25.5 3.1 %collective-permute-done.2 = f32[16,8,3,128]{3,0,2,1:T(8,128)S(1)} collective-permute-done((f32[16,8,3,128]{3,0,2,1:T(8,128)S(1)}, f32[16,8,3,128]{3,0,2,1:T(8,128)S(1)}, u32[]{:S(2)}, u32[]{:S(2)}) %collective-permute-start.2) | collective-permute-done | bytes 196640 | tf_op jit(solution)/shard_map/ppermute | solution.py:21
  28.6 1.2 collective-permute-done.3
  31.1 1.3 fusion.210
  32.4 1.3 convolution_bitcast_fusion.8
  34.6 1.4 fusion.5
  36.1 1.0 fusion.218
  38.4 40.3 %all-reduce.66 = f32[1024]{0:T(1024)S(1)} all-reduce(f32[1024]{0:T(1024)S(1)} %dynamic-update-slice.9), channel_id=1, replica_groups=mesh['wide'=8,'narrow'=4] {'wide','narrow'}, use_global_device_ids=true, to_apply=%add.66 | all-reduce | flops 1024 | bytes 8192
  78.7 1.1 convolution_bitcast_fusion.13
  80.1 2.7 %fusion.4 = f32[3,6,12,128]{3,0,2,1:T(4,128)S(1)} fusion(f32[3,6,12,128]{3,0,2,1:T(4,128)S(1)} %fusion.5, bf16[6,12,128,128]{3,2,1,0:T(8,128)(2,1)S(1)} %copy-done, f32[3,6,12,64]{3,0,2,1:T(4,128)} %get-tuple-element.103, f32[3,6,12,64]{3,0,2,1:T(4,128)} %get-tuple-element.104, f32[3,6,12,64]{3,0,2,1:T(4,128)} %get-tuple-element.105, ...), kind=kOutput, calls=%fused_computation.12 | convolution fusion | flops 7741440 | bytes 4104192 | tf_op jit(solution)/shard_map/cpyj,pykj->cpyk/dot_general | solution.py:76
  83.8 2.3 %collective-permute-start.8 = (f32[3,2,8,128]{3,0,2,1:T(4,128)S(1)}, f32[3,2,8,128]{3,0,2,1:T(4,128)S(1)}, u32[]{:S(2)}, u32[]{:S(2)}) collective-permute-start(f32[3,2,8,128]{3,0,2,1:T(4,128)S(1)} %get-tuple-element.122), channel_id=1, source_target_pairs={{0,4},{4,8},{8,12},{12,16},{16,20},{20,24},{24,28},{28,0},{1,5},{5... | collective-permute-start | bytes 73736 | tf_op jit(solution)/shard_map/ppermute | solution.py:21
  86.1 2.5 %collective-permute-start.9 = (f32[3,2,8,128]{3,0,2,1:T(4,128)S(1)}, f32[3,2,8,128]{3,0,2,1:T(4,128)S(1)}, u32[]{:S(2)}, u32[]{:S(2)}) collective-permute-start(f32[3,2,8,128]{3,0,2,1:T(4,128)S(1)} %get-tuple-element.123), channel_id=1, source_target_pairs={{4,0},{8,4},{12,8},{16,12},{20,16},{24,20},{28,24},{0,28},{5,1},{9... | collective-permute-start | bytes 73736 | tf_op jit(solution)/shard_map/ppermute | solution.py:23
  88.5 1.9 collective-permute-done.8
  90.5 1.7 collective-permute-start.11
  92.3 1.8 collective-permute-done.10
  94.9 1.7 fusion.29
  96.6 1.3 convolution_bitcast_fusion.5
  98.4 2.2 fusion.3
  100.6 1.0 fusion.216
  102.9 41.2 %all-reduce.67 = f32[1024]{0:T(1024)S(1)} all-reduce(f32[1024]{0:T(1024)S(1)} %dynamic-update-slice.10), channel_id=1, replica_groups=mesh['wide'=8,'narrow'=4] {'wide','narrow'}, use_global_device_ids=true, to_apply=%add.67 | all-reduce | flops 1024 | bytes 8192
  144.1 1.1 convolution_bitcast_fusion.11
  145.2 1.0 fusion.7
  146.2 2.7 %fusion.2 = f32[3,6,12,128]{3,0,2,1:T(4,128)S(1)} fusion(f32[3,6,12,128]{3,0,2,1:T(4,128)S(1)} %fusion.3, bf16[6,12,128,128]{3,2,1,0:T(8,128)(2,1)S(1)} %copy-done, f32[3,6,12,64]{3,0,2,1:T(4,128)} %get-tuple-element.95, f32[3,6,12,64]{3,0,2,1:T(4,128)} %get-tuple-element.96, f32[3,6,12,64]{3,0,2,1:T(4,128)} %get-tuple-element.97, ...), kind=kOutput, calls=%fused_computation.7 | convolution fusion | flops 7741440 | bytes 4104192 | tf_op jit(solution)/shard_map/cpyj,pykj->cpyk/dot_general | solution.py:76
  149.1 2.3 %collective-permute-start.12 = (f32[3,2,8,128]{3,0,2,1:T(4,128)S(1)}, f32[3,2,8,128]{3,0,2,1:T(4,128)S(1)}, u32[]{:S(2)}, u32[]{:S(2)}) collective-permute-start(f32[3,2,8,128]{3,0,2,1:T(4,128)S(1)} %get-tuple-element.120), channel_id=1, source_target_pairs={{0,4},{4,8},{8,12},{12,16},{16,20},{20,24},{24,28},{28,0},{1,5},{5... | collective-permute-start | bytes 73736 | tf_op jit(solution)/shard_map/ppermute | solution.py:21
  151.4 2.5 %collective-permute-start.13 = (f32[3,2,8,128]{3,0,2,1:T(4,128)S(1)}, f32[3,2,8,128]{3,0,2,1:T(4,128)S(1)}, u32[]{:S(2)}, u32[]{:S(2)}) collective-permute-start(f32[3,2,8,128]{3,0,2,1:T(4,128)S(1)} %get-tuple-element.121), channel_id=1, source_target_pairs={{4,0},{8,4},{12,8},{16,12},{20,16},{24,20},{28,24},{0,28},{5,1},{9... | collective-permute-start | bytes 73736 | tf_op jit(solution)/shard_map/ppermute | solution.py:23
  153.9 1.9 collective-permute-done.12
  155.9 1.7 collective-permute-start.15
  157.6 1.8 collective-permute-done.14
  160.2 1.7 fusion.37
  162.0 1.3 convolution_bitcast_fusion.2
  163.7 1.4 fusion.1
  165.2 1.0 fusion.214
  167.4 41.2 %all-reduce.68 = f32[1024]{0:T(1024)S(1)} all-reduce(f32[1024]{0:T(1024)S(1)} %dynamic-update-slice.11), channel_id=1, replica_groups=mesh['wide'=8,'narrow'=4] {'wide','narrow'}, use_global_device_ids=true, to_apply=%add.68 | all-reduce | flops 1024 | bytes 8192
  208.6 1.1 convolution_bitcast_fusion.9
  210.0 2.7 %fusion = f32[3,6,12,128]{3,0,2,1:T(4,128)S(1)} fusion(f32[3,6,12,128]{3,0,2,1:T(4,128)S(1)} %fusion.1, bf16[6,12,128,128]{3,2,1,0:T(8,128)(2,1)S(1)} %copy-done, f32[3,6,12,64]{3,0,2,1:T(4,128)} %get-tuple-element.87, f32[3,6,12,64]{3,0,2,1:T(4,128)} %get-tuple-element.88, f32[3,6,12,64]{3,0,2,1:T(4,128)} %get-tuple-element.89, ...), kind=kOutput, calls=%fused_computation.2 | convolution fusion | flops 7741440 | bytes 4104192 | tf_op jit(solution)/shard_map/cpyj,pykj->cpyk/dot_general | solution.py:76
  212.9 2.3 %collective-permute-start.16 = (f32[3,2,8,128]{3,0,2,1:T(4,128)S(1)}, f32[3,2,8,128]{3,0,2,1:T(4,128)S(1)}, u32[]{:S(2)}, u32[]{:S(2)}) collective-permute-start(f32[3,2,8,128]{3,0,2,1:T(4,128)S(1)} %get-tuple-element.118), channel_id=1, source_target_pairs={{0,4},{4,8},{8,12},{12,16},{16,20},{20,24},{24,28},{28,0},{1,5},{5... | collective-permute-start | bytes 73736 | tf_op jit(solution)/shard_map/ppermute | solution.py:21
  215.2 2.5 %collective-permute-start.17 = (f32[3,2,8,128]{3,0,2,1:T(4,128)S(1)}, f32[3,2,8,128]{3,0,2,1:T(4,128)S(1)}, u32[]{:S(2)}, u32[]{:S(2)}) collective-permute-start(f32[3,2,8,128]{3,0,2,1:T(4,128)S(1)} %get-tuple-element.119), channel_id=1, source_target_pairs={{4,0},{8,4},{12,8},{16,12},{20,16},{24,20},{28,24},{0,28},{5,1},{9... | collective-permute-start | bytes 73736 | tf_op jit(solution)/shard_map/ppermute | solution.py:23
  217.7 1.9 collective-permute-done.16
  219.7 1.7 collective-permute-start.19
  224.6 1.0 fusion.184
  (221 shorter events, 18.9 us)
Async XLA Ops:
  0.6 31.8 %copy-start = (bf16[6,12,128,128]{3,2,1,0:T(8,128)(2,1)S(1)}, bf16[6,12,128,128]{3,2,1,0:T(8,128)(2,1)}, u32[]{:S(2)}) copy-start(bf16[6,12,128,128]{3,2,1,0:T(8,128)(2,1)} %param.24) | copy-start | bytes 7077892
  0.6 12.1 %copy-start.19 = (f32[3,4,8,128]{3,2,1,0:T(8,128)S(1)}, f32[3,4,8,128]{3,2,1,0:T(8,128)}, u32[]{:S(2)}) copy-start(f32[3,4,8,128]{3,2,1,0:T(8,128)} %param.17) | copy-start | bytes 147460
  6.7 16.5 %collective-permute-start = (f32[16,2,8,128]{3,0,2,1:T(8,128)}, f32[16,2,8,128]{3,0,2,1:T(8,128)S(1)}, u32[]{:S(2)}, u32[]{:S(2)}) collective-permute-start(f32[16,2,8,128]{3,0,2,1:T(8,128)} %get-tuple-element.64), channel_id=1, source_target_pairs={{0,4},{4,8},{8,12},{12,16},{16,20},{20,24},{24,28},{28,0},{1,5},{5... | collective-permute-start | bytes 393224 | tf_op jit(solution)/shard_map/ppermute | solution.py:21
  9.7 13.5 %collective-permute-start.1 = (f32[16,2,8,128]{3,0,2,1:T(8,128)S(1)}, f32[16,2,8,128]{3,0,2,1:T(8,128)S(1)}, u32[]{:S(2)}, u32[]{:S(2)}) collective-permute-start(f32[16,2,8,128]{3,0,2,1:T(8,128)S(1)} %get-tuple-element.65), channel_id=1, source_target_pairs={{4,0},{8,4},{12,8},{16,12},{20,16},{24,20},{28,24},{0,28},{5,1},{9... | collective-permute-start | bytes 393224 | tf_op jit(solution)/shard_map/ppermute | solution.py:23
  12.8 6.7 %collective-permute-start.4 = (f32[3,2,8,128]{3,0,2,1:T(4,128)S(1)}, f32[3,2,8,128]{3,0,2,1:T(4,128)S(1)}, u32[]{:S(2)}, u32[]{:S(2)}) collective-permute-start(f32[3,2,8,128]{3,0,2,1:T(4,128)S(1)} %copy.304), channel_id=1, source_target_pairs={{0,4},{4,8},{8,12},{12,16},{16,20},{20,24},{24,28},{28,0},{1,5},{5... | collective-permute-start | bytes 73736 | tf_op jit(solution)/shard_map/ppermute | solution.py:21
  12.9 6.6 %collective-permute-start.5 = (f32[3,2,8,128]{3,0,2,1:T(4,128)S(1)}, f32[3,2,8,128]{3,0,2,1:T(4,128)S(1)}, u32[]{:S(2)}, u32[]{:S(2)}) collective-permute-start(f32[3,2,8,128]{3,0,2,1:T(4,128)S(1)} %copy.305), channel_id=1, source_target_pairs={{4,0},{8,4},{12,8},{16,12},{20,16},{24,20},{28,24},{0,28},{5,1},{9... | collective-permute-start | bytes 73736 | tf_op jit(solution)/shard_map/ppermute | solution.py:23
  19.5 3.6 %collective-permute-start.6 = (f32[3,8,3,128]{3,0,2,1:T(4,128)S(1)}, f32[3,8,3,128]{3,0,2,1:T(4,128)S(1)}, u32[]{:S(2)}, u32[]{:S(2)}) collective-permute-start(f32[3,8,3,128]{3,0,2,1:T(4,128)S(1)} %get-tuple-element.116), channel_id=1, source_target_pairs={{0,1},{1,2},{2,3},{3,0},{4,5},{5,6},{6,7},{7,4},{8,9},{9,10},{10,1... | collective-permute-start | bytes 110600 | tf_op jit(solution)/shard_map/ppermute | solution.py:21
  19.6 3.5 %collective-permute-start.7 = (f32[3,8,3,128]{3,0,2,1:T(4,128)S(1)}, f32[3,8,3,128]{3,0,2,1:T(4,128)S(1)}, u32[]{:S(2)}, u32[]{:S(2)}) collective-permute-start(f32[3,8,3,128]{3,0,2,1:T(4,128)S(1)} %get-tuple-element.117), channel_id=1, source_target_pairs={{1,0},{2,1},{3,2},{0,3},{5,4},{6,5},{7,6},{4,7},{9,8},{10,9},{11,1... | collective-permute-start | bytes 110600 | tf_op jit(solution)/shard_map/ppermute | solution.py:23
  23.3 5.2 %collective-permute-start.2 = (f32[16,8,3,128]{3,0,2,1:T(8,128)S(1)}, f32[16,8,3,128]{3,0,2,1:T(8,128)S(1)}, u32[]{:S(2)}, u32[]{:S(2)}) collective-permute-start(f32[16,8,3,128]{3,0,2,1:T(8,128)S(1)} %get-tuple-element.59), channel_id=1, source_target_pairs={{0,1},{1,2},{2,3},{3,0},{4,5},{5,6},{6,7},{7,4},{8,9},{9,10},{10,1... | collective-permute-start | bytes 589832 | tf_op jit(solution)/shard_map/ppermute | solution.py:21
  25.1 4.6 %collective-permute-start.3 = (f32[16,8,3,128]{3,0,2,1:T(8,128)S(1)}, f32[16,8,3,128]{3,0,2,1:T(8,128)S(1)}, u32[]{:S(2)}, u32[]{:S(2)}) collective-permute-start(f32[16,8,3,128]{3,0,2,1:T(8,128)S(1)} %get-tuple-element.60), channel_id=1, source_target_pairs={{1,0},{2,1},{3,2},{0,3},{5,4},{6,5},{7,6},{4,7},{9,8},{10,9},{11,1... | collective-permute-start | bytes 589832 | tf_op jit(solution)/shard_map/ppermute | solution.py:23
  30.5 64.3 %copy-start.2 = (f32[8,14,128]{2,1,0:T(8,128)}, f32[8,14,128]{2,1,0:T(8,128)S(1)}, u32[]{:S(2)}) copy-start(f32[8,14,128]{2,1,0:T(8,128)S(1)} %get-tuple-element.130) | copy-start | bytes 172036
  30.9 65.6 %copy-start.4 = (f32[6,12,128]{2,1,0:T(8,128)}, f32[6,12,128]{2,1,0:T(8,128)S(1)}, u32[]{:S(2)}) copy-start(f32[6,12,128]{2,1,0:T(8,128)S(1)} %copy.186) | copy-start | bytes 110596
  31.0 3.6 %copy-start.10 = (f32[1,1,6,12,128]{4,0,3,2,1:T(1,128)}, f32[1,1,6,12,128]{4,0,3,2,1:T(1,128)S(1)}, u32[]{:S(2)}) copy-start(f32[1,1,6,12,128]{4,0,3,2,1:T(1,128)S(1)} %copy.307) | copy-start | bytes 110596
  31.1 3.5 %copy-start.13 = (f32[1,6,12,128]{3,0,2,1:T(1,128)}, f32[1,6,12,128]{3,0,2,1:T(1,128)S(1)}, u32[]{:S(2)}) copy-start(f32[1,6,12,128]{3,0,2,1:T(1,128)S(1)} %get-tuple-element.134) | copy-start | bytes 110596
  31.1 3.5 %copy-start.16 = (f32[1,6,12,128]{3,0,2,1:T(1,128)}, f32[1,6,12,128]{3,0,2,1:T(1,128)S(1)}, u32[]{:S(2)}) copy-start(f32[1,6,12,128]{3,0,2,1:T(1,128)S(1)} %get-tuple-element.135) | copy-start | bytes 110596
  32.4 4.6 %copy-start.7 = (f32[3,8,14,128]{3,0,2,1:T(4,128)}, f32[3,8,14,128]{3,0,2,1:T(4,128)S(1)}, u32[]{:S(2)}) copy-start(f32[3,8,14,128]{3,0,2,1:T(4,128)S(1)} %get-tuple-element.53) | copy-start | bytes 516100
  34.1 1.9 copy-start.20
  34.2 1.8 copy-start.23
  34.6 3.2 %copy-start.38 = (s32[4,8,128]{2,1,0:T(8,128)S(1)}, s32[4,8,128]{2,1,0:T(8,128)}, u32[]{:S(2)}) copy-start(s32[4,8,128]{2,1,0:T(8,128)} %param.23) | copy-start | bytes 49156
  83.8 6.7 %collective-permute-start.8 = (f32[3,2,8,128]{3,0,2,1:T(4,128)S(1)}, f32[3,2,8,128]{3,0,2,1:T(4,128)S(1)}, u32[]{:S(2)}, u32[]{:S(2)}) collective-permute-start(f32[3,2,8,128]{3,0,2,1:T(4,128)S(1)} %get-tuple-element.122), channel_id=1, source_target_pairs={{0,4},{4,8},{8,12},{12,16},{16,20},{20,24},{24,28},{28,0},{1,5},{5... | collective-permute-start | bytes 73736 | tf_op jit(solution)/shard_map/ppermute | solution.py:21
  86.1 4.3 %collective-permute-start.9 = (f32[3,2,8,128]{3,0,2,1:T(4,128)S(1)}, f32[3,2,8,128]{3,0,2,1:T(4,128)S(1)}, u32[]{:S(2)}, u32[]{:S(2)}) collective-permute-start(f32[3,2,8,128]{3,0,2,1:T(4,128)S(1)} %get-tuple-element.123), channel_id=1, source_target_pairs={{4,0},{8,4},{12,8},{16,12},{20,16},{24,20},{28,24},{0,28},{5,1},{9... | collective-permute-start | bytes 73736 | tf_op jit(solution)/shard_map/ppermute | solution.py:23
  90.5 3.6 %collective-permute-start.10 = (f32[3,8,3,128]{3,0,2,1:T(4,128)S(1)}, f32[3,8,3,128]{3,0,2,1:T(4,128)S(1)}, u32[]{:S(2)}, u32[]{:S(2)}) collective-permute-start(f32[3,8,3,128]{3,0,2,1:T(4,128)S(1)} %get-tuple-element.114), channel_id=1, source_target_pairs={{0,1},{1,2},{2,3},{3,0},{4,5},{5,6},{6,7},{7,4},{8,9},{9,10},{10,1... | collective-permute-start | bytes 110600 | tf_op jit(solution)/shard_map/ppermute | solution.py:21
  90.5 3.8 %collective-permute-start.11 = (f32[3,8,3,128]{3,0,2,1:T(4,128)S(1)}, f32[3,8,3,128]{3,0,2,1:T(4,128)S(1)}, u32[]{:S(2)}, u32[]{:S(2)}) collective-permute-start(f32[3,8,3,128]{3,0,2,1:T(4,128)S(1)} %get-tuple-element.115), channel_id=1, source_target_pairs={{1,0},{2,1},{3,2},{0,3},{5,4},{6,5},{7,6},{4,7},{9,8},{10,9},{11,1... | collective-permute-start | bytes 110600 | tf_op jit(solution)/shard_map/ppermute | solution.py:23
  94.5 2.1 copy-start.11
  94.5 2.1 copy-start.14
  94.5 2.1 copy-start.17
  96.6 5.0 %copy-start.9 = (f32[3,8,14,128]{3,0,2,1:T(4,128)}, f32[3,8,14,128]{3,0,2,1:T(4,128)S(1)}, u32[]{:S(2)}) copy-start(f32[3,8,14,128]{3,0,2,1:T(4,128)S(1)} %fusion.29) | copy-start | bytes 516100
  96.6 1.7 copy-start.21
  96.6 1.7 copy-start.24
  96.6 1.7 copy-start.27
  98.4 4.0 %copy-start.39 = (s32[4,8,128]{2,1,0:T(8,128)S(1)}, s32[4,8,128]{2,1,0:T(8,128)}, u32[]{:S(2)}) copy-start(s32[4,8,128]{2,1,0:T(8,128)} %param.23) | copy-start | bytes 49156
  100.6 45.7 %copy-start.5 = (f32[6,12,128]{2,1,0:T(8,128)S(1)}, f32[6,12,128]{2,1,0:T(8,128)}, u32[]{:S(2)}) copy-start(f32[6,12,128]{2,1,0:T(8,128)} %copy-done.4) | copy-start | bytes 110596
  148.9 11.3 %copy-start.3 = (f32[8,14,128]{2,1,0:T(8,128)S(1)}, f32[8,14,128]{2,1,0:T(8,128)}, u32[]{:S(2)}) copy-start(f32[8,14,128]{2,1,0:T(8,128)} %copy-done.2) | copy-start | bytes 172036
  149.1 6.7 %collective-permute-start.12 = (f32[3,2,8,128]{3,0,2,1:T(4,128)S(1)}, f32[3,2,8,128]{3,0,2,1:T(4,128)S(1)}, u32[]{:S(2)}, u32[]{:S(2)}) collective-permute-start(f32[3,2,8,128]{3,0,2,1:T(4,128)S(1)} %get-tuple-element.120), channel_id=1, source_target_pairs={{0,4},{4,8},{8,12},{12,16},{16,20},{20,24},{24,28},{28,0},{1,5},{5... | collective-permute-start | bytes 73736 | tf_op jit(solution)/shard_map/ppermute | solution.py:21
  151.4 4.3 %collective-permute-start.13 = (f32[3,2,8,128]{3,0,2,1:T(4,128)S(1)}, f32[3,2,8,128]{3,0,2,1:T(4,128)S(1)}, u32[]{:S(2)}, u32[]{:S(2)}) collective-permute-start(f32[3,2,8,128]{3,0,2,1:T(4,128)S(1)} %get-tuple-element.121), channel_id=1, source_target_pairs={{4,0},{8,4},{12,8},{16,12},{20,16},{24,20},{28,24},{0,28},{5,1},{9... | collective-permute-start | bytes 73736 | tf_op jit(solution)/shard_map/ppermute | solution.py:23
  155.8 3.6 %collective-permute-start.14 = (f32[3,8,3,128]{3,0,2,1:T(4,128)S(1)}, f32[3,8,3,128]{3,0,2,1:T(4,128)S(1)}, u32[]{:S(2)}, u32[]{:S(2)}) collective-permute-start(f32[3,8,3,128]{3,0,2,1:T(4,128)S(1)} %get-tuple-element.112), channel_id=1, source_target_pairs={{0,1},{1,2},{2,3},{3,0},{4,5},{5,6},{6,7},{7,4},{8,9},{9,10},{10,1... | collective-permute-start | bytes 110600 | tf_op jit(solution)/shard_map/ppermute | solution.py:21
  155.9 3.8 %collective-permute-start.15 = (f32[3,8,3,128]{3,0,2,1:T(4,128)S(1)}, f32[3,8,3,128]{3,0,2,1:T(4,128)S(1)}, u32[]{:S(2)}, u32[]{:S(2)}) collective-permute-start(f32[3,8,3,128]{3,0,2,1:T(4,128)S(1)} %get-tuple-element.113), channel_id=1, source_target_pairs={{1,0},{2,1},{3,2},{0,3},{5,4},{6,5},{7,6},{4,7},{9,8},{10,9},{11,1... | collective-permute-start | bytes 110600 | tf_op jit(solution)/shard_map/ppermute | solution.py:23
  159.8 2.1 copy-start.6
  159.8 2.1 copy-start.12
  159.8 2.1 copy-start.15
  159.8 2.1 copy-start.18
  161.9 4.2 %copy-start.8 = (f32[3,8,14,128]{3,0,2,1:T(4,128)}, f32[3,8,14,128]{3,0,2,1:T(4,128)S(1)}, u32[]{:S(2)}) copy-start(f32[3,8,14,128]{3,0,2,1:T(4,128)S(1)} %fusion.37) | copy-start | bytes 516100
  161.9 1.7 copy-start.22
  163.7 3.2 %copy-start.40 = (s32[4,8,128]{2,1,0:T(8,128)S(1)}, s32[4,8,128]{2,1,0:T(8,128)}, u32[]{:S(2)}) copy-start(s32[4,8,128]{2,1,0:T(8,128)} %param.23) | copy-start | bytes 49156
  212.9 6.7 %collective-permute-start.16 = (f32[3,2,8,128]{3,0,2,1:T(4,128)S(1)}, f32[3,2,8,128]{3,0,2,1:T(4,128)S(1)}, u32[]{:S(2)}, u32[]{:S(2)}) collective-permute-start(f32[3,2,8,128]{3,0,2,1:T(4,128)S(1)} %get-tuple-element.118), channel_id=1, source_target_pairs={{0,4},{4,8},{8,12},{12,16},{16,20},{20,24},{24,28},{28,0},{1,5},{5... | collective-permute-start | bytes 73736 | tf_op jit(solution)/shard_map/ppermute | solution.py:21
  215.2 4.3 %collective-permute-start.17 = (f32[3,2,8,128]{3,0,2,1:T(4,128)S(1)}, f32[3,2,8,128]{3,0,2,1:T(4,128)S(1)}, u32[]{:S(2)}, u32[]{:S(2)}) collective-permute-start(f32[3,2,8,128]{3,0,2,1:T(4,128)S(1)} %get-tuple-element.119), channel_id=1, source_target_pairs={{4,0},{8,4},{12,8},{16,12},{20,16},{24,20},{28,24},{0,28},{5,1},{9... | collective-permute-start | bytes 73736 | tf_op jit(solution)/shard_map/ppermute | solution.py:23
  219.6 3.6 %collective-permute-start.18 = (f32[3,8,3,128]{3,0,2,1:T(4,128)S(1)}, f32[3,8,3,128]{3,0,2,1:T(4,128)S(1)}, u32[]{:S(2)}, u32[]{:S(2)}) collective-permute-start(f32[3,8,3,128]{3,0,2,1:T(4,128)S(1)} %get-tuple-element.110), channel_id=1, source_target_pairs={{0,1},{1,2},{2,3},{3,0},{4,5},{5,6},{6,7},{7,4},{8,9},{9,10},{10,1... | collective-permute-start | bytes 110600 | tf_op jit(solution)/shard_map/ppermute | solution.py:21
  219.7 3.8 %collective-permute-start.19 = (f32[3,8,3,128]{3,0,2,1:T(4,128)S(1)}, f32[3,8,3,128]{3,0,2,1:T(4,128)S(1)}, u32[]{:S(2)}, u32[]{:S(2)}) collective-permute-start(f32[3,8,3,128]{3,0,2,1:T(4,128)S(1)} %get-tuple-element.111), channel_id=1, source_target_pairs={{1,0},{2,1},{3,2},{0,3},{5,4},{6,5},{7,6},{4,7},{9,8},{10,9},{11,1... | collective-permute-start | bytes 110600 | tf_op jit(solution)/shard_map/ppermute | solution.py:23
  (13 other events, 21.4 us)
where the time goes:
time: 229 us; the launch traced here: 226 us
  blocking collectives  123 us (54%)
  starting transfers between devices  34.2 us (15%)
  matrix products  22.9 us (10%)
  waiting for transfers between devices  18.4 us (8%)
  local copies, waits for them, and re-layouts  13.6 us (6%)
  other arithmetic  12.5 us (5%)
    unnamed x3, blocking collectives  123 us
    ppermute x10, starting transfers between devices, padded(): lax.ppermute(head, axis, [((i + 1) % count, i) for i in range(count)])  22.1 us
    dot_general x9, matrix products, tile_apply(): jnp.einsum('cpyj,pykj->cpyk', scaled, factors, preferred_element_type=jnp...  17 us
    ppermute x10, waiting for transfers between devices, padded(): lax.ppermute(tail, axis, [(i, (i + 1) % count) for i in range(count)])  16.2 us
    ppermute x10, starting transfers between devices, padded(): lax.ppermute(tail, axis, [(i, (i + 1) % count) for i in range(count)])  12.1 us
    unnamed x98, local copies, waits for them, and re-layouts  4.69 us
  transfers between devices with their start and end apart: 20, of which 13 were waited for; matrix products, arithmetic and copies ran while one was open for 1% of the time, Pallas kernels for 0%

commit v1 on v0

--- a/solution.py
+++ b/solution.py
@@ -11,19 +11,25 @@
 best_precision = lax.Precision.HIGHEST
 
 
+def halos(tail, head, axis):
+    count = lax.axis_size(axis)
+    if count % 2:
+        low = lax.ppermute(tail, axis, [(i, (i + 1) % count) for i in range(count)])
+        high = lax.ppermute(head, axis, [((i + 1) % count, i) for i in range(count)])
+        return low, high
+    even = lax.axis_index(axis) % 2 == 0
+    first = lax.ppermute(jnp.where(even, tail, head), axis, [(i, i ^ 1) for i in range(count)])
+    other = [(i, (i - 1 if i % 2 == 0 else i + 1) % count) for i in range(count)]
+    second = lax.ppermute(jnp.where(even, head, tail), axis, other)
+    return jnp.where(even, second, first), jnp.where(even, first, second)
+
+
 def padded(cells, sides, width):
     for axis, dim in sides:
-        count = lax.axis_size(axis)
         head = lax.slice_in_dim(cells, 0, width, axis=dim)
         tail = lax.slice_in_dim(cells, cells.shape[dim] - width, cells.shape[dim], axis=dim)
-        cells = jnp.concatenate(
-            [
-                lax.ppermute(tail, axis, [(i, (i + 1) % count) for i in range(count)]),
-                cells,
-                lax.ppermute(head, axis, [((i + 1) % count, i) for i in range(count)]),
-            ],
-            axis=dim,
-        )
+        low, high = halos(tail, head, axis)
+        cells = jnp.concatenate([low, cells, high], axis=dim)
     return cells
 
 
@@ -98,6 +104,7 @@
     coarse_inverse,
 ):
     phases = rhs.shape[0]
+    devices = lax.axis_size("wide") * lax.axis_size("narrow")
     accum_flat = accum.reshape(-1).at[well_cells.reshape(-1)].add(well_index.reshape(-1))
     accum_w = accum_flat.reshape(accum.shape)
     stacked = jnp.concatenate(
@@ -126,7 +133,8 @@
     for _ in range(SWEEPS):
         extended, owned_misfit = extended_fn(current)
         coarse_rhs = jnp.dot(member_of, owned_misfit[0].reshape(-1), precision=best_precision)
-        coarse_all = lax.all_gather(coarse_rhs, ("wide", "narrow"), axis=0, tiled=True)
+        copies = jnp.broadcast_to(coarse_rhs, (devices,) + coarse_rhs.shape)
+        coarse_all = lax.all_to_all(copies, ("wide", "narrow"), 0, 0, tiled=True).reshape(-1)
         coarse_sol = jnp.dot(coarse_inverse, coarse_all, precision=best_precision)
         update = local_solve(extended, ext_set, inverse_diag, tile_factors)[..., 1:-1, 2:-2, :]
         lifted = jnp.dot(coarse_sol, member_of, precision=best_precision).reshape(accum.shape)

time: 229 us -> 136 us (0.59)
  blocking collectives: 123 us -> 0 us
  waiting for transfers between devices: 18.4 us -> 45.2 us
  starting transfers between devices: 34.2 us -> 28.7 us
  other arithmetic: 12.5 us -> 17.9 us
  local copies, waits for them, and re-layouts: 13.6 us -> 17.1 us
    unnamed x3 -> x0, blocking collectives: 123 us -> none
    ppermute x20, waiting for transfers between devices: 18.4 us -> 33.7 us  [the longest x10 32.6 us: halos(): second = lax.ppermute(jnp.where(even, head, tail), axis, other)]
    ppermute x20, starting transfers between devices: 34.2 us -> 20 us  [the longest x10 13.3 us: halos(): second = lax.ppermute(jnp.where(even, head, tail), axis, other)]
    all_to_all x0 -> x3, waiting for transfers between devices: none -> 11.5 us  [per_device(): lax.all_to_all(copies, ('wide', 'narrow'), 0, 0, tiled=True).reshape(-1)]
    all_to_all x0 -> x3, starting transfers between devices: none -> 8.75 us  [per_device(): lax.all_to_all(copies, ('wide', 'narrow'), 0, 0, tiled=True).reshape(-1)]
    add x6, other arithmetic: 0.95 us -> 3.49 us  [per_device(): current = current + update.at[0].add(lifted)]
    unnamed x98 -> x95, local copies, waits for them, and re-layouts: 4.69 us -> 6.1 us
  transfers between devices with their start and end apart: 20 -> 23, of which waited for: 13 -> 13; matrix products, arithmetic and copies ran while one was open for 1% -> 7% of each run, Pallas kernels for 0% -> 0%
where the time goes in v1:
time: 136 us; the launch traced here: 135 us
  waiting for transfers between devices  45.2 us (33%)
  starting transfers between devices  28.7 us (21%)
  matrix products  24.4 us (18%)
  other arithmetic  17.9 us (13%)
  local copies, waits for them, and re-layouts  17.1 us (13%)
  between operations  1.95 us (1%)
    ppermute x10, waiting for transfers between devices, halos(): second = lax.ppermute(jnp.where(even, head, tail), axis, other)  32.6 us
    dot_general x9, matrix products, tile_apply(): jnp.einsum('cpyj,pykj->cpyk', scaled, factors, preferred_element_type=jnp...  17 us
    ppermute x10, starting transfers between devices, halos(): second = lax.ppermute(jnp.where(even, head, tail), axis, other)  13.3 us
    all_to_all x3, waiting for transfers between devices, per_device(): lax.all_to_all(copies, ('wide', 'narrow'), 0, 0, tiled=True).reshape(-1)  11.5 us
    all_to_all x3, starting transfers between devices, per_device(): lax.all_to_all(copies, ('wide', 'narrow'), 0, 0, tiled=True).reshape(-1)  8.75 us
    ppermute x10, starting transfers between devices, halos(): lax.ppermute(jnp.where(even, tail, head), axis, [(i, i ^ 1) for i in rang...  6.62 us
    unnamed x95, local copies, waits for them, and re-layouts  6.1 us
    sub x3, other arithmetic, extended_fn(): extended = (rim_full[13:] - applied)[..., 1:-1, 1:-1, :]  4.23 us
  transfers between devices with their start and end apart: 23, of which 13 were waited for; matrix products, arithmetic and copies ran while one was open for 7% of the time, Pallas kernels for 0%

profile of v1, /device:TPU:0, one launch (start us, length us, event | category | flops | bytes accessed | tf_op | source)
XLA Modules:
  0.0 135.2 jit_solution(12250236395324469209)
XLA Ops:
  0.7 0.9 copy.310
  1.5 1.0 copy.180
  4.9 1.0 scatter_fusion
  6.7 6.0 %collective-permute-start = (f32[16,2,8,128]{3,0,2,1:T(8,128)}, f32[16,2,8,128]{3,0,2,1:T(8,128)S(1)}, u32[]{:S(2)}, u32[]{:S(2)}) collective-permute-start(f32[16,2,8,128]{3,0,2,1:T(8,128)} %get-tuple-element.69), channel_id=1, source_target_pairs={{0,28},{4,8},{8,4},{12,16},{16,12},{20,24},{24,20},{28,0},{1,29},{... | collective-permute-start | bytes 393224 | tf_op jit(solution)/shard_map/ppermute | solution.py:23
  12.8 2.0 %collective-permute-start.4 = (f32[3,2,8,128]{3,0,2,1:T(4,128)S(1)}, f32[3,2,8,128]{3,0,2,1:T(4,128)S(1)}, u32[]{:S(2)}, u32[]{:S(2)}) collective-permute-start(f32[3,2,8,128]{3,0,2,1:T(4,128)S(1)} %get-tuple-element.145), channel_id=1, source_target_pairs={{0,28},{4,8},{8,4},{12,16},{16,12},{20,24},{24,20},{28,0},{1,29},{... | collective-permute-start | bytes 73736 | tf_op jit(solution)/shard_map/ppermute | solution.py:23
  15.0 4.6 %collective-permute-done.4 = f32[3,2,8,128]{3,0,2,1:T(4,128)S(1)} collective-permute-done((f32[3,2,8,128]{3,0,2,1:T(4,128)S(1)}, f32[3,2,8,128]{3,0,2,1:T(4,128)S(1)}, u32[]{:S(2)}, u32[]{:S(2)}) %collective-permute-start.4) | collective-permute-done | bytes 24608 | tf_op jit(solution)/shard_map/ppermute | solution.py:23
  19.6 1.1 collective-permute-done.5
  20.7 1.2 collective-permute-start.6
  22.4 2.2 %collective-permute-done.6 = f32[3,8,3,128]{3,0,2,1:T(4,128)S(1)} collective-permute-done((f32[3,8,3,128]{3,0,2,1:T(4,128)S(1)}, f32[3,8,3,128]{3,0,2,1:T(4,128)S(1)}, u32[]{:S(2)}, u32[]{:S(2)}) %collective-permute-start.6) | collective-permute-done | bytes 36896 | tf_op jit(solution)/shard_map/ppermute | solution.py:23
  25.1 1.5 %collective-permute-start.2 = (f32[16,8,3,128]{3,0,2,1:T(8,128)S(1)}, f32[16,8,3,128]{3,0,2,1:T(8,128)S(1)}, u32[]{:S(2)}, u32[]{:S(2)}) collective-permute-start(f32[16,8,3,128]{3,0,2,1:T(8,128)S(1)} %get-tuple-element.52), channel_id=1, source_target_pairs={{0,3},{1,2},{2,1},{3,0},{4,7},{5,6},{6,5},{7,4},{8,11},{9,10},{10,... | collective-permute-start | bytes 589832 | tf_op jit(solution)/shard_map/ppermute | solution.py:23
  26.9 4.8 %collective-permute-done.2 = f32[16,8,3,128]{3,0,2,1:T(8,128)S(1)} collective-permute-done((f32[16,8,3,128]{3,0,2,1:T(8,128)S(1)}, f32[16,8,3,128]{3,0,2,1:T(8,128)S(1)}, u32[]{:S(2)}, u32[]{:S(2)}) %collective-permute-start.2) | collective-permute-done | bytes 196640 | tf_op jit(solution)/shard_map/ppermute | solution.py:23
  33.1 1.3 fusion.210
  34.4 1.3 convolution_bitcast_fusion.8
  36.6 1.4 %fusion.5 = f32[3,6,12,128]{3,0,2,1:T(4,128)S(1)} fusion(f32[3,6,12,128]{3,0,2,1:T(4,128)S(1)} %convolution_bitcast_fusion.8, bf16[6,12,128,128]{3,2,1,0:T(8,128)(2,1)S(1)} %copy-done, f32[3,6,12,64]{3,0,2,1:T(4,128)S(1)} %get-tuple-element.112, f32[3,6,12,64]{3,0,2,1:T(4,128)S(1)} %get-tuple-element.113, f32[3,6,12,64]{3,0,2,1:T(4,128)S(1)} %get-tuple-element.114, ...), kind=kOutput, calls=%fused_computation.14 | convolution fusion | flops 7741440 | bytes 4104192 | tf_op jit(solution)/shard_map/cpyj,pykj->cpyk/dot_general | solution.py:82
  38.1 0.9 fusion.217
  40.8 3.0 %all-to-all-start = ((f32[32,1,32]{2,1,0:T(1,128)}), f32[32,1,32]{2,1,0:T(1,128)S(1)}, u32[]{:S(2)}, u32[]{:S(2)}) async-start(f32[32,1,32]{2,1,0:T(1,128)} %broadcast_in_dim.14), calls=%async_computation | async-start | bytes 32768 | tf_op jit(solution)/shard_map/all_to_all | solution.py:137
  43.8 2.7 %fusion.4 = f32[3,6,12,128]{3,0,2,1:T(4,128)S(1)} fusion(f32[3,6,12,128]{3,0,2,1:T(4,128)S(1)} %fusion.5, bf16[6,12,128,128]{3,2,1,0:T(8,128)(2,1)S(1)} %copy-done, f32[3,6,12,64]{3,0,2,1:T(4,128)} %get-tuple-element.108, f32[3,6,12,64]{3,0,2,1:T(4,128)} %get-tuple-element.109, f32[3,6,12,64]{3,0,2,1:T(4,128)} %get-tuple-element.110, ...), kind=kOutput, calls=%fused_computation.12 | convolution fusion | flops 7741440 | bytes 4104192 | tf_op jit(solution)/shard_map/cpyj,pykj->cpyk/dot_general | solution.py:82
  47.1 3.8 %all-to-all-done = f32[32,1,32]{2,1,0:T(1,128)S(1)} async-done(((f32[32,1,32]{2,1,0:T(1,128)}), f32[32,1,32]{2,1,0:T(1,128)S(1)}, u32[]{:S(2)}, u32[]{:S(2)}) %all-to-all-start) | async-done | bytes 4128 | tf_op jit(solution)/shard_map/all_to_all | solution.py:137
  52.3 1.1 convolution_bitcast_fusion.13
  53.4 1.0 fusion.8
  57.2 1.3 collective-permute-start.9
  58.5 4.6 %collective-permute-done.8 = f32[3,2,8,128]{3,0,2,1:T(4,128)S(1)} collective-permute-done((f32[3,2,8,128]{3,0,2,1:T(4,128)S(1)}, f32[3,2,8,128]{3,0,2,1:T(4,128)S(1)}, u32[]{:S(2)}, u32[]{:S(2)}) %collective-permute-start.8) | collective-permute-done | bytes 24608 | tf_op jit(solution)/shard_map/ppermute | solution.py:23
  63.9 2.9 %collective-permute-done.10 = f32[3,8,3,128]{3,0,2,1:T(4,128)S(1)} collective-permute-done((f32[3,8,3,128]{3,0,2,1:T(4,128)S(1)}, f32[3,8,3,128]{3,0,2,1:T(4,128)S(1)}, u32[]{:S(2)}, u32[]{:S(2)}) %collective-permute-start.10) | collective-permute-done | bytes 36896 | tf_op jit(solution)/shard_map/ppermute | solution.py:23
  67.3 1.6 %fusion.29 = f32[3,8,14,128]{3,0,2,1:T(4,128)S(1)} fusion(f32[3,8,14,128]{3,0,2,1:T(4,128)S(1)} %pad_maximum_fusion.3, f32[3,8,14,64]{3,0,2,1:T(4,128)S(1)} %get-tuple-element.85, f32[3,8,14,64]{3,0,2,1:T(4,128)S(1)} %get-tuple-element.86, f32[3,8,14,64]{3,0,2,1:T(4,128)S(1)} %get-tuple-element.84, f32[3,8,14,64]{3,0,2,1:T(4,128)S(1)} %get-tuple-element.83, ...), kind=kLoop, calls=%fused_computation.94 | loop fusion | flops 731136 | bytes 1433600 | tf_op jit(solution)/shard_map/sub | solution.py:127
  69.0 1.3 convolution_bitcast_fusion.5
  70.8 2.3 %fusion.3 = f32[3,6,12,128]{3,0,2,1:T(4,128)S(1)} fusion(f32[3,6,12,128]{3,0,2,1:T(4,128)S(1)} %convolution_bitcast_fusion.5, bf16[6,12,128,128]{3,2,1,0:T(8,128)(2,1)S(1)} %copy-done, f32[3,6,12,64]{3,0,2,1:T(4,128)S(1)} %get-tuple-element.104, f32[3,6,12,64]{3,0,2,1:T(4,128)S(1)} %get-tuple-element.105, f32[3,6,12,64]{3,0,2,1:T(4,128)S(1)} %get-tuple-element.106, ...), kind=kOutput, calls=%fused_computation.9 | convolution fusion | flops 7741440 | bytes 4091904 | tf_op jit(solution)/shard_map/cpyj,pykj->cpyk/dot_general | solution.py:82
  73.1 0.9 fusion.215
  75.8 2.8 %all-to-all-start.1 = ((f32[32,1,32]{2,1,0:T(1,128)}), f32[32,1,32]{2,1,0:T(1,128)S(1)}, u32[]{:S(2)}, u32[]{:S(2)}) async-start(f32[32,1,32]{2,1,0:T(1,128)} %broadcast_in_dim.15), calls=%async_computation.1 | async-start | bytes 32768 | tf_op jit(solution)/shard_map/all_to_all | solution.py:137
  78.6 2.7 %fusion.2 = f32[3,6,12,128]{3,0,2,1:T(4,128)S(1)} fusion(f32[3,6,12,128]{3,0,2,1:T(4,128)S(1)} %fusion.3, bf16[6,12,128,128]{3,2,1,0:T(8,128)(2,1)S(1)} %copy-done, f32[3,6,12,64]{3,0,2,1:T(4,128)} %get-tuple-element.100, f32[3,6,12,64]{3,0,2,1:T(4,128)} %get-tuple-element.101, f32[3,6,12,64]{3,0,2,1:T(4,128)} %get-tuple-element.102, ...), kind=kOutput, calls=%fused_computation.7 | convolution fusion | flops 7741440 | bytes 4104192 | tf_op jit(solution)/shard_map/cpyj,pykj->cpyk/dot_general | solution.py:82
  82.0 3.8 %all-to-all-done.1 = f32[32,1,32]{2,1,0:T(1,128)S(1)} async-done(((f32[32,1,32]{2,1,0:T(1,128)}), f32[32,1,32]{2,1,0:T(1,128)S(1)}, u32[]{:S(2)}, u32[]{:S(2)}) %all-to-all-start.1) | async-done | bytes 4128 | tf_op jit(solution)/shard_map/all_to_all | solution.py:137
  86.6 1.1 convolution_bitcast_fusion.11
  87.6 1.0 fusion.7
  90.5 1.3 collective-permute-start.13
  91.8 4.6 %collective-permute-done.12 = f32[3,2,8,128]{3,0,2,1:T(4,128)S(1)} collective-permute-done((f32[3,2,8,128]{3,0,2,1:T(4,128)S(1)}, f32[3,2,8,128]{3,0,2,1:T(4,128)S(1)}, u32[]{:S(2)}, u32[]{:S(2)}) %collective-permute-start.12) | collective-permute-done | bytes 24608 | tf_op jit(solution)/shard_map/ppermute | solution.py:23
  97.1 2.9 %collective-permute-done.14 = f32[3,8,3,128]{3,0,2,1:T(4,128)S(1)} collective-permute-done((f32[3,8,3,128]{3,0,2,1:T(4,128)S(1)}, f32[3,8,3,128]{3,0,2,1:T(4,128)S(1)}, u32[]{:S(2)}, u32[]{:S(2)}) %collective-permute-start.14) | collective-permute-done | bytes 36896 | tf_op jit(solution)/shard_map/ppermute | solution.py:23
  100.5 1.6 %fusion.37 = f32[3,8,14,128]{3,0,2,1:T(4,128)S(1)} fusion(f32[3,8,14,128]{3,0,2,1:T(4,128)S(1)} %pad_maximum_fusion.4, f32[3,8,14,64]{3,0,2,1:T(4,128)S(1)} %get-tuple-element.81, f32[3,8,14,64]{3,0,2,1:T(4,128)S(1)} %get-tuple-element.82, f32[3,8,14,64]{3,0,2,1:T(4,128)S(1)} %get-tuple-element.80, f32[3,8,14,64]{3,0,2,1:T(4,128)S(1)} %get-tuple-element.79, ...), kind=kLoop, calls=%fused_computation.102 | loop fusion | flops 731136 | bytes 1433600 | tf_op jit(solution)/shard_map/sub | solution.py:127
  102.3 1.3 convolution_bitcast_fusion.2
  104.0 1.4 %fusion.1 = f32[3,6,12,128]{3,0,2,1:T(4,128)S(1)} fusion(f32[3,6,12,128]{3,0,2,1:T(4,128)S(1)} %convolution_bitcast_fusion.2, bf16[6,12,128,128]{3,2,1,0:T(8,128)(2,1)S(1)} %copy-done, f32[3,6,12,64]{3,0,2,1:T(4,128)S(1)} %get-tuple-element.96, f32[3,6,12,64]{3,0,2,1:T(4,128)S(1)} %get-tuple-element.97, f32[3,6,12,64]{3,0,2,1:T(4,128)S(1)} %get-tuple-element.98, ...), kind=kOutput, calls=%fused_computation.4 | convolution fusion | flops 7741440 | bytes 4104192 | tf_op jit(solution)/shard_map/cpyj,pykj->cpyk/dot_general | solution.py:82
  105.5 1.0 fusion.213
  108.2 2.9 %all-to-all-start.2 = ((f32[32,1,32]{2,1,0:T(1,128)}), f32[32,1,32]{2,1,0:T(1,128)S(1)}, u32[]{:S(2)}, u32[]{:S(2)}) async-start(f32[32,1,32]{2,1,0:T(1,128)} %broadcast_in_dim.16), calls=%async_computation.2 | async-start | bytes 32768 | tf_op jit(solution)/shard_map/all_to_all | solution.py:137
  111.1 2.7 %fusion = f32[3,6,12,128]{3,0,2,1:T(4,128)S(1)} fusion(f32[3,6,12,128]{3,0,2,1:T(4,128)S(1)} %fusion.1, bf16[6,12,128,128]{3,2,1,0:T(8,128)(2,1)S(1)} %copy-done, f32[3,6,12,64]{3,0,2,1:T(4,128)} %get-tuple-element.92, f32[3,6,12,64]{3,0,2,1:T(4,128)} %get-tuple-element.93, f32[3,6,12,64]{3,0,2,1:T(4,128)} %get-tuple-element.94, ...), kind=kOutput, calls=%fused_computation.2 | convolution fusion | flops 7741440 | bytes 4104192 | tf_op jit(solution)/shard_map/cpyj,pykj->cpyk/dot_general | solution.py:82
  114.5 3.8 %all-to-all-done.2 = f32[32,1,32]{2,1,0:T(1,128)S(1)} async-done(((f32[32,1,32]{2,1,0:T(1,128)}), f32[32,1,32]{2,1,0:T(1,128)S(1)}, u32[]{:S(2)}, u32[]{:S(2)}) %all-to-all-start.2) | async-done | bytes 4128 | tf_op jit(solution)/shard_map/all_to_all | solution.py:137
  119.1 1.1 convolution_bitcast_fusion.9
  120.1 1.0 fusion.6
  123.0 1.3 collective-permute-start.17
  124.3 4.6 %collective-permute-done.16 = f32[3,2,8,128]{3,0,2,1:T(4,128)S(1)} collective-permute-done((f32[3,2,8,128]{3,0,2,1:T(4,128)S(1)}, f32[3,2,8,128]{3,0,2,1:T(4,128)S(1)}, u32[]{:S(2)}, u32[]{:S(2)}) %collective-permute-start.16) | collective-permute-done | bytes 24608 | tf_op jit(solution)/shard_map/ppermute | solution.py:23
  131.0 1.5 %collective-permute-done.18 = f32[3,8,3,128]{3,0,2,1:T(4,128)S(1)} collective-permute-done((f32[3,8,3,128]{3,0,2,1:T(4,128)S(1)}, f32[3,8,3,128]{3,0,2,1:T(4,128)S(1)}, u32[]{:S(2)}, u32[]{:S(2)}) %collective-permute-start.18) | collective-permute-done | bytes 36896 | tf_op jit(solution)/shard_map/ppermute | solution.py:23
  133.6 1.0 fusion.184
  (241 shorter events, 30.2 us)
Async XLA Ops:
  0.6 33.8 %copy-start = (bf16[6,12,128,128]{3,2,1,0:T(8,128)(2,1)S(1)}, bf16[6,12,128,128]{3,2,1,0:T(8,128)(2,1)}, u32[]{:S(2)}) copy-start(bf16[6,12,128,128]{3,2,1,0:T(8,128)(2,1)} %param.24) | copy-start | bytes 7077892
  0.6 12.1 %copy-start.19 = (f32[3,4,8,128]{3,2,1,0:T(8,128)S(1)}, f32[3,4,8,128]{3,2,1,0:T(8,128)}, u32[]{:S(2)}) copy-start(f32[3,4,8,128]{3,2,1,0:T(8,128)} %param.17) | copy-start | bytes 147460
  6.7 18.0 %collective-permute-start = (f32[16,2,8,128]{3,0,2,1:T(8,128)}, f32[16,2,8,128]{3,0,2,1:T(8,128)S(1)}, u32[]{:S(2)}, u32[]{:S(2)}) collective-permute-start(f32[16,2,8,128]{3,0,2,1:T(8,128)} %get-tuple-element.69), channel_id=1, source_target_pairs={{0,28},{4,8},{8,4},{12,16},{16,12},{20,24},{24,20},{28,0},{1,29},{... | collective-permute-start | bytes 393224 | tf_op jit(solution)/shard_map/ppermute | solution.py:23
  12.7 12.0 %collective-permute-start.1 = (f32[16,2,8,128]{3,0,2,1:T(8,128)S(1)}, f32[16,2,8,128]{3,0,2,1:T(8,128)S(1)}, u32[]{:S(2)}, u32[]{:S(2)}) collective-permute-start(f32[16,2,8,128]{3,0,2,1:T(8,128)S(1)} %get-tuple-element.70), channel_id=1, source_target_pairs={{0,4},{4,0},{8,12},{12,8},{16,20},{20,16},{24,28},{28,24},{1,5},{5... | collective-permute-start | bytes 393224 | tf_op jit(solution)/shard_map/ppermute | solution.py:21
  12.8 6.8 %collective-permute-start.4 = (f32[3,2,8,128]{3,0,2,1:T(4,128)S(1)}, f32[3,2,8,128]{3,0,2,1:T(4,128)S(1)}, u32[]{:S(2)}, u32[]{:S(2)}) collective-permute-start(f32[3,2,8,128]{3,0,2,1:T(4,128)S(1)} %get-tuple-element.145), channel_id=1, source_target_pairs={{0,28},{4,8},{8,4},{12,16},{16,12},{20,24},{24,20},{28,0},{1,29},{... | collective-permute-start | bytes 73736 | tf_op jit(solution)/shard_map/ppermute | solution.py:23
  14.8 5.9 %collective-permute-start.5 = (f32[3,2,8,128]{3,0,2,1:T(4,128)S(1)}, f32[3,2,8,128]{3,0,2,1:T(4,128)S(1)}, u32[]{:S(2)}, u32[]{:S(2)}) collective-permute-start(f32[3,2,8,128]{3,0,2,1:T(4,128)S(1)} %get-tuple-element.146), channel_id=1, source_target_pairs={{0,4},{4,0},{8,12},{12,8},{16,20},{20,16},{24,28},{28,24},{1,5},{5... | collective-permute-start | bytes 73736 | tf_op jit(solution)/shard_map/ppermute | solution.py:21
  20.7 3.9 %collective-permute-start.6 = (f32[3,8,3,128]{3,0,2,1:T(4,128)S(1)}, f32[3,8,3,128]{3,0,2,1:T(4,128)S(1)}, u32[]{:S(2)}, u32[]{:S(2)}) collective-permute-start(f32[3,8,3,128]{3,0,2,1:T(4,128)S(1)} %get-tuple-element.121), channel_id=1, source_target_pairs={{0,3},{1,2},{2,1},{3,0},{4,7},{5,6},{6,5},{7,4},{8,11},{9,10},{10,... | collective-permute-start | bytes 110600 | tf_op jit(solution)/shard_map/ppermute | solution.py:23
  21.9 2.7 %collective-permute-start.7 = (f32[3,8,3,128]{3,0,2,1:T(4,128)S(1)}, f32[3,8,3,128]{3,0,2,1:T(4,128)S(1)}, u32[]{:S(2)}, u32[]{:S(2)}) collective-permute-start(f32[3,8,3,128]{3,0,2,1:T(4,128)S(1)} %get-tuple-element.122), channel_id=1, source_target_pairs={{0,1},{1,0},{2,3},{3,2},{4,5},{5,4},{6,7},{7,6},{8,9},{9,8},{10,11... | collective-permute-start | bytes 110600 | tf_op jit(solution)/shard_map/ppermute | solution.py:21
  24.9 2.0 %collective-permute-start.3 = (f32[16,8,3,128]{3,0,2,1:T(8,128)S(1)}, f32[16,8,3,128]{3,0,2,1:T(8,128)S(1)}, u32[]{:S(2)}, u32[]{:S(2)}) collective-permute-start(f32[16,8,3,128]{3,0,2,1:T(8,128)S(1)} %broadcast_select_fusion.3), channel_id=1, source_target_pairs={{0,1},{1,0},{2,3},{3,2},{4,5},{5,4},{6,7},{7,6},{8,9},{9,8},{10,11... | collective-permute-start | bytes 589832 | tf_op jit(solution)/shard_map/ppermute | solution.py:21
  25.1 6.6 %collective-permute-start.2 = (f32[16,8,3,128]{3,0,2,1:T(8,128)S(1)}, f32[16,8,3,128]{3,0,2,1:T(8,128)S(1)}, u32[]{:S(2)}, u32[]{:S(2)}) collective-permute-start(f32[16,8,3,128]{3,0,2,1:T(8,128)S(1)} %get-tuple-element.52), channel_id=1, source_target_pairs={{0,3},{1,2},{2,1},{3,0},{4,7},{5,6},{6,5},{7,4},{8,11},{9,10},{10,... | collective-permute-start | bytes 589832 | tf_op jit(solution)/shard_map/ppermute | solution.py:23
  32.9 34.3 %copy-start.2 = (f32[8,14,128]{2,1,0:T(8,128)}, f32[8,14,128]{2,1,0:T(8,128)S(1)}, u32[]{:S(2)}) copy-start(f32[8,14,128]{2,1,0:T(8,128)S(1)} %copy.200) | copy-start | bytes 172036
  33.0 35.9 %copy-start.4 = (f32[6,12,128]{2,1,0:T(8,128)}, f32[6,12,128]{2,1,0:T(8,128)S(1)}, u32[]{:S(2)}) copy-start(f32[6,12,128]{2,1,0:T(8,128)S(1)} %copy.186) | copy-start | bytes 110596
  33.0 3.5 %copy-start.10 = (f32[1,1,6,12,128]{4,0,3,2,1:T(1,128)}, f32[1,1,6,12,128]{4,0,3,2,1:T(1,128)S(1)}, u32[]{:S(2)}) copy-start(f32[1,1,6,12,128]{4,0,3,2,1:T(1,128)S(1)} %copy.304) | copy-start | bytes 110596
  33.1 3.4 %copy-start.13 = (f32[1,6,12,128]{3,0,2,1:T(1,128)}, f32[1,6,12,128]{3,0,2,1:T(1,128)S(1)}, u32[]{:S(2)}) copy-start(f32[1,6,12,128]{3,0,2,1:T(1,128)S(1)} %get-tuple-element.155) | copy-start | bytes 110596
  33.1 3.4 %copy-start.16 = (f32[1,6,12,128]{3,0,2,1:T(1,128)}, f32[1,6,12,128]{3,0,2,1:T(1,128)S(1)}, u32[]{:S(2)}) copy-start(f32[1,6,12,128]{3,0,2,1:T(1,128)S(1)} %get-tuple-element.156) | copy-start | bytes 110596
  34.4 4.6 %copy-start.7 = (f32[3,8,14,128]{3,0,2,1:T(4,128)}, f32[3,8,14,128]{3,0,2,1:T(4,128)S(1)}, u32[]{:S(2)}) copy-start(f32[3,8,14,128]{3,0,2,1:T(4,128)S(1)} %get-tuple-element.56) | copy-start | bytes 516100
  36.1 1.9 %copy-start.20 = (f32[6,12,128]{2,1,0:T(8,128)}, f32[6,12,128]{2,1,0:T(8,128)S(1)}, u32[]{:S(2)}) copy-start(f32[6,12,128]{2,1,0:T(8,128)S(1)} %copy.206) | copy-start | bytes 110596
  36.2 1.8 %copy-start.23 = (f32[6,12,128]{2,1,0:T(8,128)}, f32[6,12,128]{2,1,0:T(8,128)S(1)}, u32[]{:S(2)}) copy-start(f32[6,12,128]{2,1,0:T(8,128)S(1)} %copy.208) | copy-start | bytes 110596
  36.6 3.2 %copy-start.41 = (s32[4,8,128]{2,1,0:T(8,128)S(1)}, s32[4,8,128]{2,1,0:T(8,128)}, u32[]{:S(2)}) copy-start(s32[4,8,128]{2,1,0:T(8,128)} %param.23) | copy-start | bytes 49156
  40.8 10.2 %all-to-all-start = ((f32[32,1,32]{2,1,0:T(1,128)}), f32[32,1,32]{2,1,0:T(1,128)S(1)}, u32[]{:S(2)}, u32[]{:S(2)}) async-start(f32[32,1,32]{2,1,0:T(1,128)} %broadcast_in_dim.14), calls=%async_computation | async-start | bytes 32768 | tf_op jit(solution)/shard_map/all_to_all | solution.py:137
  56.4 6.7 %collective-permute-start.8 = (f32[3,2,8,128]{3,0,2,1:T(4,128)S(1)}, f32[3,2,8,128]{3,0,2,1:T(4,128)S(1)}, u32[]{:S(2)}, u32[]{:S(2)}) collective-permute-start(f32[3,2,8,128]{3,0,2,1:T(4,128)S(1)} %get-tuple-element.141), channel_id=1, source_target_pairs={{0,28},{4,8},{8,4},{12,16},{16,12},{20,24},{24,20},{28,0},{1,29},{... | collective-permute-start | bytes 73736 | tf_op jit(solution)/shard_map/ppermute | solution.py:23
  57.2 5.9 %collective-permute-start.9 = (f32[3,2,8,128]{3,0,2,1:T(4,128)S(1)}, f32[3,2,8,128]{3,0,2,1:T(4,128)S(1)}, u32[]{:S(2)}, u32[]{:S(2)}) collective-permute-start(f32[3,2,8,128]{3,0,2,1:T(4,128)S(1)} %get-tuple-element.142), channel_id=1, source_target_pairs={{0,4},{4,0},{8,12},{12,8},{16,20},{20,16},{24,28},{28,24},{1,5},{5... | collective-permute-start | bytes 73736 | tf_op jit(solution)/shard_map/ppermute | solution.py:21
  63.2 3.6 %collective-permute-start.10 = (f32[3,8,3,128]{3,0,2,1:T(4,128)S(1)}, f32[3,8,3,128]{3,0,2,1:T(4,128)S(1)}, u32[]{:S(2)}, u32[]{:S(2)}) collective-permute-start(f32[3,8,3,128]{3,0,2,1:T(4,128)S(1)} %get-tuple-element.119), channel_id=1, source_target_pairs={{0,3},{1,2},{2,1},{3,0},{4,7},{5,6},{6,5},{7,4},{8,11},{9,10},{10,... | collective-permute-start | bytes 110600 | tf_op jit(solution)/shard_map/ppermute | solution.py:23
  63.2 3.5 %collective-permute-start.11 = (f32[3,8,3,128]{3,0,2,1:T(4,128)S(1)}, f32[3,8,3,128]{3,0,2,1:T(4,128)S(1)}, u32[]{:S(2)}, u32[]{:S(2)}) collective-permute-start(f32[3,8,3,128]{3,0,2,1:T(4,128)S(1)} %get-tuple-element.120), channel_id=1, source_target_pairs={{0,1},{1,0},{2,3},{3,2},{4,5},{5,4},{6,7},{7,6},{8,9},{9,8},{10,11... | collective-permute-start | bytes 110600 | tf_op jit(solution)/shard_map/ppermute | solution.py:21
  66.9 2.0 %copy-start.11 = (f32[1,1,6,12,128]{4,0,3,2,1:T(1,128)S(1)}, f32[1,1,6,12,128]{4,0,3,2,1:T(1,128)}, u32[]{:S(2)}) copy-start(f32[1,1,6,12,128]{4,0,3,2,1:T(1,128)} %copy-done.10) | copy-start | bytes 110596
  66.9 2.0 %copy-start.14 = (f32[1,6,12,128]{3,0,2,1:T(1,128)S(1)}, f32[1,6,12,128]{3,0,2,1:T(1,128)}, u32[]{:S(2)}) copy-start(f32[1,6,12,128]{3,0,2,1:T(1,128)} %copy-done.13) | copy-start | bytes 110596
  66.9 2.0 %copy-start.17 = (f32[1,6,12,128]{3,0,2,1:T(1,128)S(1)}, f32[1,6,12,128]{3,0,2,1:T(1,128)}, u32[]{:S(2)}) copy-start(f32[1,6,12,128]{3,0,2,1:T(1,128)} %copy-done.16) | copy-start | bytes 110596
  68.9 5.1 %copy-start.9 = (f32[3,8,14,128]{3,0,2,1:T(4,128)}, f32[3,8,14,128]{3,0,2,1:T(4,128)S(1)}, u32[]{:S(2)}) copy-start(f32[3,8,14,128]{3,0,2,1:T(4,128)S(1)} %fusion.29) | copy-start | bytes 516100
  69.0 1.7 %copy-start.21 = (f32[6,12,128]{2,1,0:T(8,128)S(1)}, f32[6,12,128]{2,1,0:T(8,128)}, u32[]{:S(2)}) copy-start(f32[6,12,128]{2,1,0:T(8,128)} %copy-done.20) | copy-start | bytes 110596
  70.7 4.1 %copy-start.42 = (s32[4,8,128]{2,1,0:T(8,128)S(1)}, s32[4,8,128]{2,1,0:T(8,128)}, u32[]{:S(2)}) copy-start(s32[4,8,128]{2,1,0:T(8,128)} %param.23) | copy-start | bytes 49156
  70.8 7.9 %copy-start.5 = (f32[6,12,128]{2,1,0:T(8,128)S(1)}, f32[6,12,128]{2,1,0:T(8,128)}, u32[]{:S(2)}) copy-start(f32[6,12,128]{2,1,0:T(8,128)} %copy-done.4) | copy-start | bytes 110596
  75.8 10.0 %all-to-all-start.1 = ((f32[32,1,32]{2,1,0:T(1,128)}), f32[32,1,32]{2,1,0:T(1,128)S(1)}, u32[]{:S(2)}, u32[]{:S(2)}) async-start(f32[32,1,32]{2,1,0:T(1,128)} %broadcast_in_dim.15), calls=%async_computation.1 | async-start | bytes 32768 | tf_op jit(solution)/shard_map/all_to_all | solution.py:137
  82.0 18.6 %copy-start.3 = (f32[8,14,128]{2,1,0:T(8,128)S(1)}, f32[8,14,128]{2,1,0:T(8,128)}, u32[]{:S(2)}) copy-start(f32[8,14,128]{2,1,0:T(8,128)} %copy-done.2) | copy-start | bytes 172036
  89.7 6.7 %collective-permute-start.12 = (f32[3,2,8,128]{3,0,2,1:T(4,128)S(1)}, f32[3,2,8,128]{3,0,2,1:T(4,128)S(1)}, u32[]{:S(2)}, u32[]{:S(2)}) collective-permute-start(f32[3,2,8,128]{3,0,2,1:T(4,128)S(1)} %get-tuple-element.137), channel_id=1, source_target_pairs={{0,28},{4,8},{8,4},{12,16},{16,12},{20,24},{24,20},{28,0},{1,29},{... | collective-permute-start | bytes 73736 | tf_op jit(solution)/shard_map/ppermute | solution.py:23
  90.5 5.8 %collective-permute-start.13 = (f32[3,2,8,128]{3,0,2,1:T(4,128)S(1)}, f32[3,2,8,128]{3,0,2,1:T(4,128)S(1)}, u32[]{:S(2)}, u32[]{:S(2)}) collective-permute-start(f32[3,2,8,128]{3,0,2,1:T(4,128)S(1)} %get-tuple-element.138), channel_id=1, source_target_pairs={{0,4},{4,0},{8,12},{12,8},{16,20},{20,16},{24,28},{28,24},{1,5},{5... | collective-permute-start | bytes 73736 | tf_op jit(solution)/shard_map/ppermute | solution.py:21
  96.4 3.6 %collective-permute-start.14 = (f32[3,8,3,128]{3,0,2,1:T(4,128)S(1)}, f32[3,8,3,128]{3,0,2,1:T(4,128)S(1)}, u32[]{:S(2)}, u32[]{:S(2)}) collective-permute-start(f32[3,8,3,128]{3,0,2,1:T(4,128)S(1)} %get-tuple-element.117), channel_id=1, source_target_pairs={{0,3},{1,2},{2,1},{3,0},{4,7},{5,6},{6,5},{7,4},{8,11},{9,10},{10,... | collective-permute-start | bytes 110600 | tf_op jit(solution)/shard_map/ppermute | solution.py:23
  96.5 3.5 %collective-permute-start.15 = (f32[3,8,3,128]{3,0,2,1:T(4,128)S(1)}, f32[3,8,3,128]{3,0,2,1:T(4,128)S(1)}, u32[]{:S(2)}, u32[]{:S(2)}) collective-permute-start(f32[3,8,3,128]{3,0,2,1:T(4,128)S(1)} %get-tuple-element.118), channel_id=1, source_target_pairs={{0,1},{1,0},{2,3},{3,2},{4,5},{5,4},{6,7},{7,6},{8,9},{9,8},{10,11... | collective-permute-start | bytes 110600 | tf_op jit(solution)/shard_map/ppermute | solution.py:21
  100.1 2.0 %copy-start.6 = (f32[6,12,128]{2,1,0:T(8,128)S(1)}, f32[6,12,128]{2,1,0:T(8,128)}, u32[]{:S(2)}) copy-start(f32[6,12,128]{2,1,0:T(8,128)} %copy-done.4) | copy-start | bytes 110596
  100.2 2.0 %copy-start.12 = (f32[1,1,6,12,128]{4,0,3,2,1:T(1,128)S(1)}, f32[1,1,6,12,128]{4,0,3,2,1:T(1,128)}, u32[]{:S(2)}) copy-start(f32[1,1,6,12,128]{4,0,3,2,1:T(1,128)} %copy-done.10) | copy-start | bytes 110596
  100.2 2.0 %copy-start.15 = (f32[1,6,12,128]{3,0,2,1:T(1,128)S(1)}, f32[1,6,12,128]{3,0,2,1:T(1,128)}, u32[]{:S(2)}) copy-start(f32[1,6,12,128]{3,0,2,1:T(1,128)} %copy-done.13) | copy-start | bytes 110596
  100.2 2.0 %copy-start.18 = (f32[1,6,12,128]{3,0,2,1:T(1,128)S(1)}, f32[1,6,12,128]{3,0,2,1:T(1,128)}, u32[]{:S(2)}) copy-start(f32[1,6,12,128]{3,0,2,1:T(1,128)} %copy-done.16) | copy-start | bytes 110596
  102.2 4.3 %copy-start.8 = (f32[3,8,14,128]{3,0,2,1:T(4,128)}, f32[3,8,14,128]{3,0,2,1:T(4,128)S(1)}, u32[]{:S(2)}) copy-start(f32[3,8,14,128]{3,0,2,1:T(4,128)S(1)} %fusion.37) | copy-start | bytes 516100
  104.0 3.2 %copy-start.43 = (s32[4,8,128]{2,1,0:T(8,128)S(1)}, s32[4,8,128]{2,1,0:T(8,128)}, u32[]{:S(2)}) copy-start(s32[4,8,128]{2,1,0:T(8,128)} %param.23) | copy-start | bytes 49156
  108.2 10.1 %all-to-all-start.2 = ((f32[32,1,32]{2,1,0:T(1,128)}), f32[32,1,32]{2,1,0:T(1,128)S(1)}, u32[]{:S(2)}, u32[]{:S(2)}) async-start(f32[32,1,32]{2,1,0:T(1,128)} %broadcast_in_dim.16), calls=%async_computation.2 | async-start | bytes 32768 | tf_op jit(solution)/shard_map/all_to_all | solution.py:137
  122.2 6.7 %collective-permute-start.16 = (f32[3,2,8,128]{3,0,2,1:T(4,128)S(1)}, f32[3,2,8,128]{3,0,2,1:T(4,128)S(1)}, u32[]{:S(2)}, u32[]{:S(2)}) collective-permute-start(f32[3,2,8,128]{3,0,2,1:T(4,128)S(1)} %get-tuple-element.133), channel_id=1, source_target_pairs={{0,28},{4,8},{8,4},{12,16},{16,12},{20,24},{24,20},{28,0},{1,29},{... | collective-permute-start | bytes 73736 | tf_op jit(solution)/shard_map/ppermute | solution.py:23
  123.0 5.9 %collective-permute-start.17 = (f32[3,2,8,128]{3,0,2,1:T(4,128)S(1)}, f32[3,2,8,128]{3,0,2,1:T(4,128)S(1)}, u32[]{:S(2)}, u32[]{:S(2)}) collective-permute-start(f32[3,2,8,128]{3,0,2,1:T(4,128)S(1)} %get-tuple-element.134), channel_id=1, source_target_pairs={{0,4},{4,0},{8,12},{12,8},{16,20},{20,16},{24,28},{28,24},{1,5},{5... | collective-permute-start | bytes 73736 | tf_op jit(solution)/shard_map/ppermute | solution.py:21
  128.9 3.6 %collective-permute-start.18 = (f32[3,8,3,128]{3,0,2,1:T(4,128)S(1)}, f32[3,8,3,128]{3,0,2,1:T(4,128)S(1)}, u32[]{:S(2)}, u32[]{:S(2)}) collective-permute-start(f32[3,8,3,128]{3,0,2,1:T(4,128)S(1)} %get-tuple-element.115), channel_id=1, source_target_pairs={{0,3},{1,2},{2,1},{3,0},{4,7},{5,6},{6,5},{7,4},{8,11},{9,10},{10,... | collective-permute-start | bytes 110600 | tf_op jit(solution)/shard_map/ppermute | solution.py:23
  129.0 3.5 %collective-permute-start.19 = (f32[3,8,3,128]{3,0,2,1:T(4,128)S(1)}, f32[3,8,3,128]{3,0,2,1:T(4,128)S(1)}, u32[]{:S(2)}, u32[]{:S(2)}) collective-permute-start(f32[3,8,3,128]{3,0,2,1:T(4,128)S(1)} %get-tuple-element.116), channel_id=1, source_target_pairs={{0,1},{1,0},{2,3},{3,2},{4,5},{5,4},{6,7},{7,6},{8,9},{9,8},{10,11... | collective-permute-start | bytes 110600 | tf_op jit(solution)/shard_map/ppermute | solution.py:21
  (19 other events, 28.7 us)

commit v2 on v0

v2 whole, which is shorter than its diff:
```python
import functools

import jax
import jax.numpy as jnp
from jax import lax
from jax.experimental import pallas as pl
from jax.experimental.pallas import tpu as pltpu
from jax.sharding import PartitionSpec as P

AGG_LOC = 32
SWEEPS = 3
INNER = 3
HX = 2
HY = 3

TX, TY, TZ, ACC, CPL, RHS, CUR, IDX, FIELDS = 0, 1, 2, 3, 4, 13, 16, 19, 20
OUTER_X = (TX, CUR, CUR + 1, CUR + 2, IDX)
OUTER_Y = (TY, CUR, CUR + 1, CUR + 2, IDX)
GC, GI, GR, GFIELDS = 3, 12, 15, 18

PARAMS = pltpu.CompilerParams(vmem_limit_bytes=16 * 1024 * 1024)


HBM = pl.BlockSpec(memory_space=pltpu.HBM)
VMEM = pl.BlockSpec(memory_space=pltpu.VMEM)


def call(body, outs, scratch=(), far=(), far_outs=()):
    def run(flags, *args):
        specs = [pl.BlockSpec(memory_space=pltpu.SMEM)]
        specs += [HBM if number in far else VMEM for number in range(len(args))]
        args = [
            pltpu.with_memory_space_constraint(arg, pltpu.HBM) if number in far else arg
            for number, arg in enumerate(args)
        ]
        return pl.pallas_call(
            body,
            out_shape=tuple(
                (pltpu.HBM if number in far_outs else jax.ShapeDtypeStruct)(*out) for number, out in enumerate(outs)
            ),
            in_specs=specs,
            out_specs=tuple(HBM if number in far_outs else VMEM for number in range(len(outs))),
            scratch_shapes=list(scratch),
            compiler_params=PARAMS,
            name=body.func.__name__ if isinstance(body, functools.partial) else body.__name__,
        )(flags, *args)

    return run


def rows_of(ref):
    size = 1
    for length in ref.shape[:-1]:
        size *= length
    return ref.reshape(size, ref.shape[-1])


def sent(flags, axis, tail, head):
    low_first = flags[2 * axis] == 0
    return jnp.where(low_first, tail, head), jnp.where(low_first, head, tail)


def received(flags, axis, first, second):
    swapped = flags[2 * axis + 1] == 0
    return jnp.where(swapped, second, first), jnp.where(swapped, first, second)


def split3(values):
    high = values.astype(jnp.bfloat16)
    rest = values - high.astype(jnp.float32)
    middle = rest.astype(jnp.bfloat16)
    low = (rest - middle.astype(jnp.float32)).astype(jnp.bfloat16)
    return high, middle, low


def nt_dot(left, right):
    return lax.dot_general(left, right, (((1,), (1,)), ((), ())), preferred_element_type=jnp.float32)


def pack_wide(flags, trans, accum, coupling, rhs, start, agg, far_cells, far_index, block, first, second, groups, cells, index, sems):
    phases, px, cy, tile = rhs.shape
    conn = cells.shape[-1]
    copies = [
        (far_cells, cells),
        (far_index, index),
        (accum, block.at[ACC]),
        (agg, groups),
        (trans, block.at[pl.ds(TX, 3)]),
        (rhs, block.at[pl.ds(RHS, phases)]),
        (start, block.at[pl.ds(CUR, phases)]),
    ]
    copies += [(coupling.at[c], block.at[pl.ds(CPL + c * phases, phases)]) for c in range(phases)]
    copies = [pltpu.make_async_copy(source, target, sems.at[k]) for k, (source, target) in enumerate(copies)]
    for copy in copies:
        copy.start()
    for copy in copies[:2]:
        copy.wait()
    where_to = cells[0]
    row_no = lax.broadcasted_iota(jnp.int32, (px * cy, conn), 0)
    lane_no = lax.broadcasted_iota(jnp.int32, (tile, conn), 0)
    lanes = jnp.where(lane_no == where_to % tile, 1.0, 0.0).astype(jnp.bfloat16)
    rows = jnp.where(row_no == where_to // tile, index[0], 0.0)
    added = sum(nt_dot(part, lanes) for part in split3(rows))
    for copy in copies[2:]:
        copy.wait()
    for pair in range(px):
        block[ACC, pair] = block[ACC, pair] + added[pair * cy : (pair + 1) * cy]
        block[IDX, pair] = (groups[pair] + flags[4]).astype(jnp.float32)
    for number in range(FIELDS):
        one, two = sent(flags, 0, block[number, px - 1], block[number, 0])
        first[number] = one
        second[number] = two
    for place, number in enumerate(OUTER_X):
        one, two = sent(flags, 0, block[number, px - 2], block[number, 1])
        first[FIELDS + place] = one
        second[FIELDS + place] = two


def pack_narrow(flags, block, got_first, got_second, own, first, second):
    px, cy, tile = block.shape[1:]
    width = px + 2 * HX
    own_rows = rows_of(own)

    def put(number, pair, values):
        own_rows[pl.ds(number * cy * width + pair, cy, stride=width), :] = values

    for number in range(FIELDS):
        low, high = received(flags, 0, got_first[number], got_second[number])
        put(number, HX - 1, low)
        put(number, HX + px, high)
        if number in OUTER_X:
            place = FIELDS + OUTER_X.index(number)
            low, high = received(flags, 0, got_first[place], got_second[place])
        else:
            low = high = jnp.zeros((cy, tile), jnp.float32)
        put(number, 0, low)
        put(number, width - 1, high)
        for pair in range(px):
            put(number, HX + pair, block[number, pair])
    for number in range(FIELDS):
        for column in range(HY - 1):
            one, two = sent(flags, 1, own[number, cy - HY + 1 + column], own[number, column])
            first[number * (HY - 1) + column] = one
            second[number * (HY - 1) + column] = two
    for place, number in enumerate(OUTER_Y):
        one, two = sent(flags, 1, own[number, cy - HY], own[number, HY - 1])
        first[FIELDS * (HY - 1) + place] = one
        second[FIELDS * (HY - 1) + place] = two


def lane_half(shape):
    return lax.broadcasted_iota(jnp.int32, shape, len(shape) - 1) < shape[-1] // 2


def swap_half(values):
    return pltpu.roll(values, values.shape[-1] // 2, values.ndim - 1)


def east_of(values, half):
    turned = swap_half(values)
    return jnp.where(half, turned, pltpu.roll(turned, values.shape[-2] - 1, values.ndim - 2))


def west_of(values, half):
    turned = swap_half(values)
    return jnp.where(half, pltpu.roll(turned, 1, values.ndim - 2), turned)


def above(values):
    return pltpu.roll(values, values.shape[-1] - 1, values.ndim - 1)


def below(values):
    return pltpu.roll(values, 1, values.ndim - 1)


def operate(field, coeffs, column, half):
    phases = 3
    here = [field(c, column) for c in range(phases)]
    tx, ty, tz = coeffs[0, column], coeffs[1, column], coeffs[2, column]
    ty_before = coeffs[1, column - 1]
    results = []
    for c in range(phases):
        value = here[c]
        mixed = sum(coeffs[GC + c * phases + b, column] * here[b] for b in range(phases))
        inflow = tx * east_of(value, half) + west_of(tx * value, half)
        inflow = inflow + (ty * field(c, column + 1) + ty_before * field(c, column - 1))
        inflow = inflow + (tz * above(value) + below(tz * value))
        results.append(mixed - inflow)
    return results


def coarse_share(own_misfit, agg_rows, cinv, share, slots, px, cy, narrow):
    count, total = cinv.shape
    lanes = total // share.shape[0]
    width = px + 2 * HX
    agg_no = lax.broadcasted_iota(jnp.int32, (count, own_misfit.shape[-1]), 0)
    parts = [jnp.zeros(agg_no.shape, jnp.float32) for _ in range(4)]
    for column in range(cy):
        for pair in range(px):
            row = column * width + HX + pair
            here = agg_rows[pl.ds(row, 1), :]
            value = own_misfit[pl.ds(row, 1), :]
            spot = (column * px + pair) % len(parts)
            parts[spot] = parts[spot] + jnp.where(agg_no == here, value, 0.0)
    sums = jnp.sum((parts[0] + parts[1]) + (parts[2] + parts[3]), axis=1, keepdims=True)
    wide = share.shape[0]
    for i in range(wide):
        share[pl.ds(i, 1), :] = jnp.sum(cinv[:, i * lanes : (i + 1) * lanes] * sums, axis=0, keepdims=True)
    pair_no = lax.broadcasted_iota(jnp.int32, (width, lanes), 0)
    for i in range(wide):
        before = share[pl.ds((i - 1) % wide, 1), :]
        here = share[pl.ds(i, 1), :]
        after = share[pl.ds((i + 1) % wide, 1), :]
        table = jnp.where(pair_no < HX, before, jnp.where(pair_no < HX + px, here, after))
        for j in range(narrow):
            slots[i * narrow + j] = table


def misfit_and_share(flags, coeffs, current, misfit, index, cinv, slots, own_misfit, own_agg, share, px, cy, narrow):
    columns = current.shape[1]
    half = lane_half(current.shape[2:])
    for column in range(1, columns - 1):
        applied = operate(lambda c, y: current[c, y], coeffs, column, half)
        for c in range(3):
            value = coeffs[GR + c, column] - applied[c]
            misfit[c, column] = value
            if c == 0 and HY <= column < HY + cy:
                own_misfit[column - HY] = value
    for column in range(cy):
        own_agg[column] = index[HY + column] - flags[4]
    coarse_share(rows_of(own_misfit), rows_of(own_agg), cinv, share, slots, px, cy, narrow)


def sweep_body(flags, coeffs, current, index, cinv, hot, factors, update, slots, first, second, px, narrow, scratch):
    misfit, work, hold, own_misfit, own_agg, share, near_slots, cold, sems = scratch
    cy = update.shape[1]
    edge = HY - 1
    boxes = factors.shape[1]
    loads = [
        pltpu.make_async_copy(factors.at[:, pl.ds(0, edge)], cold.at[:, pl.ds(0, edge)], sems.at[0]),
        pltpu.make_async_copy(factors.at[:, pl.ds(boxes - edge, edge)], cold.at[:, pl.ds(edge, edge)], sems.at[1]),
    ]
    for load in loads:
        load.start()
    misfit_and_share(flags, coeffs, current, misfit, index, cinv, near_slots, own_misfit, own_agg, share, px, cy, narrow)
    send = pltpu.make_async_copy(near_slots, slots, sems.at[2])
    send.start()
    solve(flags, misfit, coeffs, hot, cold, loads, update, first, second, work, hold)
    send.wait()


def prepare(flags, own, got_first, got_second, cinv, hot, factors, coeffs, index, current, update, slots, first, second, field, *scratch, px, narrow):
    cy = own.shape[1]
    columns = cy + 2 * HY
    half = lane_half(own.shape[2:])
    depth = lax.broadcasted_iota(jnp.int32, own.shape[2:], 1) % (own.shape[3] // 2)
    for number in range(FIELDS):
        for column in range(cy):
            field[number, HY + column] = own[number, column]
        for column in range(HY - 1):
            low, high = received(
                flags, 1, got_first[number * (HY - 1) + column], got_second[number * (HY - 1) + column]
            )
            field[number, 1 + column] = low
            field[number, HY + cy + column] = high
    for place, number in enumerate(OUTER_Y):
        place = FIELDS * (HY - 1) + place
        low, high = received(flags, 1, got_first[place], got_second[place])
        field[number, 0] = low
        field[number, columns - 1] = high
    for column in range(columns):
        index[column] = field[IDX, column].astype(jnp.int32)
        for c in range(3):
            current[c, column] = field[CUR + c, column]
    coeffs[1, 0] = field[TY, 0]
    for column in range(1, columns - 1):
        tx, ty = field[TX, column], field[TY, column]
        tz = jnp.where(depth < own.shape[3] // 2 - 1, field[TZ, column], 0.0)
        faces = (tx + west_of(tx, half)) + (ty + field[TY, column - 1]) + (tz + below(tz))
        centre = field[ACC, column] + faces
        coeffs[0, column] = tx
        coeffs[1, column] = ty
        coeffs[2, column] = tz
        for number in range(9):
            value = field[CPL + number, column]
            if number % 4 == 0:
                value = value + centre
                coeffs[GI + number // 4, column] = 1.0 / value
            coeffs[GC + number, column] = value
        for c in range(3):
            coeffs[GR + c, column] = field[RHS + c, column]
    sweep_body(flags, coeffs, current, index, cinv, hot, factors, update, slots, first, second, px, narrow, scratch)


def tile_apply(values, coeffs, tiles, column, first, last):
    scaled = [coeffs[GI + c, column] * values[c] for c in range(3)]
    stacked = jnp.concatenate(scaled, axis=0)
    width = scaled[0].shape[0]
    pair_no = lax.broadcasted_iota(jnp.int32, stacked.shape, 0) % width
    left = [jnp.where(pair_no == a + HX - 1, stacked, 0.0).astype(jnp.bfloat16) for a in range(first, last)]
    right = [tiles(a, column - 1) for a in range(first, last)]
    result = nt_dot(jnp.concatenate(left, axis=1), jnp.concatenate(right, axis=1))
    return [result[c * width : (c + 1) * width] for c in range(3)]


def solve(flags, misfit, coeffs, hot, cold, loads, update, first, second, work, hold):
    phases, columns = work.shape[:2]
    cy = columns - 2 * HY
    boxes = hot.shape[0]
    width = work.shape[2]
    px = width - 2 * HX
    edge = HY - 1
    half = lane_half(work.shape[2:])

    def tiles(a, b):
        if b < edge:
            return cold[a, b]
        return hot[a, b - edge] if b < edge + cy else cold[a, b - cy]

    for c in range(phases):
        work[c, 0] = jnp.zeros(work.shape[2:], jnp.float32)
        work[c, columns - 1] = jnp.zeros(work.shape[2:], jnp.float32)
    inside = list(range(HY, HY + cy))
    outside = [column for column in range(1, columns - 1) if column not in inside]
    for column in inside + outside:
        if column == outside[0]:
            for load in loads:
                load.wait()
        new = tile_apply([misfit[c, column] for c in range(phases)], coeffs, tiles, column, 0, boxes)
        for c in range(phases):
            work[c, column] = new[c]
    for step in range(1, INNER):
        spare = max(HY - 1 - (INNER - 1 - step), 0)
        needed = range(1 + spare, columns - 1 - spare)
        last = step == INNER - 1
        first_box, last_box = (1, boxes - 1) if last else (0, boxes)
        for column in needed:
            applied = operate(lambda c, y: work[c, y], coeffs, column, half)
            left = [misfit[c, column] - applied[c] for c in range(phases)]
            new = tile_apply(left, coeffs, tiles, column, first_box, last_box)
            for c in range(phases):
                hold[c, column] = work[c, column] + new[c]
        for column in needed:
            for c in range(phases):
                if last:
                    update[c, column - HY] = hold[c, column]
                else:
                    work[c, column] = hold[c, column]
    rows = rows_of(update)
    for c in range(phases):
        for pair in range(HX):
            tail = rows[pl.ds(c * cy * width + px + pair, cy, stride=width), :]
            head = rows[pl.ds(c * cy * width + HX + pair, cy, stride=width), :]
            one, two = sent(flags, 0, tail, head)
            first[c, pair] = one
            second[c, pair] = two


def widen(flags, update, got_first, got_second, whole, first, second):
    phases, cy, width, _ = update.shape
    px = width - 2 * HX
    whole[...] = update[...]
    rows = rows_of(whole)
    for c in range(phases):
        for pair in range(HX):
            low, high = received(flags, 0, got_first[c, pair], got_second[c, pair])
            rows[pl.ds(c * cy * width + pair, cy, stride=width), :] = low
            rows[pl.ds(c * cy * width + HX + px + pair, cy, stride=width), :] = high
    for c in range(phases):
        for column in range(HY):
            one, two = sent(flags, 1, whole[c, cy - HY + column], whole[c, column])
            first[c, column] = one
            second[c, column] = two


def advance(flags, current, index, whole, got_first, got_second, slots_in, result):
    phases, columns = current.shape[:2]
    cy = columns - 2 * HY
    total = [slots_in[d] for d in range(min(4, slots_in.shape[0]))]
    for d in range(4, slots_in.shape[0]):
        total[d % 4] = total[d % 4] + slots_in[d]
    table = sum(total[1:], total[0])
    for column in range(columns):
        for c in range(phases):
            if column < HY:
                change = received(flags, 1, got_first[c, column], got_second[c, column])[0]
            elif column < HY + cy:
                change = whole[c, column - HY]
            else:
                place = column - HY - cy
                change = received(flags, 1, got_first[c, place], got_second[c, place])[1]
            value = current[c, column] + change
            if c == 0:
                value = value + jnp.take_along_axis(table, index[column], axis=1)
            result[c, column] = value


def next_sweep(flags, current, coeffs, index, whole, got_first, got_second, slots_in, cinv, hot, factors, result, update, slots, first, second, *scratch, px, narrow):
    advance(flags, current, index, whole, got_first, got_second, slots_in, result)
    sweep_body(flags, coeffs, result, index, cinv, hot, factors, update, slots, first, second, px, narrow, scratch)


def finish(flags, current, coeffs, index, whole, got_first, got_second, slots_in, iterate, residual, result, misfit):
    advance(flags, current, index, whole, got_first, got_second, slots_in, result)
    phases, px, cy, _ = iterate.shape
    columns, width = current.shape[1:3]
    half = lane_half(current.shape[2:])
    for column in range(HY, HY + cy):
        applied = operate(lambda c, y: result[c, y], coeffs, column, half)
        for c in range(phases):
            misfit[c, column] = coeffs[GR + c, column] - applied[c]
    for source, target in ((rows_of(result), iterate), (rows_of(misfit), residual)):
        for c in range(phases):
            for pair in range(px):
                target[c, pair] = source[pl.ds((c * columns + HY) * width + HX + pair, cy, stride=width), :]


def swap(first, second, axis):
    count = lax.axis_size(axis)
    if count % 2:
        pairs = [[(i, (i + 1) % count) for i in range(count)], [((i + 1) % count, i) for i in range(count)]]
    else:
        pairs = [
            [(i, i ^ 1) for i in range(count)],
            [(i, (i + 1 if i % 2 else i - 1) % count) for i in range(count)],
        ]
    return lax.ppermute(first, axis, pairs[0]), lax.ppermute(second, axis, pairs[1])


def order_flags():
    flags = []
    for axis in ("wide", "narrow"):
        place = lax.axis_index(axis) % 2
        odd = lax.axis_size(axis) % 2
        flags += [0, 1] if odd else [place, place]
    return jnp.stack([jnp.asarray(flag, jnp.int32) for flag in flags + [lax.axis_index("narrow") * AGG_LOC]])


def per_device(
    rhs,
    start,
    trans,
    accum,
    coupling,
    well_cells,
    well_index,
    agg_map,
    tile_factors,
    coarse_inverse,
):
    phases, px, cy, tile = rhs.shape
    wide, narrow = lax.axis_size("wide"), lax.axis_size("narrow")
    width, columns = px + 2 * HX, cy + 2 * HY
    f32 = jnp.float32
    flags = order_flags()
    lanes = narrow * AGG_LOC

    face = ((FIELDS + len(OUTER_X), cy, tile), f32)
    block, first, second = call(
        pack_wide,
        [((FIELDS, px, cy, tile), f32), face, face],
        [
            pltpu.VMEM((px, cy, tile), jnp.int32),
            pltpu.VMEM(well_cells.shape, jnp.int32),
            pltpu.VMEM(well_index.shape, f32),
            pltpu.SemaphoreType.DMA((7 + phases,)),
        ],
        far=range(8),
    )(flags, trans, accum, coupling, rhs, start, agg_map, well_cells, well_index)
    first, second = swap(first, second, "wide")
    face = ((FIELDS * (HY - 1) + len(OUTER_Y), width, tile), f32)
    own, first, second = call(pack_narrow, [((FIELDS, cy, width, tile), f32), face, face])(
        flags, block, first, second
    )
    first, second = swap(first, second, "narrow")

    vec = (width, tile)
    field = ((phases, columns) + vec, f32)
    inner = ((phases, columns - 1) + vec, f32)
    slot = ((wide * narrow, width, lanes), f32)
    part = ((phases, cy) + vec, f32)
    face = ((phases, HX, cy, tile), f32)
    edge_face = ((phases, HY) + vec, f32)
    boxes = tile_factors.shape
    scratch = [
        pltpu.VMEM(*inner),
        pltpu.VMEM(*field),
        pltpu.VMEM(*field),
        pltpu.VMEM((cy,) + vec, f32),
        pltpu.VMEM((cy,) + vec, jnp.int32),
        pltpu.VMEM((wide, lanes), f32),
        pltpu.VMEM(*slot),
        pltpu.VMEM((boxes[0], 2 * (HY - 1)) + boxes[2:], tile_factors.dtype),
        pltpu.SemaphoreType.DMA((3,)),
    ]
    hot = tile_factors[:, HY - 1 : HY - 1 + cy]
    coeffs, index, current, update, slots, first, second = call(
        functools.partial(prepare, px=px, narrow=narrow),
        [((GFIELDS, columns - 1) + vec, f32), ((columns,) + vec, jnp.int32), field, part, slot, face, face],
        [pltpu.VMEM((FIELDS, columns) + vec, f32)] + scratch,
        far=(5,),
        far_outs=(4,),
    )(flags, own, first, second, coarse_inverse, hot, tile_factors)
    for sweep in range(SWEEPS):
        gathered = lax.all_to_all(slots, ("wide", "narrow"), 0, 0, tiled=True)
        first, second = swap(first, second, "wide")
        whole, first, second = call(widen, [part, edge_face, edge_face])(flags, update, first, second)
        first, second = swap(first, second, "narrow")
        if sweep < SWEEPS - 1:
            current, update, slots, first, second = call(
                functools.partial(next_sweep, px=px, narrow=narrow),
                [field, part, slot, face, face],
                scratch,
                far=(9,),
                far_outs=(2,),
            )(flags, current, coeffs, index, whole, first, second, gathered, coarse_inverse, hot, tile_factors)
    out = (rhs.shape, f32)
    return call(finish, [out, out], [pltpu.VMEM(*field), pltpu.VMEM(*field)])(
        flags, current, coeffs, index, whole, first, second, gathered
    )


def solution(mesh):
    return jax.shard_map(
        per_device,
        mesh=mesh,
        in_specs=(
            P(None, "wide", "narrow", None),
            P(None, "wide", "narrow", None),
            P(None, "wide", "narrow", None),
            P("wide", "narrow", None),
            P(None, None, "wide", "narrow", None),
            P("wide", "narrow", None),
            P("wide", "narrow", None),
            P("wide", "narrow", None),
            P("wide", "narrow", None, None),
            P(("wide", "narrow"), None),
        ),
        out_specs=(P(None, "wide", "narrow", None), P(None, "wide", "narrow", None)),
        check_vma=False,
    )
```

time: 229 us -> 84.9 us (0.37); the launches traced: 226 us -> 84.5 us
  blocking collectives: 123 us -> 0 us
  matrix products: 22.9 us -> 0 us
  Pallas kernels: 0 us -> 16.9 us
  other arithmetic: 12.5 us -> 0 us
  local copies, waits for them, and re-layouts: 13.6 us -> 1.6 us
  starting transfers between devices: 34.2 us -> 42.6 us
  waiting for transfers between devices: 18.4 us -> 22.6 us
    unnamed x3 -> x0, blocking collectives: 123 us -> none
    dot_general x18 -> x0, matrix products: 22.9 us -> none  [the longest x9 17 us: tile_apply(): jnp.einsum('cpyj,pykj->cpyk', scaled, factors, preferred_element_type=jnp...]
    pallas_call x0 -> x9, Pallas kernels: none -> 16.9 us  [run(): pl.pallas_call(body, out_shape=tuple(((pltpu.HBM if number in far_outs el...]
    all_to_all x0 -> x3, starting transfers between devices: none -> 14.1 us  [per_device(): gathered = lax.all_to_all(slots, ('wide', 'narrow'), 0, 0, tiled=True)]
    ppermute x20 -> x16, starting transfers between devices: 34.2 us -> 28.5 us  [the longest x8 19.6 us: swap(): lax.ppermute(second, axis, pairs[1])]
    slice x47 -> x1, local copies, waits for them, and re-layouts: 7.04 us -> 1.51 us  [per_device(): hot = tile_factors[:, HY - 1:HY - 1 + cy]]
    unnamed x98 -> x2, local copies, waits for them, and re-layouts: 4.69 us -> 0.01 us
    sub x3 -> x0, other arithmetic: 4.27 us -> none  [extended_fn(): extended = (rim_full[13:] - applied)[..., 1:-1, 1:-1, :]]
  transfers between devices with their start and end apart: 20 -> 19, of which waited for: 13 -> 9; matrix products, arithmetic and copies ran while one was open for 1% -> 2% of each run, Pallas kernels for 0% -> 2%
where the time goes in v2:
time: 84.9 us; the launch traced here: 84.5 us
  starting transfers between devices  42.6 us (50%)
  waiting for transfers between devices  22.6 us (27%)
  Pallas kernels  16.9 us (20%)
  local copies, waits for them, and re-layouts  1.6 us (2%)
    ppermute x8, waiting for transfers between devices, swap(): lax.ppermute(second, axis, pairs[1])  21.8 us
    ppermute x8, starting transfers between devices, swap(): lax.ppermute(second, axis, pairs[1])  19.6 us
    pallas_call x9, Pallas kernels, run(): pl.pallas_call(body, out_shape=tuple(((pltpu.HBM if number in far_outs el...  16.9 us
    all_to_all x3, starting transfers between devices, per_device(): gathered = lax.all_to_all(slots, ('wide', 'narrow'), 0, 0, tiled=True)  14.1 us
    ppermute x8, starting transfers between devices, swap(): lax.ppermute(first, axis, pairs[0])  8.85 us
  transfers between devices with their start and end apart: 19, of which 9 were waited for; matrix products, arithmetic and copies ran while one was open for 2% of the time, Pallas kernels for 2%

profile of v2, /device:TPU:0, one launch (start us, length us, event | category | flops | bytes accessed | tf_op | source)
XLA Modules:
  0.0 84.5 jit_solution(6058910443762921423)
XLA Ops:
  0.7 0.1 stack.17.flags
  0.7 1.6 %pack_wide.1 = (f32[20,4,8,128]{3,2,1,0:T(8,128)S(1)}, f32[25,8,128]{2,1,0:T(8,128)S(1)}, f32[25,8,128]{2,1,0:T(8,128)S(1)}) custom-call(s32[5]{0:T(128)S(1)} %stack.17.flags, f32[3,4,8,128]{3,2,1,0:T(8,128)} %trans.1, f32[4,8,128]{2,1,0:T(8,128)} %accum.1, f32[3,3,4,8,128]{4,3,2,1,0:T(8,128)} %coupling.1, f32[3,4,8,128]{3,2,1,0:T(8,128)} %rhs.1, ...), custom_call_target="tpu_custom_call" | custom-call | tf_op jit(solution)/shard_map/pack_wide/pallas_call | solution.py:36
  2.4 3.1 %collective-permute-start = (f32[25,8,128]{2,1,0:T(8,128)S(1)}, f32[25,8,128]{2,1,0:T(8,128)S(1)}, u32[]{:S(2)}, u32[]{:S(2)}) collective-permute-start(f32[25,8,128]{2,1,0:T(8,128)S(1)} %get-tuple-element.35), channel_id=1, source_target_pairs={{0,4},{4,0},{8,12},{12,8},{16,20},{20,16},{24,28},{28,24},{1,5},{5... | collective-permute-start | bytes 307208 | tf_op jit(solution)/shard_map/ppermute | solution.py:428
  5.4 3.5 %collective-permute-start.1 = (f32[25,8,128]{2,1,0:T(8,128)S(1)}, f32[25,8,128]{2,1,0:T(8,128)S(1)}, u32[]{:S(2)}, u32[]{:S(2)}) collective-permute-start(f32[25,8,128]{2,1,0:T(8,128)S(1)} %get-tuple-element.36), channel_id=1, source_target_pairs={{0,28},{4,8},{8,4},{12,16},{16,12},{20,24},{24,20},{28,0},{1,29},{... | collective-permute-start | bytes 307208 | tf_op jit(solution)/shard_map/ppermute | solution.py:428
  9.0 0.8 collective-permute-done.got_first
  9.8 3.0 %collective-permute-done.1.got_second = f32[25,8,128]{2,1,0:T(8,128)S(1)} collective-permute-done((f32[25,8,128]{2,1,0:T(8,128)S(1)}, f32[25,8,128]{2,1,0:T(8,128)S(1)}, u32[]{:S(2)}, u32[]{:S(2)}) %collective-permute-start.1) | collective-permute-done | bytes 102432 | tf_op jit(solution)/shard_map/ppermute | solution.py:428
  12.8 0.7 pack_narrow.1
  13.5 0.1 collective-permute-start.2
  13.6 1.6 %collective-permute-start.3 = (f32[45,8,128]{2,1,0:T(8,128)S(1)}, f32[45,8,128]{2,1,0:T(8,128)S(1)}, u32[]{:S(2)}, u32[]{:S(2)}) collective-permute-start(f32[45,8,128]{2,1,0:T(8,128)S(1)} %get-tuple-element.39), channel_id=1, source_target_pairs={{0,3},{1,2},{2,1},{3,0},{4,7},{5,6},{6,5},{7,4},{8,11},{9,10},{10,... | collective-permute-start | bytes 552968 | tf_op jit(solution)/shard_map/ppermute | solution.py:428
  15.1 1.5 %slice.3.hot = bf16[6,8,128,128]{3,2,1,0:T(8,128)(2,1)S(1)} slice(bf16[6,12,128,128]{3,2,1,0:T(8,128)(2,1)} %factors.5), slice={[0:6], [2:10], [0:128], [0:128]} | slice | bytes 3145728 | tf_op jit(solution)/shard_map/slice | solution.py:497
  16.7 0.0 collective-permute-done.2.got_first
  16.7 3.3 %collective-permute-done.3.got_second = f32[45,8,128]{2,1,0:T(8,128)S(1)} collective-permute-done((f32[45,8,128]{2,1,0:T(8,128)S(1)}, f32[45,8,128]{2,1,0:T(8,128)S(1)}, u32[]{:S(2)}, u32[]{:S(2)}) %collective-permute-start.3) | collective-permute-done | bytes 184352 | tf_op jit(solution)/shard_map/ppermute | solution.py:428
  19.9 3.8 %prepare.1 = (f32[18,13,8,128]{3,2,1,0:T(8,128)S(1)}, s32[14,8,128]{2,1,0:T(8,128)S(1)}, f32[3,14,8,128]{3,2,1,0:T(8,128)S(1)}, f32[3,8,8,128]{3,2,1,0:T(8,128)S...) custom-call(s32[5]{0:T(128)S(1)} %stack.17.flags, ...), custom_call_target="tpu_custom_call" | custom-call | tf_op jit(solution)/shard_map/prepare/pallas_call | solution.py:36
  23.8 4.9 %all-to-all-start = ((f32[32,8,128]{2,1,0:T(8,128)}), f32[32,8,128]{2,1,0:T(8,128)S(1)}, u32[]{:S(2)}, u32[]{:S(2)}) async-start(f32[32,8,128]{2,1,0:T(8,128)} %get-tuple-element.49), calls=%async_computation | async-start | bytes 262144 | tf_op jit(solution)/shard_map/all_to_all | solution.py:506
  28.7 1.8 %collective-permute-start.4 = (f32[3,2,8,128]{3,2,1,0:T(8,128)S(1)}, f32[3,2,8,128]{3,2,1,0:T(8,128)S(1)}, u32[]{:S(2)}, u32[]{:S(2)}) collective-permute-start(f32[3,2,8,128]{3,2,1,0:T(8,128)S(1)} %get-tuple-element.44), channel_id=1, source_target_pairs={{0,4},{4,0},{8,12},{12,8},{16,20},{20,16},{24,28},{28,24},{1,5},{5... | collective-permute-start | bytes 73736 | tf_op jit(solution)/shard_map/ppermute | solution.py:428
  30.5 3.3 %collective-permute-start.5 = (f32[3,2,8,128]{3,2,1,0:T(8,128)S(1)}, f32[3,2,8,128]{3,2,1,0:T(8,128)S(1)}, u32[]{:S(2)}, u32[]{:S(2)}) collective-permute-start(f32[3,2,8,128]{3,2,1,0:T(8,128)S(1)} %get-tuple-element.45), channel_id=1, source_target_pairs={{0,28},{4,8},{8,4},{12,16},{16,12},{20,24},{24,20},{28,0},{1,29},{... | collective-permute-start | bytes 73736 | tf_op jit(solution)/shard_map/ppermute | solution.py:428
  33.8 0.0 collective-permute-done.4.got_first
  33.8 3.3 %collective-permute-done.5.got_second = f32[3,2,8,128]{3,2,1,0:T(8,128)S(1)} collective-permute-done((f32[3,2,8,128]{3,2,1,0:T(8,128)S(1)}, f32[3,2,8,128]{3,2,1,0:T(8,128)S(1)}, u32[]{:S(2)}, u32[]{:S(2)}) %collective-permute-start.5) | collective-permute-done | bytes 24608 | tf_op jit(solution)/shard_map/ppermute | solution.py:428
  37.1 0.6 widen.3
  37.7 0.1 collective-permute-start.6
  37.7 1.5 %collective-permute-start.7 = (f32[3,3,8,128]{3,2,1,0:T(8,128)S(1)}, f32[3,3,8,128]{3,2,1,0:T(8,128)S(1)}, u32[]{:S(2)}, u32[]{:S(2)}) collective-permute-start(f32[3,3,8,128]{3,2,1,0:T(8,128)S(1)} %get-tuple-element.48), channel_id=1, source_target_pairs={{0,3},{1,2},{2,1},{3,0},{4,7},{5,6},{6,5},{7,4},{8,11},{9,10},{10,... | collective-permute-start | bytes 110600 | tf_op jit(solution)/shard_map/ppermute | solution.py:428
  39.3 0.0 collective-permute-done.6.got_first
  39.3 1.9 %collective-permute-done.7.got_second = f32[3,3,8,128]{3,2,1,0:T(8,128)S(1)} collective-permute-done((f32[3,3,8,128]{3,2,1,0:T(8,128)S(1)}, f32[3,3,8,128]{3,2,1,0:T(8,128)S(1)}, u32[]{:S(2)}, u32[]{:S(2)}) %collective-permute-start.7) | collective-permute-done | bytes 36896 | tf_op jit(solution)/shard_map/ppermute | solution.py:428
  41.2 0.0 all-to-all-done.slots_in
  41.2 3.8 %next_sweep.2 = (f32[3,14,8,128]{3,2,1,0:T(8,128)S(1)}, f32[3,8,8,128]{3,2,1,0:T(8,128)S(1)}, f32[32,8,128]{2,1,0:T(8,128)}, f32[3,2,8,128]{3,2,1,0:T(8,128)S(1)}, f32[3,2,8,128]{3,2,1,0:T(8,128)S(1)}) custom-call(s32[5]{0:T(128)S(1)} %stack.17.flags, f32[3,14,8,128]{3,2,1,0:T(8,128)S(1)} %get-tuple-element.40.current, ...), custom_call_target="tpu_custom_call" | custom-call | tf_op jit(solution)/shard_map/next_sweep/pallas_call | solution.py:36
  45.0 4.6 %all-to-all-start.1 = ((f32[32,8,128]{2,1,0:T(8,128)}), f32[32,8,128]{2,1,0:T(8,128)S(1)}, u32[]{:S(2)}, u32[]{:S(2)}) async-start(f32[32,8,128]{2,1,0:T(8,128)} %get-tuple-element.57), calls=%async_computation.1 | async-start | bytes 262144 | tf_op jit(solution)/shard_map/all_to_all | solution.py:506
  49.6 1.8 %collective-permute-start.8 = (f32[3,2,8,128]{3,2,1,0:T(8,128)S(1)}, f32[3,2,8,128]{3,2,1,0:T(8,128)S(1)}, u32[]{:S(2)}, u32[]{:S(2)}) collective-permute-start(f32[3,2,8,128]{3,2,1,0:T(8,128)S(1)} %get-tuple-element.52), channel_id=1, source_target_pairs={{0,4},{4,0},{8,12},{12,8},{16,20},{20,16},{24,28},{28,24},{1,5},{5... | collective-permute-start | bytes 73736 | tf_op jit(solution)/shard_map/ppermute | solution.py:428
  51.5 3.3 %collective-permute-start.9 = (f32[3,2,8,128]{3,2,1,0:T(8,128)S(1)}, f32[3,2,8,128]{3,2,1,0:T(8,128)S(1)}, u32[]{:S(2)}, u32[]{:S(2)}) collective-permute-start(f32[3,2,8,128]{3,2,1,0:T(8,128)S(1)} %get-tuple-element.53), channel_id=1, source_target_pairs={{0,28},{4,8},{8,4},{12,16},{16,12},{20,24},{24,20},{28,0},{1,29},{... | collective-permute-start | bytes 73736 | tf_op jit(solution)/shard_map/ppermute | solution.py:428
  54.8 0.0 collective-permute-done.8.got_first
  54.8 3.3 %collective-permute-done.9.got_second = f32[3,2,8,128]{3,2,1,0:T(8,128)S(1)} collective-permute-done((f32[3,2,8,128]{3,2,1,0:T(8,128)S(1)}, f32[3,2,8,128]{3,2,1,0:T(8,128)S(1)}, u32[]{:S(2)}, u32[]{:S(2)}) %collective-permute-start.9) | collective-permute-done | bytes 24608 | tf_op jit(solution)/shard_map/ppermute | solution.py:428
  58.0 0.6 widen.4
  58.6 0.1 collective-permute-start.10
  58.7 1.5 %collective-permute-start.11 = (f32[3,3,8,128]{3,2,1,0:T(8,128)S(1)}, f32[3,3,8,128]{3,2,1,0:T(8,128)S(1)}, u32[]{:S(2)}, u32[]{:S(2)}) collective-permute-start(f32[3,3,8,128]{3,2,1,0:T(8,128)S(1)} %get-tuple-element.56), channel_id=1, source_target_pairs={{0,3},{1,2},{2,1},{3,0},{4,7},{5,6},{6,5},{7,4},{8,11},{9,10},{10,... | collective-permute-start | bytes 110600 | tf_op jit(solution)/shard_map/ppermute | solution.py:428
  60.2 0.0 collective-permute-done.10.got_first
  60.2 1.9 %collective-permute-done.11.got_second = f32[3,3,8,128]{3,2,1,0:T(8,128)S(1)} collective-permute-done((f32[3,3,8,128]{3,2,1,0:T(8,128)S(1)}, f32[3,3,8,128]{3,2,1,0:T(8,128)S(1)}, u32[]{:S(2)}, u32[]{:S(2)}) %collective-permute-start.11) | collective-permute-done | bytes 36896 | tf_op jit(solution)/shard_map/ppermute | solution.py:428
  62.1 0.0 all-to-all-done.1.slots_in
  62.1 3.8 %next_sweep.3 = (f32[3,14,8,128]{3,2,1,0:T(8,128)S(1)}, f32[3,8,8,128]{3,2,1,0:T(8,128)S(1)}, f32[32,8,128]{2,1,0:T(8,128)}, f32[3,2,8,128]{3,2,1,0:T(8,128)S(1)}, f32[3,2,8,128]{3,2,1,0:T(8,128)S(1)}) custom-call(s32[5]{0:T(128)S(1)} %stack.17.flags, f32[3,14,8,128]{3,2,1,0:T(8,128)S(1)} %get-tuple-element.50.current, ...), custom_call_target="tpu_custom_call" | custom-call | tf_op jit(solution)/shard_map/next_sweep/pallas_call | solution.py:36
  66.0 4.6 %all-to-all-start.2 = ((f32[32,8,128]{2,1,0:T(8,128)}), f32[32,8,128]{2,1,0:T(8,128)S(1)}, u32[]{:S(2)}, u32[]{:S(2)}) async-start(f32[32,8,128]{2,1,0:T(8,128)} %get-tuple-element.65), calls=%async_computation.2 | async-start | bytes 262144 | tf_op jit(solution)/shard_map/all_to_all | solution.py:506
  70.6 1.8 %collective-permute-start.12 = (f32[3,2,8,128]{3,2,1,0:T(8,128)S(1)}, f32[3,2,8,128]{3,2,1,0:T(8,128)S(1)}, u32[]{:S(2)}, u32[]{:S(2)}) collective-permute-start(f32[3,2,8,128]{3,2,1,0:T(8,128)S(1)} %get-tuple-element.60), channel_id=1, source_target_pairs={{0,4},{4,0},{8,12},{12,8},{16,20},{20,16},{24,28},{28,24},{1,5},{5... | collective-permute-start | bytes 73736 | tf_op jit(solution)/shard_map/ppermute | solution.py:428
  72.4 3.3 %collective-permute-start.13 = (f32[3,2,8,128]{3,2,1,0:T(8,128)S(1)}, f32[3,2,8,128]{3,2,1,0:T(8,128)S(1)}, u32[]{:S(2)}, u32[]{:S(2)}) collective-permute-start(f32[3,2,8,128]{3,2,1,0:T(8,128)S(1)} %get-tuple-element.61), channel_id=1, source_target_pairs={{0,28},{4,8},{8,4},{12,16},{16,12},{20,24},{24,20},{28,0},{1,29},{... | collective-permute-start | bytes 73736 | tf_op jit(solution)/shard_map/ppermute | solution.py:428
  75.7 0.0 collective-permute-done.12.got_first
  75.7 3.3 %collective-permute-done.13.got_second = f32[3,2,8,128]{3,2,1,0:T(8,128)S(1)} collective-permute-done((f32[3,2,8,128]{3,2,1,0:T(8,128)S(1)}, f32[3,2,8,128]{3,2,1,0:T(8,128)S(1)}, u32[]{:S(2)}, u32[]{:S(2)}) %collective-permute-start.13) | collective-permute-done | bytes 24608 | tf_op jit(solution)/shard_map/ppermute | solution.py:428
  79.0 0.6 widen.5
  79.5 0.1 collective-permute-start.14
  79.6 1.5 %collective-permute-start.15 = (f32[3,3,8,128]{3,2,1,0:T(8,128)S(1)}, f32[3,3,8,128]{3,2,1,0:T(8,128)S(1)}, u32[]{:S(2)}, u32[]{:S(2)}) collective-permute-start(f32[3,3,8,128]{3,2,1,0:T(8,128)S(1)} %get-tuple-element.64), channel_id=1, source_target_pairs={{0,3},{1,2},{2,1},{3,0},{4,7},{5,6},{6,5},{7,4},{8,11},{9,10},{10,... | collective-permute-start | bytes 110600 | tf_op jit(solution)/shard_map/ppermute | solution.py:428
  81.1 0.0 collective-permute-done.14.got_first
  81.2 1.9 %collective-permute-done.15.got_second = f32[3,3,8,128]{3,2,1,0:T(8,128)S(1)} collective-permute-done((f32[3,3,8,128]{3,2,1,0:T(8,128)S(1)}, f32[3,3,8,128]{3,2,1,0:T(8,128)S(1)}, u32[]{:S(2)}, u32[]{:S(2)}) %collective-permute-start.15) | collective-permute-done | bytes 36896 | tf_op jit(solution)/shard_map/ppermute | solution.py:428
  83.1 1.4 %finish.1 = (f32[3,4,8,128]{3,2,1,0:T(8,128)}, f32[3,4,8,128]{3,2,1,0:T(8,128)}) custom-call(s32[5]{0:T(128)S(1)} %stack.17.flags, f32[3,14,8,128]{3,2,1,0:T(8,128)S(1)} %get-tuple-element.58.current, f32[18,13,8,128]{3,2,1,0:T(8,128)S(1)} %get-tuple-element.41.coeffs, s32[14,8,128]{2,1,0:T(8,128)S(1)} %get-tuple-element.42.index, ...), custom_call_target="tpu_custom_call" | custom-call | tf_op jit(solution)/shard_map/finish/pallas_call | solution.py:36
  (3 shorter events, 0.0 us)
Async XLA Ops:
  0.6 19.3 %copy-start = (f32[32,1024]{1,0:T(8,128)S(1)}, f32[32,1024]{1,0:T(8,128)}, u32[]{:S(2)}) copy-start(f32[32,1024]{1,0:T(8,128)} %cinv.5) | copy-start | bytes 393220
  2.4 7.4 %collective-permute-start = (f32[25,8,128]{2,1,0:T(8,128)S(1)}, f32[25,8,128]{2,1,0:T(8,128)S(1)}, u32[]{:S(2)}, u32[]{:S(2)}) collective-permute-start(f32[25,8,128]{2,1,0:T(8,128)S(1)} %get-tuple-element.35), channel_id=1, source_target_pairs={{0,4},{4,0},{8,12},{12,8},{16,20},{20,16},{24,28},{28,24},{1,5},{5... | collective-permute-start | bytes 307208 | tf_op jit(solution)/shard_map/ppermute | solution.py:428
  5.4 7.4 %collective-permute-start.1 = (f32[25,8,128]{2,1,0:T(8,128)S(1)}, f32[25,8,128]{2,1,0:T(8,128)S(1)}, u32[]{:S(2)}, u32[]{:S(2)}) collective-permute-start(f32[25,8,128]{2,1,0:T(8,128)S(1)} %get-tuple-element.36), channel_id=1, source_target_pairs={{0,28},{4,8},{8,4},{12,16},{16,12},{20,24},{24,20},{28,0},{1,29},{... | collective-permute-start | bytes 307208 | tf_op jit(solution)/shard_map/ppermute | solution.py:428
  13.5 3.2 %collective-permute-start.2 = (f32[45,8,128]{2,1,0:T(8,128)S(1)}, f32[45,8,128]{2,1,0:T(8,128)S(1)}, u32[]{:S(2)}, u32[]{:S(2)}) collective-permute-start(f32[45,8,128]{2,1,0:T(8,128)S(1)} %get-tuple-element.38), channel_id=1, source_target_pairs={{0,1},{1,0},{2,3},{3,2},{4,5},{5,4},{6,7},{7,6},{8,9},{9,8},{10,11... | collective-permute-start | bytes 552968 | tf_op jit(solution)/shard_map/ppermute | solution.py:428
  13.6 6.4 %collective-permute-start.3 = (f32[45,8,128]{2,1,0:T(8,128)S(1)}, f32[45,8,128]{2,1,0:T(8,128)S(1)}, u32[]{:S(2)}, u32[]{:S(2)}) collective-permute-start(f32[45,8,128]{2,1,0:T(8,128)S(1)} %get-tuple-element.39), channel_id=1, source_target_pairs={{0,3},{1,2},{2,1},{3,0},{4,7},{5,6},{6,5},{7,4},{8,11},{9,10},{10,... | collective-permute-start | bytes 552968 | tf_op jit(solution)/shard_map/ppermute | solution.py:428
  23.8 17.4 %all-to-all-start = ((f32[32,8,128]{2,1,0:T(8,128)}), f32[32,8,128]{2,1,0:T(8,128)S(1)}, u32[]{:S(2)}, u32[]{:S(2)}) async-start(f32[32,8,128]{2,1,0:T(8,128)} %get-tuple-element.49), calls=%async_computation | async-start | bytes 262144 | tf_op jit(solution)/shard_map/all_to_all | solution.py:506
  28.7 5.2 %collective-permute-start.4 = (f32[3,2,8,128]{3,2,1,0:T(8,128)S(1)}, f32[3,2,8,128]{3,2,1,0:T(8,128)S(1)}, u32[]{:S(2)}, u32[]{:S(2)}) collective-permute-start(f32[3,2,8,128]{3,2,1,0:T(8,128)S(1)} %get-tuple-element.44), channel_id=1, source_target_pairs={{0,4},{4,0},{8,12},{12,8},{16,20},{20,16},{24,28},{28,24},{1,5},{5... | collective-permute-start | bytes 73736 | tf_op jit(solution)/shard_map/ppermute | solution.py:428
  30.5 6.6 %collective-permute-start.5 = (f32[3,2,8,128]{3,2,1,0:T(8,128)S(1)}, f32[3,2,8,128]{3,2,1,0:T(8,128)S(1)}, u32[]{:S(2)}, u32[]{:S(2)}) collective-permute-start(f32[3,2,8,128]{3,2,1,0:T(8,128)S(1)} %get-tuple-element.45), channel_id=1, source_target_pairs={{0,28},{4,8},{8,4},{12,16},{16,12},{20,24},{24,20},{28,0},{1,29},{... | collective-permute-start | bytes 73736 | tf_op jit(solution)/shard_map/ppermute | solution.py:428
  37.7 1.6 %collective-permute-start.6 = (f32[3,3,8,128]{3,2,1,0:T(8,128)S(1)}, f32[3,3,8,128]{3,2,1,0:T(8,128)S(1)}, u32[]{:S(2)}, u32[]{:S(2)}) collective-permute-start(f32[3,3,8,128]{3,2,1,0:T(8,128)S(1)} %get-tuple-element.47), channel_id=1, source_target_pairs={{0,1},{1,0},{2,3},{3,2},{4,5},{5,4},{6,7},{7,6},{8,9},{9,8},{10,11... | collective-permute-start | bytes 110600 | tf_op jit(solution)/shard_map/ppermute | solution.py:428
  37.7 3.4 %collective-permute-start.7 = (f32[3,3,8,128]{3,2,1,0:T(8,128)S(1)}, f32[3,3,8,128]{3,2,1,0:T(8,128)S(1)}, u32[]{:S(2)}, u32[]{:S(2)}) collective-permute-start(f32[3,3,8,128]{3,2,1,0:T(8,128)S(1)} %get-tuple-element.48), channel_id=1, source_target_pairs={{0,3},{1,2},{2,1},{3,0},{4,7},{5,6},{6,5},{7,4},{8,11},{9,10},{10,... | collective-permute-start | bytes 110600 | tf_op jit(solution)/shard_map/ppermute | solution.py:428
  45.0 17.1 %all-to-all-start.1 = ((f32[32,8,128]{2,1,0:T(8,128)}), f32[32,8,128]{2,1,0:T(8,128)S(1)}, u32[]{:S(2)}, u32[]{:S(2)}) async-start(f32[32,8,128]{2,1,0:T(8,128)} %get-tuple-element.57), calls=%async_computation.1 | async-start | bytes 262144 | tf_op jit(solution)/shard_map/all_to_all | solution.py:506
  49.6 5.2 %collective-permute-start.8 = (f32[3,2,8,128]{3,2,1,0:T(8,128)S(1)}, f32[3,2,8,128]{3,2,1,0:T(8,128)S(1)}, u32[]{:S(2)}, u32[]{:S(2)}) collective-permute-start(f32[3,2,8,128]{3,2,1,0:T(8,128)S(1)} %get-tuple-element.52), channel_id=1, source_target_pairs={{0,4},{4,0},{8,12},{12,8},{16,20},{20,16},{24,28},{28,24},{1,5},{5... | collective-permute-start | bytes 73736 | tf_op jit(solution)/shard_map/ppermute | solution.py:428
  51.5 6.6 %collective-permute-start.9 = (f32[3,2,8,128]{3,2,1,0:T(8,128)S(1)}, f32[3,2,8,128]{3,2,1,0:T(8,128)S(1)}, u32[]{:S(2)}, u32[]{:S(2)}) collective-permute-start(f32[3,2,8,128]{3,2,1,0:T(8,128)S(1)} %get-tuple-element.53), channel_id=1, source_target_pairs={{0,28},{4,8},{8,4},{12,16},{16,12},{20,24},{24,20},{28,0},{1,29},{... | collective-permute-start | bytes 73736 | tf_op jit(solution)/shard_map/ppermute | solution.py:428
  58.6 1.6 %collective-permute-start.10 = (f32[3,3,8,128]{3,2,1,0:T(8,128)S(1)}, f32[3,3,8,128]{3,2,1,0:T(8,128)S(1)}, u32[]{:S(2)}, u32[]{:S(2)}) collective-permute-start(f32[3,3,8,128]{3,2,1,0:T(8,128)S(1)} %get-tuple-element.55), channel_id=1, source_target_pairs={{0,1},{1,0},{2,3},{3,2},{4,5},{5,4},{6,7},{7,6},{8,9},{9,8},{10,11... | collective-permute-start | bytes 110600 | tf_op jit(solution)/shard_map/ppermute | solution.py:428
  58.7 3.4 %collective-permute-start.11 = (f32[3,3,8,128]{3,2,1,0:T(8,128)S(1)}, f32[3,3,8,128]{3,2,1,0:T(8,128)S(1)}, u32[]{:S(2)}, u32[]{:S(2)}) collective-permute-start(f32[3,3,8,128]{3,2,1,0:T(8,128)S(1)} %get-tuple-element.56), channel_id=1, source_target_pairs={{0,3},{1,2},{2,1},{3,0},{4,7},{5,6},{6,5},{7,4},{8,11},{9,10},{10,... | collective-permute-start | bytes 110600 | tf_op jit(solution)/shard_map/ppermute | solution.py:428
  66.0 17.1 %all-to-all-start.2 = ((f32[32,8,128]{2,1,0:T(8,128)}), f32[32,8,128]{2,1,0:T(8,128)S(1)}, u32[]{:S(2)}, u32[]{:S(2)}) async-start(f32[32,8,128]{2,1,0:T(8,128)} %get-tuple-element.65), calls=%async_computation.2 | async-start | bytes 262144 | tf_op jit(solution)/shard_map/all_to_all | solution.py:506
  70.6 5.2 %collective-permute-start.12 = (f32[3,2,8,128]{3,2,1,0:T(8,128)S(1)}, f32[3,2,8,128]{3,2,1,0:T(8,128)S(1)}, u32[]{:S(2)}, u32[]{:S(2)}) collective-permute-start(f32[3,2,8,128]{3,2,1,0:T(8,128)S(1)} %get-tuple-element.60), channel_id=1, source_target_pairs={{0,4},{4,0},{8,12},{12,8},{16,20},{20,16},{24,28},{28,24},{1,5},{5... | collective-permute-start | bytes 73736 | tf_op jit(solution)/shard_map/ppermute | solution.py:428
  72.4 6.6 %collective-permute-start.13 = (f32[3,2,8,128]{3,2,1,0:T(8,128)S(1)}, f32[3,2,8,128]{3,2,1,0:T(8,128)S(1)}, u32[]{:S(2)}, u32[]{:S(2)}) collective-permute-start(f32[3,2,8,128]{3,2,1,0:T(8,128)S(1)} %get-tuple-element.61), channel_id=1, source_target_pairs={{0,28},{4,8},{8,4},{12,16},{16,12},{20,24},{24,20},{28,0},{1,29},{... | collective-permute-start | bytes 73736 | tf_op jit(solution)/shard_map/ppermute | solution.py:428
  79.5 1.6 %collective-permute-start.14 = (f32[3,3,8,128]{3,2,1,0:T(8,128)S(1)}, f32[3,3,8,128]{3,2,1,0:T(8,128)S(1)}, u32[]{:S(2)}, u32[]{:S(2)}) collective-permute-start(f32[3,3,8,128]{3,2,1,0:T(8,128)S(1)} %get-tuple-element.63), channel_id=1, source_target_pairs={{0,1},{1,0},{2,3},{3,2},{4,5},{5,4},{6,7},{7,6},{8,9},{9,8},{10,11... | collective-permute-start | bytes 110600 | tf_op jit(solution)/shard_map/ppermute | solution.py:428
  79.6 3.4 %collective-permute-start.15 = (f32[3,3,8,128]{3,2,1,0:T(8,128)S(1)}, f32[3,3,8,128]{3,2,1,0:T(8,128)S(1)}, u32[]{:S(2)}, u32[]{:S(2)}) collective-permute-start(f32[3,3,8,128]{3,2,1,0:T(8,128)S(1)} %get-tuple-element.64), channel_id=1, source_target_pairs={{0,3},{1,2},{2,1},{3,0},{4,7},{5,6},{6,5},{7,4},{8,11},{9,10},{10,... | collective-permute-start | bytes 110600 | tf_op jit(solution)/shard_map/ppermute | solution.py:428

commit v3 on v2

--- a/solution.py
+++ b/solution.py
@@ -9,13 +9,16 @@
 
 AGG_LOC = 32
 SWEEPS = 3
-INNER = 3
 HX = 2
 HY = 3
 
-TX, TY, TZ, ACC, CPL, RHS, CUR, IDX, FIELDS = 0, 1, 2, 3, 4, 13, 16, 19, 20
+TX, TY, TZ, CPL, RHS, CUR, IDX, FIELDS = 0, 1, 2, 3, 12, 15, 18, 19
 OUTER_X = (TX, CUR, CUR + 1, CUR + 2, IDX)
 OUTER_Y = (TY, CUR, CUR + 1, CUR + 2, IDX)
+CORNERS = ((-1, -1), (-1, 1), (1, -1), (1, 1))
+CORNER_TILES = ((1, 1), (1, 2), (2, 1))
+COLD = 2
+SLOT = (3, 4)
 GC, GI, GR, GFIELDS = 3, 12, 15, 18
 
 PARAMS = pltpu.CompilerParams(vmem_limit_bytes=16 * 1024 * 1024)
@@ -42,7 +45,6 @@
             out_specs=tuple(HBM if number in far_outs else VMEM for number in range(len(outs))),
             scratch_shapes=list(scratch),
             compiler_params=PARAMS,
-            name=body.func.__name__ if isinstance(body, functools.partial) else body.__name__,
         )(flags, *args)
 
     return run
@@ -77,13 +79,30 @@
     return lax.dot_general(left, right, (((1,), (1,)), ((), ())), preferred_element_type=jnp.float32)
 
 
-def pack_wide(flags, trans, accum, coupling, rhs, start, agg, far_cells, far_index, block, first, second, groups, cells, index, sems):
+def fetch(flags, factors, after, *refs):
+    *near, sems = refs
+    cold = near[0]
+    side = cold.shape[1] // 2
+    inside = factors.shape[1] - 2 * side
+    copies = [
+        (factors.at[:, pl.ds(0, side)], cold.at[:, pl.ds(0, side)]),
+        (factors.at[:, pl.ds(side + inside, side)], cold.at[:, pl.ds(side, side)]),
+    ]
+    copies += [(factors.at[:, pl.ds(side, inside)], hot) for hot in near[1:]]
+    copies = [pltpu.make_async_copy(source, target, sems.at[k]) for k, (source, target) in enumerate(copies)]
+    for copy in copies:
+        copy.start()
+    for copy in copies:
+        copy.wait()
+
+
+def pack_wide(flags, trans, accum, coupling, rhs, start, agg, far_cells, far_index, block, first, second, groups, near_accum, cells, index, sems):
     phases, px, cy, tile = rhs.shape
     conn = cells.shape[-1]
     copies = [
         (far_cells, cells),
         (far_index, index),
-        (accum, block.at[ACC]),
+        (accum, near_accum),
         (agg, groups),
         (trans, block.at[pl.ds(TX, 3)]),
         (rhs, block.at[pl.ds(RHS, phases)]),
@@ -104,7 +123,10 @@
     for copy in copies[2:]:
         copy.wait()
     for pair in range(px):
-        block[ACC, pair] = block[ACC, pair] + added[pair * cy : (pair + 1) * cy]
+        accum_w = near_accum[pair] + added[pair * cy : (pair + 1) * cy]
+        for c in range(phases):
+            number = CPL + c * phases + c
+            block[number, pair] = block[number, pair] + accum_w
         block[IDX, pair] = (groups[pair] + flags[4]).astype(jnp.float32)
     for number in range(FIELDS):
         one, two = sent(flags, 0, block[number, px - 1], block[number, 0])
@@ -207,18 +229,16 @@
     wide = share.shape[0]
     for i in range(wide):
         share[pl.ds(i, 1), :] = jnp.sum(cinv[:, i * lanes : (i + 1) * lanes] * sums, axis=0, keepdims=True)
-    pair_no = lax.broadcasted_iota(jnp.int32, (width, lanes), 0)
     for i in range(wide):
-        before = share[pl.ds((i - 1) % wide, 1), :]
-        here = share[pl.ds(i, 1), :]
-        after = share[pl.ds((i + 1) % wide, 1), :]
-        table = jnp.where(pair_no < HX, before, jnp.where(pair_no < HX + px, here, after))
-        for j in range(narrow):
-            slots[i * narrow + j] = table
-
-
-def misfit_and_share(flags, coeffs, current, misfit, index, cinv, slots, own_misfit, own_agg, share, px, cy, narrow):
+        for place in range(3):
+            row = share[pl.ds((i + place - 1) % wide, 1), :]
+            for j in range(narrow):
+                slots[i * narrow + j, pl.ds(place, 1), :] = row
+
+
+def find_misfit(coeffs, current, misfit, own_misfit):
     columns = current.shape[1]
+    cy = columns - 2 * HY
     half = lane_half(current.shape[2:])
     for column in range(1, columns - 1):
         applied = operate(lambda c, y: current[c, y], coeffs, column, half)
@@ -227,30 +247,63 @@
             misfit[c, column] = value
             if c == 0 and HY <= column < HY + cy:
                 own_misfit[column - HY] = value
+
+
+def sweep_body(flags, coeffs, current, index, cinv, hot, cold, slots, first, second, third, fourth, px, narrow, scratch, before):
+    misfit, work, hold, own_misfit, own_agg, share, update, near_slots, near_corners, sems = scratch
+    cy = update.shape[1]
+    owned = lax.broadcasted_iota(jnp.int32, current.shape[2:], 0) - HX
+    owned = (owned >= 0) & (owned < px)
+    before()
+    find_misfit(coeffs, current, misfit, own_misfit)
+    send = pltpu.make_async_copy(near_slots, slots.at[:, 0], sems.at[0])
+
+    def send_shares():
+        for column in range(cy):
+            own_agg[column] = index[HY + column] - flags[4]
+        coarse_share(rows_of(own_misfit), rows_of(own_agg), cinv, share, near_slots, px, cy, narrow)
+        send.start()
+
+    sends = []
+
+    def send_corners():
+        near = lane_half(update.shape[2:])
+        for number, (x, y) in enumerate(CORNERS):
+            rows = []
+            for pairs, columns in CORNER_TILES:
+                pair = HX + (px - pairs if x > 0 else pairs - 1)
+                column = cy - columns if y > 0 else columns - 1
+                tile = [update[c, column] for c in range(update.shape[0])]
+                if pairs == 2:
+                    turned = swap_half(tile[1])
+                    tile[0] = jnp.where(near, turned, tile[0]) if x > 0 else jnp.where(near, tile[0], turned)
+                    tile = [tile[0], tile[2]]
+                rows += [value[pair : pair + 1] for value in tile]
+            for spot, row in enumerate(rows):
+                near_corners[number, spot // SLOT[1], pl.ds(spot % SLOT[1], 1), :] = row
+            target = slots.at[flags[5 + number], pl.ds(1, SLOT[0] - 1)]
+            sends.append(pltpu.make_async_copy(near_corners.at[number], target, sems.at[1 + number]))
+        for corner in sends:
+            corner.start()
+
+    solve(flags, misfit, coeffs, hot, cold, update, first, second, third, fourth, work, hold, send_shares, send_corners)
     for column in range(cy):
-        own_agg[column] = index[HY + column] - flags[4]
-    coarse_share(rows_of(own_misfit), rows_of(own_agg), cinv, share, slots, px, cy, narrow)
-
-
-def sweep_body(flags, coeffs, current, index, cinv, hot, factors, update, slots, first, second, px, narrow, scratch):
-    misfit, work, hold, own_misfit, own_agg, share, near_slots, cold, sems = scratch
-    cy = update.shape[1]
-    edge = HY - 1
-    boxes = factors.shape[1]
-    loads = [
-        pltpu.make_async_copy(factors.at[:, pl.ds(0, edge)], cold.at[:, pl.ds(0, edge)], sems.at[0]),
-        pltpu.make_async_copy(factors.at[:, pl.ds(boxes - edge, edge)], cold.at[:, pl.ds(edge, edge)], sems.at[1]),
-    ]
-    for load in loads:
-        load.start()
-    misfit_and_share(flags, coeffs, current, misfit, index, cinv, near_slots, own_misfit, own_agg, share, px, cy, narrow)
-    send = pltpu.make_async_copy(near_slots, slots, sems.at[2])
-    send.start()
-    solve(flags, misfit, coeffs, hot, cold, loads, update, first, second, work, hold)
+        for c in range(update.shape[0]):
+            here = jnp.where(owned, update[c, column], 0.0)
+            current[c, HY + column] = current[c, HY + column] + here
     send.wait()
-
-
-def prepare(flags, own, got_first, got_second, cinv, hot, factors, coeffs, index, current, update, slots, first, second, field, *scratch, px, narrow):
+    for corner in sends:
+        corner.wait()
+
+
+def prepare(flags, own, got_first, got_second, cinv, hot, cold, coeffs, index, current, slots, first, second, third, fourth, field, *scratch, px, narrow):
+    def before():
+        assemble(flags, own, got_first, got_second, coeffs, index, current, field)
+
+    sweep_body(flags, coeffs, current, index, cinv, hot, cold, slots, first, second, third, fourth, px, narrow, scratch, before)
+
+
+def assemble(flags, own, got_first, got_second, coeffs, index, current, field):
     cy = own.shape[1]
     columns = cy + 2 * HY
     half = lane_half(own.shape[2:])
@@ -278,19 +331,17 @@
         tx, ty = field[TX, column], field[TY, column]
         tz = jnp.where(depth < own.shape[3] // 2 - 1, field[TZ, column], 0.0)
         faces = (tx + west_of(tx, half)) + (ty + field[TY, column - 1]) + (tz + below(tz))
-        centre = field[ACC, column] + faces
         coeffs[0, column] = tx
         coeffs[1, column] = ty
         coeffs[2, column] = tz
         for number in range(9):
             value = field[CPL + number, column]
             if number % 4 == 0:
-                value = value + centre
+                value = value + faces
                 coeffs[GI + number // 4, column] = 1.0 / value
             coeffs[GC + number, column] = value
         for c in range(3):
             coeffs[GR + c, column] = field[RHS + c, column]
-    sweep_body(flags, coeffs, current, index, cinv, hot, factors, update, slots, first, second, px, narrow, scratch)
 
 
 def tile_apply(values, coeffs, tiles, column, first, last):
@@ -304,49 +355,53 @@
     return [result[c * width : (c + 1) * width] for c in range(3)]
 
 
-def solve(flags, misfit, coeffs, hot, cold, loads, update, first, second, work, hold):
+def solve(flags, misfit, coeffs, hot, cold, update, first, second, third, fourth, work, hold, send_shares, send_corners):
     phases, columns = work.shape[:2]
     cy = columns - 2 * HY
-    boxes = hot.shape[0]
+    boxes, inside = hot.shape[:2]
     width = work.shape[2]
     px = width - 2 * HX
-    edge = HY - 1
     half = lane_half(work.shape[2:])
+    side = cold.shape[1] // 2
 
     def tiles(a, b):
-        if b < edge:
+        if b < side:
             return cold[a, b]
-        return hot[a, b - edge] if b < edge + cy else cold[a, b - cy]
+        return hot[a, b - side] if b < side + inside else cold[a, b - inside]
 
     for c in range(phases):
         work[c, 0] = jnp.zeros(work.shape[2:], jnp.float32)
         work[c, columns - 1] = jnp.zeros(work.shape[2:], jnp.float32)
-    inside = list(range(HY, HY + cy))
-    outside = [column for column in range(1, columns - 1) if column not in inside]
-    for column in inside + outside:
-        if column == outside[0]:
-            for load in loads:
-                load.wait()
+
+    def start(column):
         new = tile_apply([misfit[c, column] for c in range(phases)], coeffs, tiles, column, 0, boxes)
         for c in range(phases):
             work[c, column] = new[c]
-    for step in range(1, INNER):
-        spare = max(HY - 1 - (INNER - 1 - step), 0)
-        needed = range(1 + spare, columns - 1 - spare)
-        last = step == INNER - 1
-        first_box, last_box = (1, boxes - 1) if last else (0, boxes)
-        for column in needed:
-            applied = operate(lambda c, y: work[c, y], coeffs, column, half)
-            left = [misfit[c, column] - applied[c] for c in range(phases)]
-            new = tile_apply(left, coeffs, tiles, column, first_box, last_box)
-            for c in range(phases):
-                hold[c, column] = work[c, column] + new[c]
-        for column in needed:
-            for c in range(phases):
-                if last:
-                    update[c, column - HY] = hold[c, column]
-                else:
-                    work[c, column] = hold[c, column]
+
+    def step(source, target, shift, column, first_box, last_box):
+        applied = operate(lambda c, y: source[c, y], coeffs, column, half)
+        left = [misfit[c, column] - applied[c] for c in range(phases)]
+        new = tile_apply(left, coeffs, tiles, column, first_box, last_box)
+        for c in range(phases):
+            target[c, column - shift] = source[c, column] + new[c]
+
+    for column in range(1, columns - 1):
+        start(column)
+    send_shares()
+    edge = 2 * (HY - 1)
+    middle = range(2 + edge, columns - 2 - edge)
+    for column in range(2, columns - 2):
+        if column not in middle:
+            step(work, hold, 0, column, 0, boxes)
+    ends = [column for column in range(HY, HY + cy) if min(column - HY, HY + cy - 1 - column) < HY - 1]
+    for column in ends:
+        step(hold, update, HY, column, 1, boxes - 1)
+    send_corners()
+    for column in middle:
+        step(work, hold, 0, column, 0, boxes)
+    for column in range(HY, HY + cy):
+        if column not in ends:
+            step(hold, update, HY, column, 1, boxes - 1)
     rows = rows_of(update)
     for c in range(phases):
         for pair in range(HX):
@@ -355,54 +410,65 @@
             one, two = sent(flags, 0, tail, head)
             first[c, pair] = one
             second[c, pair] = two
-
-
-def widen(flags, update, got_first, got_second, whole, first, second):
-    phases, cy, width, _ = update.shape
+        for column in range(HY):
+            one, two = sent(flags, 1, update[c, cy - HY + column], update[c, column])
+            third[c, column] = one
+            fourth[c, column] = two
+
+
+def advance(flags, current, index, got, slots_in, result):
+    phases, columns, width, tile = current.shape
+    cy = columns - 2 * HY
     px = width - 2 * HX
-    whole[...] = update[...]
-    rows = rows_of(whole)
-    for c in range(phases):
-        for pair in range(HX):
-            low, high = received(flags, 0, got_first[c, pair], got_second[c, pair])
-            rows[pl.ds(c * cy * width + pair, cy, stride=width), :] = low
-            rows[pl.ds(c * cy * width + HX + px + pair, cy, stride=width), :] = high
-    for c in range(phases):
-        for column in range(HY):
-            one, two = sent(flags, 1, whole[c, cy - HY + column], whole[c, column])
-            first[c, column] = one
-            second[c, column] = two
-
-
-def advance(flags, current, index, whole, got_first, got_second, slots_in, result):
-    phases, columns = current.shape[:2]
-    cy = columns - 2 * HY
-    total = [slots_in[d] for d in range(min(4, slots_in.shape[0]))]
+    total = [slots_in[d, 0] for d in range(min(4, slots_in.shape[0]))]
     for d in range(4, slots_in.shape[0]):
-        total[d % 4] = total[d % 4] + slots_in[d]
-    table = sum(total[1:], total[0])
+        total[d % 4] = total[d % 4] + slots_in[d, 0]
+    total = sum(total[1:], total[0])
+    pair_no = lax.broadcasted_iota(jnp.int32, (width, tile), 0)
+    table = jnp.where(pair_no < HX, total[0:1], jnp.where(pair_no < HX + px, total[1:2], total[2:3]))
+    owned = (pair_no >= HX) & (pair_no < HX + px)
+    near = lane_half((width, tile))
     for column in range(columns):
         for c in range(phases):
-            if column < HY:
-                change = received(flags, 1, got_first[c, column], got_second[c, column])[0]
-            elif column < HY + cy:
-                change = whole[c, column - HY]
-            else:
-                place = column - HY - cy
-                change = received(flags, 1, got_first[c, place], got_second[c, place])[1]
+            change = 0.0
+            if not HY <= column < HY + cy:
+                y = -1 if column < HY else 1
+                place = column if y < 0 else column - HY - cy
+                away = HY - column if y < 0 else place + 1
+                change = jnp.where(owned, received(flags, 1, got[2][c, place], got[3][c, place])[(y + 1) // 2], 0.0)
+                for number, (x, side) in enumerate(CORNERS):
+                    for tile_no, (pairs, distance) in enumerate(CORNER_TILES):
+                        if side == y and distance == away:
+                            pair = HX - pairs if x < 0 else HX + px + pairs - 1
+                            spot = SLOT[1] + 3 * tile_no + (c if pairs == 1 else c // 2)
+                            source = slots_in.at[flags[5 + number], spot // SLOT[1], pl.ds(spot % SLOT[1], 1)]
+                            row = jnp.broadcast_to(source[...], (width, tile))
+                            if pairs == 2:
+                                row = swap_half(row) if c == 1 else row
+                                row = jnp.where(near, 0.0, row) if x < 0 else jnp.where(near, row, 0.0)
+                            change = jnp.where(pair_no == pair, row, change)
             value = current[c, column] + change
             if c == 0:
                 value = value + jnp.take_along_axis(table, index[column], axis=1)
             result[c, column] = value
-
-
-def next_sweep(flags, current, coeffs, index, whole, got_first, got_second, slots_in, cinv, hot, factors, result, update, slots, first, second, *scratch, px, narrow):
-    advance(flags, current, index, whole, got_first, got_second, slots_in, result)
-    sweep_body(flags, coeffs, result, index, cinv, hot, factors, update, slots, first, second, px, narrow, scratch)
-
-
-def finish(flags, current, coeffs, index, whole, got_first, got_second, slots_in, iterate, residual, result, misfit):
-    advance(flags, current, index, whole, got_first, got_second, slots_in, result)
+    flat = rows_of(result)
+    for c in range(phases):
+        for pair in range(HX):
+            low, high = received(flags, 0, got[0][c, pair], got[1][c, pair])
+            for place, change in ((pair, low), (HX + px + pair, high)):
+                where_to = pl.ds((c * columns + HY) * width + place, cy, stride=width)
+                flat[where_to, :] = flat[where_to, :] + change
+
+
+def next_sweep(flags, current, coeffs, index, got_0, got_1, got_2, got_3, slots_in, cinv, hot, cold, result, slots, first, second, third, fourth, *scratch, px, narrow):
+    def start():
+        advance(flags, current, index, (got_0, got_1, got_2, got_3), slots_in, result)
+
+    sweep_body(flags, coeffs, result, index, cinv, hot, cold, slots, first, second, third, fourth, px, narrow, scratch, start)
+
+
+def finish(flags, current, coeffs, index, got_0, got_1, got_2, got_3, slots_in, iterate, residual, result, misfit):
+    advance(flags, current, index, (got_0, got_1, got_2, got_3), slots_in, result)
     phases, px, cy, _ = iterate.shape
     columns, width = current.shape[1:3]
     half = lane_half(current.shape[2:])
@@ -425,7 +491,9 @@
             [(i, i ^ 1) for i in range(count)],
             [(i, (i + 1 if i % 2 else i - 1) % count) for i in range(count)],
         ]
-    return lax.ppermute(first, axis, pairs[0]), lax.ppermute(second, axis, pairs[1])
+    first = lax.ppermute(first, axis, pairs[0])
+    second = lax.ppermute(second, axis, pairs[1])
+    return first, second
 
 
 def order_flags():
@@ -434,7 +502,11 @@
         place = lax.axis_index(axis) % 2
         odd = lax.axis_size(axis) % 2
         flags += [0, 1] if odd else [place, place]
-    return jnp.stack([jnp.asarray(flag, jnp.int32) for flag in flags + [lax.axis_index("narrow") * AGG_LOC]])
+    flags.append(lax.axis_index("narrow") * AGG_LOC)
+    for x, y in CORNERS:
+        row = (lax.axis_index("wide") + x) % lax.axis_size("wide")
+        flags.append(row * lax.axis_size("narrow") + (lax.axis_index("narrow") + y) % lax.axis_size("narrow"))
+    return jnp.stack([jnp.asarray(flag, jnp.int32) for flag in flags])
 
 
 def per_device(
@@ -455,6 +527,15 @@
     f32 = jnp.float32
     flags = order_flags()
     lanes = narrow * AGG_LOC
+    if min(wide, narrow) < 3 or lanes != tile:
+        raise ValueError("unsupported mesh")
+
+    boxes = tile_factors.shape
+    cold = ((boxes[0], 2 * COLD) + boxes[2:], tile_factors.dtype)
+    hot = ((boxes[0], boxes[1] - 2 * COLD) + boxes[2:], tile_factors.dtype)
+
+    def tiles_after(value, outs):
+        return call(fetch, outs, [pltpu.SemaphoreType.DMA((3,))], far=(0,))(flags, tile_factors, value)
 
     face = ((FIELDS + len(OUTER_X), cy, tile), f32)
     block, first, second = call(
@@ -462,6 +543,7 @@
         [((FIELDS, px, cy, tile), f32), face, face],
         [
             pltpu.VMEM((px, cy, tile), jnp.int32),
+            pltpu.VMEM((px, cy, tile), f32),
             pltpu.VMEM(well_cells.shape, jnp.int32),
             pltpu.VMEM(well_index.shape, f32),
             pltpu.SemaphoreType.DMA((7 + phases,)),
@@ -474,15 +556,15 @@
         flags, block, first, second
     )
     first, second = swap(first, second, "narrow")
+    cold_tiles, hot_tiles = tiles_after(own, [cold, hot])
 
     vec = (width, tile)
     field = ((phases, columns) + vec, f32)
     inner = ((phases, columns - 1) + vec, f32)
-    slot = ((wide * narrow, width, lanes), f32)
+    slot = ((wide * narrow,) + SLOT + (lanes,), f32)
     part = ((phases, cy) + vec, f32)
     face = ((phases, HX, cy, tile), f32)
     edge_face = ((phases, HY) + vec, f32)
-    boxes = tile_factors.shape
     scratch = [
         pltpu.VMEM(*inner),
         pltpu.VMEM(*field),
@@ -490,34 +572,33 @@
         pltpu.VMEM((cy,) + vec, f32),
         pltpu.VMEM((cy,) + vec, jnp.int32),
         pltpu.VMEM((wide, lanes), f32),
-        pltpu.VMEM(*slot),
-        pltpu.VMEM((boxes[0], 2 * (HY - 1)) + boxes[2:], tile_factors.dtype),
-        pltpu.SemaphoreType.DMA((3,)),
+        pltpu.VMEM(*part),
+        pltpu.VMEM((wide * narrow,) + SLOT[1:] + (lanes,), f32),
+        pltpu.VMEM((len(CORNERS), SLOT[0] - 1) + SLOT[1:] + (lanes,), f32),
+        pltpu.SemaphoreType.DMA((1 + len(CORNERS),)),
     ]
-    hot = tile_factors[:, HY - 1 : HY - 1 + cy]
-    coeffs, index, current, update, slots, first, second = call(
+    faces = [face, face, edge_face, edge_face]
+    coeffs, index, current, slots, *sends = call(
         functools.partial(prepare, px=px, narrow=narrow),
-        [((GFIELDS, columns - 1) + vec, f32), ((columns,) + vec, jnp.int32), field, part, slot, face, face],
+        [((GFIELDS, columns - 1) + vec, f32), ((columns,) + vec, jnp.int32), field, slot] + faces,
         [pltpu.VMEM((FIELDS, columns) + vec, f32)] + scratch,
-        far=(5,),
-        far_outs=(4,),
-    )(flags, own, first, second, coarse_inverse, hot, tile_factors)
+        far_outs=(3,),
+    )(flags, own, first, second, coarse_inverse, hot_tiles, cold_tiles)
     for sweep in range(SWEEPS):
         gathered = lax.all_to_all(slots, ("wide", "narrow"), 0, 0, tiled=True)
-        first, second = swap(first, second, "wide")
-        whole, first, second = call(widen, [part, edge_face, edge_face])(flags, update, first, second)
-        first, second = swap(first, second, "narrow")
+        got = swap(*sends[:2], "wide") + swap(*sends[2:], "narrow")
         if sweep < SWEEPS - 1:
-            current, update, slots, first, second = call(
+            (cold_tiles,) = tiles_after(gathered, [cold])
+        if sweep < SWEEPS - 1:
+            current, slots, *sends = call(
                 functools.partial(next_sweep, px=px, narrow=narrow),
-                [field, part, slot, face, face],
+                [field, slot] + faces,
                 scratch,
-                far=(9,),
-                far_outs=(2,),
-            )(flags, current, coeffs, index, whole, first, second, gathered, coarse_inverse, hot, tile_factors)
+                far_outs=(1,),
+            )(flags, current, coeffs, index, *got, gathered, coarse_inverse, hot_tiles, cold_tiles)
     out = (rhs.shape, f32)
     return call(finish, [out, out], [pltpu.VMEM(*field), pltpu.VMEM(*field)])(
-        flags, current, coeffs, index, whole, first, second, gathered
+        flags, current, coeffs, index, *got, gathered
     )
 
 

time: 84.9 us -> 73.8 us (0.87)
  waiting for transfers between devices: 22.6 us -> 13.9 us
  starting transfers between devices: 42.6 us -> 39.3 us
  Pallas kernels: 16.9 us -> 19.2 us
  local copies, waits for them, and re-layouts: 1.6 us -> 0.09 us
    ppermute x16, waiting for transfers between devices: 22.6 us -> 9.43 us  [the longest x8 8.8 us: swap(): second = lax.ppermute(second, axis, pairs[1])]
    all_to_all x3, waiting for transfers between devices: 0.01 us -> 4.45 us  [per_device(): gathered = lax.all_to_all(slots, ('wide', 'narrow'), 0, 0, tiled=True)]
    all_to_all x3, starting transfers between devices: 14.1 us -> 10.8 us  [per_device(): gathered = lax.all_to_all(slots, ('wide', 'narrow'), 0, 0, tiled=True)]
    pallas_call x9, Pallas kernels: 16.9 us -> 19.2 us  [run(): pl.pallas_call(body, out_shape=tuple(((pltpu.HBM if number in far_outs el...]
    slice x1 -> x0, local copies, waits for them, and re-layouts: 1.51 us -> none  [per_device(): hot = tile_factors[:, HY - 1:HY - 1 + cy]]
  transfers between devices with their start and end apart: 19 -> 19, of which waited for: 9 -> 6; matrix products, arithmetic and copies ran while one was open for 2% -> 0% of each run, Pallas kernels for 2% -> 8%
where the time goes in v3:
time: 73.8 us; the launch traced here: 73.4 us
  starting transfers between devices  39.3 us (53%)
  Pallas kernels  19.2 us (26%)
  waiting for transfers between devices  13.9 us (19%)
  between operations  0.89 us (1%)
    ppermute x8, starting transfers between devices, swap(): second = lax.ppermute(second, axis, pairs[1])  20 us
    pallas_call x9, Pallas kernels, run(): pl.pallas_call(body, out_shape=tuple(((pltpu.HBM if number in far_outs el...  19.2 us
    all_to_all x3, starting transfers between devices, per_device(): gathered = lax.all_to_all(slots, ('wide', 'narrow'), 0, 0, tiled=True)  10.8 us
    ppermute x8, waiting for transfers between devices, swap(): second = lax.ppermute(second, axis, pairs[1])  8.8 us
    ppermute x8, starting transfers between devices, swap(): first = lax.ppermute(first, axis, pairs[0])  8.47 us
    all_to_all x3, waiting for transfers between devices, per_device(): gathered = lax.all_to_all(slots, ('wide', 'narrow'), 0, 0, tiled=True)  4.45 us
  transfers between devices with their start and end apart: 19, of which 6 were waited for; matrix products, arithmetic and copies ran while one was open for 0% of the time, Pallas kernels for 8%

profile of v3, /device:TPU:0, one launch (start us, length us, event | category | flops | bytes accessed | tf_op | source)
XLA Modules:
  0.0 73.4 jit_solution(13490136634926940392)
XLA Ops:
  0.7 0.1 stack.33.flags
  0.8 1.6 %shard_map.113 = (f32[19,4,8,128]{3,2,1,0:T(8,128)S(1)}, f32[24,8,128]{2,1,0:T(8,128)S(1)}, f32[24,8,128]{2,1,0:T(8,128)S(1)}) custom-call(s32[9]{0:T(128)S(1)} %stack.33.flags, f32[3,4,8,128]{3,2,1,0:T(8,128)} %trans.1, f32[4,8,128]{2,1,0:T(8,128)} %accum.1, f32[3,3,4,8,128]{4,3,2,1,0:T(8,128)} %coupling.1, f32[3,4,8,128]{3,2,1,0:T(8,128)} %rhs.1, ...), custom_call_target="tpu_custom_call" | custom-call | tf_op jit(solution)/shard_map/pallas_call | solution.py:39
  2.4 3.1 %collective-permute-start = (f32[24,8,128]{2,1,0:T(8,128)S(1)}, f32[24,8,128]{2,1,0:T(8,128)S(1)}, u32[]{:S(2)}, u32[]{:S(2)}) collective-permute-start(f32[24,8,128]{2,1,0:T(8,128)S(1)} %get-tuple-element.31), channel_id=1, source_target_pairs={{0,4},{4,0},{8,12},{12,8},{16,20},{20,16},{24,28},{28,24},{1,5},{5... | collective-permute-start | bytes 294920 | tf_op jit(solution)/shard_map/ppermute | solution.py:494
  5.5 3.5 %collective-permute-start.1 = (f32[24,8,128]{2,1,0:T(8,128)S(1)}, f32[24,8,128]{2,1,0:T(8,128)S(1)}, u32[]{:S(2)}, u32[]{:S(2)}) collective-permute-start(f32[24,8,128]{2,1,0:T(8,128)S(1)} %get-tuple-element.32), channel_id=1, source_target_pairs={{0,28},{4,8},{8,4},{12,16},{16,12},{20,24},{24,20},{28,0},{1,29},{... | collective-permute-start | bytes 294920 | tf_op jit(solution)/shard_map/ppermute | solution.py:495
  9.0 0.6 collective-permute-done.got_first
  9.7 3.2 %collective-permute-done.1.got_second = f32[24,8,128]{2,1,0:T(8,128)S(1)} collective-permute-done((f32[24,8,128]{2,1,0:T(8,128)S(1)}, f32[24,8,128]{2,1,0:T(8,128)S(1)}, u32[]{:S(2)}, u32[]{:S(2)}) %collective-permute-start.1) | collective-permute-done | bytes 98336 | tf_op jit(solution)/shard_map/ppermute | solution.py:495
  12.8 0.7 shard_map.114
  13.5 0.1 collective-permute-start.2
  13.6 1.6 %collective-permute-start.3 = (f32[43,8,128]{2,1,0:T(8,128)S(1)}, f32[43,8,128]{2,1,0:T(8,128)S(1)}, u32[]{:S(2)}, u32[]{:S(2)}) collective-permute-start(f32[43,8,128]{2,1,0:T(8,128)S(1)} %get-tuple-element.35), channel_id=1, source_target_pairs={{0,3},{1,2},{2,1},{3,0},{4,7},{5,6},{6,5},{7,4},{8,11},{9,10},{10,... | collective-permute-start | bytes 528392 | tf_op jit(solution)/shard_map/ppermute | solution.py:495
  15.1 2.2 %shard_map.115 = (bf16[6,4,128,128]{3,2,1,0:T(8,128)(2,1)S(1)}, bf16[6,8,128,128]{3,2,1,0:T(8,128)(2,1)S(1)}) custom-call(s32[9]{0:T(128)S(1)} %stack.33.flags, bf16[6,12,128,128]{3,2,1,0:T(8,128)(2,1)} %factors.5, f32[19,8,8,128]{3,2,1,0:T(8,128)S(1)} %get-tuple-element.33.after.own), custom_call_target="tpu_custom_call" | custom-call | tf_op jit(solution)/shard_map/pallas_call | solution.py:39
  17.4 0.0 collective-permute-done.2.got_first
  17.4 2.4 %collective-permute-done.3.got_second = f32[43,8,128]{2,1,0:T(8,128)S(1)} collective-permute-done((f32[43,8,128]{2,1,0:T(8,128)S(1)}, f32[43,8,128]{2,1,0:T(8,128)S(1)}, u32[]{:S(2)}, u32[]{:S(2)}) %collective-permute-start.3) | collective-permute-done | bytes 176160 | tf_op jit(solution)/shard_map/ppermute | solution.py:495
  19.8 3.2 %shard_map.116 = (f32[18,13,8,128]{3,2,1,0:T(8,128)S(1)}, s32[14,8,128]{2,1,0:T(8,128)S(1)}, f32[3,14,8,128]{3,2,1,0:T(8,128)S(1)}, f32[32,3,4,128]{3,2,1,0:T(4,...) custom-call(s32[9]{0:T(128)S(1)} %stack.33.flags, ...), custom_call_target="tpu_custom_call" | custom-call | tf_op jit(solution)/shard_map/pallas_call | solution.py:39
  23.0 4.9 %all-to-all-start = ((f32[32,3,4,128]{3,2,1,0:T(4,128)}), f32[32,3,4,128]{3,2,1,0:T(4,128)S(1)}, u32[]{:S(2)}, u32[]{:S(2)}) async-start(f32[32,3,4,128]{3,2,1,0:T(4,128)} %get-tuple-element.45), calls=%async_computation | async-start | bytes 393216 | tf_op jit(solution)/shard_map/all_to_all | solution.py:588
  27.8 0.3 collective-permute-start.6
  28.1 1.6 %collective-permute-start.7 = (f32[3,3,8,128]{3,2,1,0:T(8,128)S(1)}, f32[3,3,8,128]{3,2,1,0:T(8,128)S(1)}, u32[]{:S(2)}, u32[]{:S(2)}) collective-permute-start(f32[3,3,8,128]{3,2,1,0:T(8,128)S(1)} %get-tuple-element.44), channel_id=1, source_target_pairs={{0,3},{1,2},{2,1},{3,0},{4,7},{5,6},{6,5},{7,4},{8,11},{9,10},{10,... | collective-permute-start | bytes 110600 | tf_op jit(solution)/shard_map/ppermute | solution.py:495
  29.8 1.5 %collective-permute-start.4 = (f32[3,2,8,128]{3,2,1,0:T(8,128)S(1)}, f32[3,2,8,128]{3,2,1,0:T(8,128)S(1)}, u32[]{:S(2)}, u32[]{:S(2)}) collective-permute-start(f32[3,2,8,128]{3,2,1,0:T(8,128)S(1)} %get-tuple-element.41), channel_id=1, source_target_pairs={{0,4},{4,0},{8,12},{12,8},{16,20},{20,16},{24,28},{28,24},{1,5},{5... | collective-permute-start | bytes 73736 | tf_op jit(solution)/shard_map/ppermute | solution.py:494
  31.2 3.3 %collective-permute-start.5 = (f32[3,2,8,128]{3,2,1,0:T(8,128)S(1)}, f32[3,2,8,128]{3,2,1,0:T(8,128)S(1)}, u32[]{:S(2)}, u32[]{:S(2)}) collective-permute-start(f32[3,2,8,128]{3,2,1,0:T(8,128)S(1)} %get-tuple-element.42), channel_id=1, source_target_pairs={{0,28},{4,8},{8,4},{12,16},{16,12},{20,24},{24,20},{28,0},{1,29},{... | collective-permute-start | bytes 73736 | tf_op jit(solution)/shard_map/ppermute | solution.py:495
  34.6 2.2 %all-to-all-done.after.slots_in = f32[32,3,4,128]{3,2,1,0:T(4,128)S(1)} async-done(((f32[32,3,4,128]{3,2,1,0:T(4,128)}), f32[32,3,4,128]{3,2,1,0:T(4,128)S(1)}, u32[]{:S(2)}, u32[]{:S(2)}) %all-to-all-start) | async-done | bytes 196640 | tf_op jit(solution)/shard_map/all_to_all | solution.py:588
  36.8 1.7 %shard_map.117.cold = bf16[6,4,128,128]{3,2,1,0:T(8,128)(2,1)S(1)} custom-call(s32[9]{0:T(128)S(1)} %stack.33.flags, bf16[6,12,128,128]{3,2,1,0:T(8,128)(2,1)} %factors.5, f32[32,3,4,128]{3,2,1,0:T(4,128)S(1)} %all-to-all-done.after.slots_in), custom_call_target="tpu_custom_call" | custom-call | tf_op jit(solution)/shard_map/pallas_call | solution.py:39
  38.5 0.0 collective-permute-done.4.got_0
  38.5 0.0 collective-permute-done.5.got_1
  38.5 0.0 collective-permute-done.6.got_2
  38.5 0.0 collective-permute-done.7.got_3
  38.5 3.4 %shard_map.118 = (f32[3,14,8,128]{3,2,1,0:T(8,128)S(1)}, f32[32,3,4,128]{3,2,1,0:T(4,128)}, f32[3,2,8,128]{3,2,1,0:T(8,128)S(1)}, f32[3,2,8,128]{3,2,1,0:T(8,128...) custom-call(s32[9]{0:T(128)S(1)} %stack.33.flags, f32[3,14,8,128]{3,2,1,0:T(8,128)S(1)} %get-tuple-element.38.current, ...), custom_call_target="tpu_custom_call" | custom-call | tf_op jit(solution)/shard_map/pallas_call | solution.py:39
  41.9 3.0 %all-to-all-start.1 = ((f32[32,3,4,128]{3,2,1,0:T(4,128)}), f32[32,3,4,128]{3,2,1,0:T(4,128)S(1)}, u32[]{:S(2)}, u32[]{:S(2)}) async-start(f32[32,3,4,128]{3,2,1,0:T(4,128)} %get-tuple-element.51), calls=%async_computation.1 | async-start | bytes 393216 | tf_op jit(solution)/shard_map/all_to_all | solution.py:588
  44.9 0.3 collective-permute-start.10
  45.2 1.6 %collective-permute-start.11 = (f32[3,3,8,128]{3,2,1,0:T(8,128)S(1)}, f32[3,3,8,128]{3,2,1,0:T(8,128)S(1)}, u32[]{:S(2)}, u32[]{:S(2)}) collective-permute-start(f32[3,3,8,128]{3,2,1,0:T(8,128)S(1)} %get-tuple-element.50), channel_id=1, source_target_pairs={{0,3},{1,2},{2,1},{3,0},{4,7},{5,6},{6,5},{7,4},{8,11},{9,10},{10,... | collective-permute-start | bytes 110600 | tf_op jit(solution)/shard_map/ppermute | solution.py:495
  46.8 1.5 %collective-permute-start.8 = (f32[3,2,8,128]{3,2,1,0:T(8,128)S(1)}, f32[3,2,8,128]{3,2,1,0:T(8,128)S(1)}, u32[]{:S(2)}, u32[]{:S(2)}) collective-permute-start(f32[3,2,8,128]{3,2,1,0:T(8,128)S(1)} %get-tuple-element.47), channel_id=1, source_target_pairs={{0,4},{4,0},{8,12},{12,8},{16,20},{20,16},{24,28},{28,24},{1,5},{5... | collective-permute-start | bytes 73736 | tf_op jit(solution)/shard_map/ppermute | solution.py:494
  48.3 3.3 %collective-permute-start.9 = (f32[3,2,8,128]{3,2,1,0:T(8,128)S(1)}, f32[3,2,8,128]{3,2,1,0:T(8,128)S(1)}, u32[]{:S(2)}, u32[]{:S(2)}) collective-permute-start(f32[3,2,8,128]{3,2,1,0:T(8,128)S(1)} %get-tuple-element.48), channel_id=1, source_target_pairs={{0,28},{4,8},{8,4},{12,16},{16,12},{20,24},{24,20},{28,0},{1,29},{... | collective-permute-start | bytes 73736 | tf_op jit(solution)/shard_map/ppermute | solution.py:495
  51.6 2.2 %all-to-all-done.1.after.slots_in = f32[32,3,4,128]{3,2,1,0:T(4,128)S(1)} async-done(((f32[32,3,4,128]{3,2,1,0:T(4,128)}), f32[32,3,4,128]{3,2,1,0:T(4,128)S(1)}, u32[]{:S(2)}, u32[]{:S(2)}) %all-to-all-start.1) | async-done | bytes 196640 | tf_op jit(solution)/shard_map/all_to_all | solution.py:588
  53.8 1.7 %shard_map.119.cold = bf16[6,4,128,128]{3,2,1,0:T(8,128)(2,1)S(1)} custom-call(s32[9]{0:T(128)S(1)} %stack.33.flags, bf16[6,12,128,128]{3,2,1,0:T(8,128)(2,1)} %factors.5, f32[32,3,4,128]{3,2,1,0:T(4,128)S(1)} %all-to-all-done.1.after.slots_in), custom_call_target="tpu_custom_call" | custom-call | tf_op jit(solution)/shard_map/pallas_call | solution.py:39
  55.5 0.0 collective-permute-done.8.got_0
  55.5 0.0 collective-permute-done.9.got_1
  55.6 0.0 collective-permute-done.10.got_2
  55.6 0.0 collective-permute-done.11.got_3
  55.6 3.4 %shard_map.120 = (f32[3,14,8,128]{3,2,1,0:T(8,128)S(1)}, f32[32,3,4,128]{3,2,1,0:T(4,128)}, f32[3,2,8,128]{3,2,1,0:T(8,128)S(1)}, f32[3,2,8,128]{3,2,1,0:T(8,128...) custom-call(s32[9]{0:T(128)S(1)} %stack.33.flags, f32[3,14,8,128]{3,2,1,0:T(8,128)S(1)} %get-tuple-element.46.current, ...), custom_call_target="tpu_custom_call" | custom-call | tf_op jit(solution)/shard_map/pallas_call | solution.py:39
  59.0 3.0 %all-to-all-start.2 = ((f32[32,3,4,128]{3,2,1,0:T(4,128)}), f32[32,3,4,128]{3,2,1,0:T(4,128)S(1)}, u32[]{:S(2)}, u32[]{:S(2)}) async-start(f32[32,3,4,128]{3,2,1,0:T(4,128)} %get-tuple-element.57), calls=%async_computation.2 | async-start | bytes 393216 | tf_op jit(solution)/shard_map/all_to_all | solution.py:588
  61.9 0.3 collective-permute-start.14
  62.2 1.6 %collective-permute-start.15 = (f32[3,3,8,128]{3,2,1,0:T(8,128)S(1)}, f32[3,3,8,128]{3,2,1,0:T(8,128)S(1)}, u32[]{:S(2)}, u32[]{:S(2)}) collective-permute-start(f32[3,3,8,128]{3,2,1,0:T(8,128)S(1)} %get-tuple-element.56), channel_id=1, source_target_pairs={{0,3},{1,2},{2,1},{3,0},{4,7},{5,6},{6,5},{7,4},{8,11},{9,10},{10,... | collective-permute-start | bytes 110600 | tf_op jit(solution)/shard_map/ppermute | solution.py:495
  63.9 1.5 %collective-permute-start.12 = (f32[3,2,8,128]{3,2,1,0:T(8,128)S(1)}, f32[3,2,8,128]{3,2,1,0:T(8,128)S(1)}, u32[]{:S(2)}, u32[]{:S(2)}) collective-permute-start(f32[3,2,8,128]{3,2,1,0:T(8,128)S(1)} %get-tuple-element.53), channel_id=1, source_target_pairs={{0,4},{4,0},{8,12},{12,8},{16,20},{20,16},{24,28},{28,24},{1,5},{5... | collective-permute-start | bytes 73736 | tf_op jit(solution)/shard_map/ppermute | solution.py:494
  65.3 3.3 %collective-permute-start.13 = (f32[3,2,8,128]{3,2,1,0:T(8,128)S(1)}, f32[3,2,8,128]{3,2,1,0:T(8,128)S(1)}, u32[]{:S(2)}, u32[]{:S(2)}) collective-permute-start(f32[3,2,8,128]{3,2,1,0:T(8,128)S(1)} %get-tuple-element.54), channel_id=1, source_target_pairs={{0,28},{4,8},{8,4},{12,16},{16,12},{20,24},{24,20},{28,0},{1,29},{... | collective-permute-start | bytes 73736 | tf_op jit(solution)/shard_map/ppermute | solution.py:495
  68.7 0.0 collective-permute-done.12.got_0
  68.7 3.3 %collective-permute-done.13.got_1 = f32[3,2,8,128]{3,2,1,0:T(8,128)S(1)} collective-permute-done((f32[3,2,8,128]{3,2,1,0:T(8,128)S(1)}, f32[3,2,8,128]{3,2,1,0:T(8,128)S(1)}, u32[]{:S(2)}, u32[]{:S(2)}) %collective-permute-start.13) | collective-permute-done | bytes 24608 | tf_op jit(solution)/shard_map/ppermute | solution.py:495
  71.9 0.0 collective-permute-done.14.got_2
  71.9 0.0 collective-permute-done.15.got_3
  71.9 0.0 all-to-all-done.2.slots_in
  71.9 1.4 %shard_map.121 = (f32[3,4,8,128]{3,2,1,0:T(8,128)}, f32[3,4,8,128]{3,2,1,0:T(8,128)}) custom-call(s32[9]{0:T(128)S(1)} %stack.33.flags, f32[3,14,8,128]{3,2,1,0:T(8,128)S(1)} %get-tuple-element.52.current, f32[18,13,8,128]{3,2,1,0:T(8,128)S(1)} %get-tuple-element.39.coeffs, s32[14,8,128]{2,1,0:T(8,128)S(1)} %get-tuple-element.40.index, ...), custom_call_target="tpu_custom_call" | custom-call | tf_op jit(solution)/shard_map/pallas_call | solution.py:39
  (2 shorter events, 0.0 us)
Async XLA Ops:
  0.6 19.1 %copy-start = (f32[32,1024]{1,0:T(8,128)S(1)}, f32[32,1024]{1,0:T(8,128)}, u32[]{:S(2)}) copy-start(f32[32,1024]{1,0:T(8,128)} %cinv.5) | copy-start | bytes 393220
  2.4 7.2 %collective-permute-start = (f32[24,8,128]{2,1,0:T(8,128)S(1)}, f32[24,8,128]{2,1,0:T(8,128)S(1)}, u32[]{:S(2)}, u32[]{:S(2)}) collective-permute-start(f32[24,8,128]{2,1,0:T(8,128)S(1)} %get-tuple-element.31), channel_id=1, source_target_pairs={{0,4},{4,0},{8,12},{12,8},{16,20},{20,16},{24,28},{28,24},{1,5},{5... | collective-permute-start | bytes 294920 | tf_op jit(solution)/shard_map/ppermute | solution.py:494
  5.5 7.3 %collective-permute-start.1 = (f32[24,8,128]{2,1,0:T(8,128)S(1)}, f32[24,8,128]{2,1,0:T(8,128)S(1)}, u32[]{:S(2)}, u32[]{:S(2)}) collective-permute-start(f32[24,8,128]{2,1,0:T(8,128)S(1)} %get-tuple-element.32), channel_id=1, source_target_pairs={{0,28},{4,8},{8,4},{12,16},{16,12},{20,24},{24,20},{28,0},{1,29},{... | collective-permute-start | bytes 294920 | tf_op jit(solution)/shard_map/ppermute | solution.py:495
  13.5 3.9 %collective-permute-start.2 = (f32[43,8,128]{2,1,0:T(8,128)S(1)}, f32[43,8,128]{2,1,0:T(8,128)S(1)}, u32[]{:S(2)}, u32[]{:S(2)}) collective-permute-start(f32[43,8,128]{2,1,0:T(8,128)S(1)} %get-tuple-element.34), channel_id=1, source_target_pairs={{0,1},{1,0},{2,3},{3,2},{4,5},{5,4},{6,7},{7,6},{8,9},{9,8},{10,11... | collective-permute-start | bytes 528392 | tf_op jit(solution)/shard_map/ppermute | solution.py:494
  13.6 6.2 %collective-permute-start.3 = (f32[43,8,128]{2,1,0:T(8,128)S(1)}, f32[43,8,128]{2,1,0:T(8,128)S(1)}, u32[]{:S(2)}, u32[]{:S(2)}) collective-permute-start(f32[43,8,128]{2,1,0:T(8,128)S(1)} %get-tuple-element.35), channel_id=1, source_target_pairs={{0,3},{1,2},{2,1},{3,0},{4,7},{5,6},{6,5},{7,4},{8,11},{9,10},{10,... | collective-permute-start | bytes 528392 | tf_op jit(solution)/shard_map/ppermute | solution.py:495
  23.0 13.8 %all-to-all-start = ((f32[32,3,4,128]{3,2,1,0:T(4,128)}), f32[32,3,4,128]{3,2,1,0:T(4,128)S(1)}, u32[]{:S(2)}, u32[]{:S(2)}) async-start(f32[32,3,4,128]{3,2,1,0:T(4,128)} %get-tuple-element.45), calls=%async_computation | async-start | bytes 393216 | tf_op jit(solution)/shard_map/all_to_all | solution.py:588
  27.8 10.7 %collective-permute-start.6 = (f32[3,3,8,128]{3,2,1,0:T(8,128)S(1)}, f32[3,3,8,128]{3,2,1,0:T(8,128)S(1)}, u32[]{:S(2)}, u32[]{:S(2)}) collective-permute-start(f32[3,3,8,128]{3,2,1,0:T(8,128)S(1)} %get-tuple-element.43), channel_id=1, source_target_pairs={{0,1},{1,0},{2,3},{3,2},{4,5},{5,4},{6,7},{7,6},{8,9},{9,8},{10,11... | collective-permute-start | bytes 110600 | tf_op jit(solution)/shard_map/ppermute | solution.py:494
  28.1 10.4 %collective-permute-start.7 = (f32[3,3,8,128]{3,2,1,0:T(8,128)S(1)}, f32[3,3,8,128]{3,2,1,0:T(8,128)S(1)}, u32[]{:S(2)}, u32[]{:S(2)}) collective-permute-start(f32[3,3,8,128]{3,2,1,0:T(8,128)S(1)} %get-tuple-element.44), channel_id=1, source_target_pairs={{0,3},{1,2},{2,1},{3,0},{4,7},{5,6},{6,5},{7,4},{8,11},{9,10},{10,... | collective-permute-start | bytes 110600 | tf_op jit(solution)/shard_map/ppermute | solution.py:495
  29.8 8.7 %collective-permute-start.4 = (f32[3,2,8,128]{3,2,1,0:T(8,128)S(1)}, f32[3,2,8,128]{3,2,1,0:T(8,128)S(1)}, u32[]{:S(2)}, u32[]{:S(2)}) collective-permute-start(f32[3,2,8,128]{3,2,1,0:T(8,128)S(1)} %get-tuple-element.41), channel_id=1, source_target_pairs={{0,4},{4,0},{8,12},{12,8},{16,20},{20,16},{24,28},{28,24},{1,5},{5... | collective-permute-start | bytes 73736 | tf_op jit(solution)/shard_map/ppermute | solution.py:494
  31.2 7.3 %collective-permute-start.5 = (f32[3,2,8,128]{3,2,1,0:T(8,128)S(1)}, f32[3,2,8,128]{3,2,1,0:T(8,128)S(1)}, u32[]{:S(2)}, u32[]{:S(2)}) collective-permute-start(f32[3,2,8,128]{3,2,1,0:T(8,128)S(1)} %get-tuple-element.42), channel_id=1, source_target_pairs={{0,28},{4,8},{8,4},{12,16},{16,12},{20,24},{24,20},{28,0},{1,29},{... | collective-permute-start | bytes 73736 | tf_op jit(solution)/shard_map/ppermute | solution.py:495
  41.9 11.9 %all-to-all-start.1 = ((f32[32,3,4,128]{3,2,1,0:T(4,128)}), f32[32,3,4,128]{3,2,1,0:T(4,128)S(1)}, u32[]{:S(2)}, u32[]{:S(2)}) async-start(f32[32,3,4,128]{3,2,1,0:T(4,128)} %get-tuple-element.51), calls=%async_computation.1 | async-start | bytes 393216 | tf_op jit(solution)/shard_map/all_to_all | solution.py:588
  44.9 10.7 %collective-permute-start.10 = (f32[3,3,8,128]{3,2,1,0:T(8,128)S(1)}, f32[3,3,8,128]{3,2,1,0:T(8,128)S(1)}, u32[]{:S(2)}, u32[]{:S(2)}) collective-permute-start(f32[3,3,8,128]{3,2,1,0:T(8,128)S(1)} %get-tuple-element.49), channel_id=1, source_target_pairs={{0,1},{1,0},{2,3},{3,2},{4,5},{5,4},{6,7},{7,6},{8,9},{9,8},{10,11... | collective-permute-start | bytes 110600 | tf_op jit(solution)/shard_map/ppermute | solution.py:494
  45.2 10.4 %collective-permute-start.11 = (f32[3,3,8,128]{3,2,1,0:T(8,128)S(1)}, f32[3,3,8,128]{3,2,1,0:T(8,128)S(1)}, u32[]{:S(2)}, u32[]{:S(2)}) collective-permute-start(f32[3,3,8,128]{3,2,1,0:T(8,128)S(1)} %get-tuple-element.50), channel_id=1, source_target_pairs={{0,3},{1,2},{2,1},{3,0},{4,7},{5,6},{6,5},{7,4},{8,11},{9,10},{10,... | collective-permute-start | bytes 110600 | tf_op jit(solution)/shard_map/ppermute | solution.py:495
  46.8 8.7 %collective-permute-start.8 = (f32[3,2,8,128]{3,2,1,0:T(8,128)S(1)}, f32[3,2,8,128]{3,2,1,0:T(8,128)S(1)}, u32[]{:S(2)}, u32[]{:S(2)}) collective-permute-start(f32[3,2,8,128]{3,2,1,0:T(8,128)S(1)} %get-tuple-element.47), channel_id=1, source_target_pairs={{0,4},{4,0},{8,12},{12,8},{16,20},{20,16},{24,28},{28,24},{1,5},{5... | collective-permute-start | bytes 73736 | tf_op jit(solution)/shard_map/ppermute | solution.py:494
  48.3 7.3 %collective-permute-start.9 = (f32[3,2,8,128]{3,2,1,0:T(8,128)S(1)}, f32[3,2,8,128]{3,2,1,0:T(8,128)S(1)}, u32[]{:S(2)}, u32[]{:S(2)}) collective-permute-start(f32[3,2,8,128]{3,2,1,0:T(8,128)S(1)} %get-tuple-element.48), channel_id=1, source_target_pairs={{0,28},{4,8},{8,4},{12,16},{16,12},{20,24},{24,20},{28,0},{1,29},{... | collective-permute-start | bytes 73736 | tf_op jit(solution)/shard_map/ppermute | solution.py:495
  59.0 13.0 %all-to-all-start.2 = ((f32[32,3,4,128]{3,2,1,0:T(4,128)}), f32[32,3,4,128]{3,2,1,0:T(4,128)S(1)}, u32[]{:S(2)}, u32[]{:S(2)}) async-start(f32[32,3,4,128]{3,2,1,0:T(4,128)} %get-tuple-element.57), calls=%async_computation.2 | async-start | bytes 393216 | tf_op jit(solution)/shard_map/all_to_all | solution.py:588
  61.9 10.0 %collective-permute-start.14 = (f32[3,3,8,128]{3,2,1,0:T(8,128)S(1)}, f32[3,3,8,128]{3,2,1,0:T(8,128)S(1)}, u32[]{:S(2)}, u32[]{:S(2)}) collective-permute-start(f32[3,3,8,128]{3,2,1,0:T(8,128)S(1)} %get-tuple-element.55), channel_id=1, source_target_pairs={{0,1},{1,0},{2,3},{3,2},{4,5},{5,4},{6,7},{7,6},{8,9},{9,8},{10,11... | collective-permute-start | bytes 110600 | tf_op jit(solution)/shard_map/ppermute | solution.py:494
  62.2 9.7 %collective-permute-start.15 = (f32[3,3,8,128]{3,2,1,0:T(8,128)S(1)}, f32[3,3,8,128]{3,2,1,0:T(8,128)S(1)}, u32[]{:S(2)}, u32[]{:S(2)}) collective-permute-start(f32[3,3,8,128]{3,2,1,0:T(8,128)S(1)} %get-tuple-element.56), channel_id=1, source_target_pairs={{0,3},{1,2},{2,1},{3,0},{4,7},{5,6},{6,5},{7,4},{8,11},{9,10},{10,... | collective-permute-start | bytes 110600 | tf_op jit(solution)/shard_map/ppermute | solution.py:495
  63.9 4.8 %collective-permute-start.12 = (f32[3,2,8,128]{3,2,1,0:T(8,128)S(1)}, f32[3,2,8,128]{3,2,1,0:T(8,128)S(1)}, u32[]{:S(2)}, u32[]{:S(2)}) collective-permute-start(f32[3,2,8,128]{3,2,1,0:T(8,128)S(1)} %get-tuple-element.53), channel_id=1, source_target_pairs={{0,4},{4,0},{8,12},{12,8},{16,20},{20,16},{24,28},{28,24},{1,5},{5... | collective-permute-start | bytes 73736 | tf_op jit(solution)/shard_map/ppermute | solution.py:494
  65.3 6.6 %collective-permute-start.13 = (f32[3,2,8,128]{3,2,1,0:T(8,128)S(1)}, f32[3,2,8,128]{3,2,1,0:T(8,128)S(1)}, u32[]{:S(2)}, u32[]{:S(2)}) collective-permute-start(f32[3,2,8,128]{3,2,1,0:T(8,128)S(1)} %get-tuple-element.54), channel_id=1, source_target_pairs={{0,28},{4,8},{8,4},{12,16},{16,12},{20,24},{24,20},{28,0},{1,29},{... | collective-permute-start | bytes 73736 | tf_op jit(solution)/shard_map/ppermute | solution.py:495

commit v4 on v3

--- a/solution.py
+++ b/solution.py
@@ -15,6 +15,8 @@
 TX, TY, TZ, CPL, RHS, CUR, IDX, FIELDS = 0, 1, 2, 3, 12, 15, 18, 19
 OUTER_X = (TX, CUR, CUR + 1, CUR + 2, IDX)
 OUTER_Y = (TY, CUR, CUR + 1, CUR + 2, IDX)
+NEXT_Y = (TX,) + OUTER_Y
+NEXT_X = OUTER_X
 CORNERS = ((-1, -1), (-1, 1), (1, -1), (1, 1))
 CORNER_TILES = ((1, 1), (1, 2), (2, 1))
 COLD = 2
@@ -138,36 +140,92 @@
         second[FIELDS + place] = two
 
 
-def pack_narrow(flags, block, got_first, got_second, own, first, second):
+def narrow_rows(px):
+    return -(-(FIELDS * (HY - 1) + len(OUTER_Y)) * px // 8) * 8
+
+
+CORNER_ROWS = -(-2 * (FIELDS + len(NEXT_Y) + len(NEXT_X)) // 8) * 8
+
+
+def pack_narrow(flags, block, first, second):
+    px, cy, _ = block.shape[1:]
+    rows = rows_of(block)
+
+    def put(place, number, tail, head):
+        sides = [rows[pl.ds(number * px * cy + column, px, stride=cy), :] for column in (tail, head)]
+        one, two = sent(flags, 1, *sides)
+        first[pl.ds(place * px, px), :] = one
+        second[pl.ds(place * px, px), :] = two
+
+    for number in range(FIELDS):
+        for column in range(HY - 1):
+            put(number * (HY - 1) + column, number, cy - HY + 1 + column, column)
+    for place, number in enumerate(OUTER_Y):
+        put(FIELDS * (HY - 1) + place, number, cy - HY, HY - 1)
+
+
+def corner_fields():
+    rows = [(number, number, 1, 1) for number in range(FIELDS)]
+    rows += [(number, number, 1, 2) for number in NEXT_Y]
+    return rows + [(number, FIELDS + place, 2, 1) for place, number in enumerate(NEXT_X)]
+
+
+def pack_corners(flags, got_first, got_second, first, second):
+    cy = got_first.shape[1]
+    row = 0
+    for side in range(2):
+        for _, place, _, distance in corner_fields():
+            sides = []
+            for column in (cy - distance, distance - 1):
+                pair = [got[place, pl.ds(column, 1), :] for got in (got_first, got_second)]
+                sides.append(received(flags, 0, *pair)[side])
+            one, two = sent(flags, 1, *sides)
+            first[pl.ds(row, 1), :] = one
+            second[pl.ds(row, 1), :] = two
+            row += 1
+
+
+def spread(flags, block, wide_first, wide_second, narrow_first, narrow_second, corner_first, corner_second, field):
     px, cy, tile = block.shape[1:]
-    width = px + 2 * HX
-    own_rows = rows_of(own)
+    columns, width = field.shape[1:3]
+    rows = rows_of(field)
+    empty = jnp.zeros((width, tile), jnp.float32)
 
     def put(number, pair, values):
-        own_rows[pl.ds(number * cy * width + pair, cy, stride=width), :] = values
+        rows[pl.ds((number * columns + HY) * width + pair, cy, stride=width), :] = values
 
     for number in range(FIELDS):
-        low, high = received(flags, 0, got_first[number], got_second[number])
+        for column in range(HY):
+            field[number, column] = empty
+            field[number, HY + cy + column] = empty
+        for pair in range(px):
+            put(number, HX + pair, block[number, pair])
+        low, high = received(flags, 0, wide_first[number], wide_second[number])
         put(number, HX - 1, low)
         put(number, HX + px, high)
         if number in OUTER_X:
             place = FIELDS + OUTER_X.index(number)
-            low, high = received(flags, 0, got_first[place], got_second[place])
+            low, high = received(flags, 0, wide_first[place], wide_second[place])
         else:
             low = high = jnp.zeros((cy, tile), jnp.float32)
         put(number, 0, low)
         put(number, width - 1, high)
-        for pair in range(px):
-            put(number, HX + pair, block[number, pair])
-    for number in range(FIELDS):
-        for column in range(HY - 1):
-            one, two = sent(flags, 1, own[number, cy - HY + 1 + column], own[number, column])
-            first[number * (HY - 1) + column] = one
-            second[number * (HY - 1) + column] = two
-    for place, number in enumerate(OUTER_Y):
-        one, two = sent(flags, 1, own[number, cy - HY], own[number, HY - 1])
-        first[FIELDS * (HY - 1) + place] = one
-        second[FIELDS * (HY - 1) + place] = two
+    places = [(number, 1 + column, HY + cy + column) for number in range(FIELDS) for column in range(HY - 1)]
+    places += [(number, 0, columns - 1) for number in OUTER_Y]
+    for place, (number, before, after) in enumerate(places):
+        some = pl.ds(place * px, px)
+        low, high = received(flags, 1, narrow_first[some, :], narrow_second[some, :])
+        field[number, before, pl.ds(HX, px), :] = low
+        field[number, after, pl.ds(HX, px), :] = high
+    row = 0
+    for side in range(2):
+        for number, _, pairs, distance in corner_fields():
+            pair = HX - pairs if side == 0 else HX + px + pairs - 1
+            some = pl.ds(row, 1)
+            low, high = received(flags, 1, corner_first[some, :], corner_second[some, :])
+            field[number, HY - distance, pl.ds(pair, 1), :] = low
+            field[number, HY + cy + distance - 1, pl.ds(pair, 1), :] = high
+            row += 1
 
 
 def lane_half(shape):
@@ -296,32 +354,19 @@
         corner.wait()
 
 
-def prepare(flags, own, got_first, got_second, cinv, hot, cold, coeffs, index, current, slots, first, second, third, fourth, field, *scratch, px, narrow):
+def prepare(flags, block, wide_first, wide_second, narrow_first, narrow_second, corner_first, corner_second, cinv, hot, cold, coeffs, index, current, slots, first, second, third, fourth, field, *scratch, px, narrow):
     def before():
-        assemble(flags, own, got_first, got_second, coeffs, index, current, field)
+        got = (wide_first, wide_second, narrow_first, narrow_second, corner_first, corner_second)
+        spread(flags, block, *got, field)
+        assemble(coeffs, index, current, field)
 
     sweep_body(flags, coeffs, current, index, cinv, hot, cold, slots, first, second, third, fourth, px, narrow, scratch, before)
 
 
-def assemble(flags, own, got_first, got_second, coeffs, index, current, field):
-    cy = own.shape[1]
-    columns = cy + 2 * HY
-    half = lane_half(own.shape[2:])
-    depth = lax.broadcasted_iota(jnp.int32, own.shape[2:], 1) % (own.shape[3] // 2)
-    for number in range(FIELDS):
-        for column in range(cy):
-            field[number, HY + column] = own[number, column]
-        for column in range(HY - 1):
-            low, high = received(
-                flags, 1, got_first[number * (HY - 1) + column], got_second[number * (HY - 1) + column]
-            )
-            field[number, 1 + column] = low
-            field[number, HY + cy + column] = high
-    for place, number in enumerate(OUTER_Y):
-        place = FIELDS * (HY - 1) + place
-        low, high = received(flags, 1, got_first[place], got_second[place])
-        field[number, 0] = low
-        field[number, columns - 1] = high
+def assemble(coeffs, index, current, field):
+    columns, width, tile = field.shape[1:]
+    half = lane_half((width, tile))
+    depth = lax.broadcasted_iota(jnp.int32, (width, tile), 1) % (tile // 2)
     for column in range(columns):
         index[column] = field[IDX, column].astype(jnp.int32)
         for c in range(3):
@@ -329,7 +374,7 @@
     coeffs[1, 0] = field[TY, 0]
     for column in range(1, columns - 1):
         tx, ty = field[TX, column], field[TY, column]
-        tz = jnp.where(depth < own.shape[3] // 2 - 1, field[TZ, column], 0.0)
+        tz = jnp.where(depth < tile // 2 - 1, field[TZ, column], 0.0)
         faces = (tx + west_of(tx, half)) + (ty + field[TY, column - 1]) + (tz + below(tz))
         coeffs[0, column] = tx
         coeffs[1, column] = ty
@@ -550,13 +595,12 @@
         ],
         far=range(8),
     )(flags, trans, accum, coupling, rhs, start, agg_map, well_cells, well_index)
-    first, second = swap(first, second, "wide")
-    face = ((FIELDS * (HY - 1) + len(OUTER_Y), width, tile), f32)
-    own, first, second = call(pack_narrow, [((FIELDS, cy, width, tile), f32), face, face])(
-        flags, block, first, second
-    )
-    first, second = swap(first, second, "narrow")
-    cold_tiles, hot_tiles = tiles_after(own, [cold, hot])
+    got = swap(first, second, "wide")
+    face = ((narrow_rows(px), tile), f32)
+    got += swap(*call(pack_narrow, [face, face])(flags, block), "narrow")
+    cold_tiles, hot_tiles = tiles_after(block, [cold, hot])
+    face = ((CORNER_ROWS, tile), f32)
+    got += swap(*call(pack_corners, [face, face])(flags, *got[:2]), "narrow")
 
     vec = (width, tile)
     field = ((phases, columns) + vec, f32)
@@ -583,7 +627,7 @@
         [((GFIELDS, columns - 1) + vec, f32), ((columns,) + vec, jnp.int32), field, slot] + faces,
         [pltpu.VMEM((FIELDS, columns) + vec, f32)] + scratch,
         far_outs=(3,),
-    )(flags, own, first, second, coarse_inverse, hot_tiles, cold_tiles)
+    )(flags, block, *got, coarse_inverse, hot_tiles, cold_tiles)
     for sweep in range(SWEEPS):
         gathered = lax.all_to_all(slots, ("wide", "narrow"), 0, 0, tiled=True)
         got = swap(*sends[:2], "wide") + swap(*sends[2:], "narrow")

time: 73.8 us -> 71.1 us (0.963)
  waiting for transfers between devices: 13.9 us -> 9.25 us
  starting transfers between devices: 39.3 us -> 40.4 us
  Pallas kernels: 19.2 us -> 20 us
    ppermute x8 -> x9, waiting for transfers between devices: 8.8 us -> 4.78 us  [swap(): second = lax.ppermute(second, axis, pairs[1])]
    ppermute x8 -> x9, starting transfers between devices: 20 us -> 21.6 us  [swap(): second = lax.ppermute(second, axis, pairs[1])]
    pallas_call x9 -> x10, Pallas kernels: 19.2 us -> 20 us  [run(): pl.pallas_call(body, out_shape=tuple(((pltpu.HBM if number in far_outs el...]
    ppermute x8 -> x9, starting transfers between devices: 8.47 us -> 8.55 us  [swap(): first = lax.ppermute(first, axis, pairs[0])]
  transfers between devices with their start and end apart: 19 -> 21, of which waited for: 6 -> 4; matrix products, arithmetic and copies ran while one was open for 0% -> 0% of each run, Pallas kernels for 8% -> 10%
where the time goes in v4:
time: 71.1 us; the launch traced here: 70.7 us
  starting transfers between devices  40.4 us (57%)
  Pallas kernels  20 us (28%)
  waiting for transfers between devices  9.25 us (13%)
  between operations  0.94 us (1%)
    ppermute x9, starting transfers between devices, swap(): second = lax.ppermute(second, axis, pairs[1])  21.6 us
    pallas_call x10, Pallas kernels, run(): pl.pallas_call(body, out_shape=tuple(((pltpu.HBM if number in far_outs el...  20 us
    all_to_all x3, starting transfers between devices, per_device(): gathered = lax.all_to_all(slots, ('wide', 'narrow'), 0, 0, tiled=True)  10.3 us
    ppermute x9, starting transfers between devices, swap(): first = lax.ppermute(first, axis, pairs[0])  8.55 us
    ppermute x9, waiting for transfers between devices, swap(): second = lax.ppermute(second, axis, pairs[1])  4.78 us
    all_to_all x3, waiting for transfers between devices, per_device(): gathered = lax.all_to_all(slots, ('wide', 'narrow'), 0, 0, tiled=True)  4.45 us
  transfers between devices with their start and end apart: 21, of which 4 were waited for; matrix products, arithmetic and copies ran while one was open for 0% of the time, Pallas kernels for 10%

profile of v4, /device:TPU:0, one launch (start us, length us, event | category | flops | bytes accessed | tf_op | source)
XLA Modules:
  0.0 70.7 jit_solution(11896830178288681836)
XLA Ops:
  0.7 0.1 stack.33.flags
  0.8 1.6 %shard_map.113 = (f32[19,4,8,128]{3,2,1,0:T(8,128)S(1)}, f32[24,8,128]{2,1,0:T(8,128)S(1)}, f32[24,8,128]{2,1,0:T(8,128)S(1)}) custom-call(s32[9]{0:T(128)S(1)} %stack.33.flags, f32[3,4,8,128]{3,2,1,0:T(8,128)} %trans.1, f32[4,8,128]{2,1,0:T(8,128)} %accum.1, f32[3,3,4,8,128]{4,3,2,1,0:T(8,128)} %coupling.1, f32[3,4,8,128]{3,2,1,0:T(8,128)} %rhs.1, ...), custom_call_target="tpu_custom_call" | custom-call | tf_op jit(solution)/shard_map/pallas_call | solution.py:41
  2.4 3.1 %collective-permute-start = (f32[24,8,128]{2,1,0:T(8,128)S(1)}, f32[24,8,128]{2,1,0:T(8,128)S(1)}, u32[]{:S(2)}, u32[]{:S(2)}) collective-permute-start(f32[24,8,128]{2,1,0:T(8,128)S(1)} %get-tuple-element.32), channel_id=1, source_target_pairs={{0,4},{4,0},{8,12},{12,8},{16,20},{20,16},{24,28},{28,24},{1,5},{5... | collective-permute-start | bytes 294920 | tf_op jit(solution)/shard_map/ppermute | solution.py:539
  5.5 3.5 %collective-permute-start.1 = (f32[24,8,128]{2,1,0:T(8,128)S(1)}, f32[24,8,128]{2,1,0:T(8,128)S(1)}, u32[]{:S(2)}, u32[]{:S(2)}) collective-permute-start(f32[24,8,128]{2,1,0:T(8,128)S(1)} %get-tuple-element.33), channel_id=1, source_target_pairs={{0,28},{4,8},{8,4},{12,16},{16,12},{20,24},{24,20},{28,0},{1,29},{... | collective-permute-start | bytes 294920 | tf_op jit(solution)/shard_map/ppermute | solution.py:540
  9.0 0.6 shard_map.114
  9.6 0.1 collective-permute-start.2
  9.7 1.6 %collective-permute-start.3 = (f32[176,128]{1,0:T(8,128)S(1)}, f32[176,128]{1,0:T(8,128)S(1)}, u32[]{:S(2)}, u32[]{:S(2)}) collective-permute-start(f32[176,128]{1,0:T(8,128)S(1)} %get-tuple-element.35), channel_id=1, source_target_pairs={{0,3},{1,2},{2,1},{3,0},{4,7},{5,6},{6,5},{7,4},{8,11},{9,10},{10,... | collective-permute-start | bytes 270344 | tf_op jit(solution)/shard_map/ppermute | solution.py:540
  11.3 0.0 collective-permute-done.got_first.wide_first
  11.3 1.5 %collective-permute-done.1.got_second.wide_second = f32[24,8,128]{2,1,0:T(8,128)S(1)} collective-permute-done((f32[24,8,128]{2,1,0:T(8,128)S(1)}, f32[24,8,128]{2,1,0:T(8,128)S(1)}, u32[]{:S(2)}, u32[]{:S(2)}) %collective-permute-start.1) | collective-permute-done | bytes 98336 | tf_op jit(solution)/shard_map/ppermute | solution.py:540
  12.8 0.6 shard_map.115
  13.4 0.1 collective-permute-start.4
  13.5 1.6 %collective-permute-start.5 = (f32[64,128]{1,0:T(8,128)S(1)}, f32[64,128]{1,0:T(8,128)S(1)}, u32[]{:S(2)}, u32[]{:S(2)}) collective-permute-start(f32[64,128]{1,0:T(8,128)S(1)} %get-tuple-element.37), channel_id=1, source_target_pairs={{0,3},{1,2},{2,1},{3,0},{4,7},{5,6},{6,5},{7,4},{8,11},{9,10},{10,... | collective-permute-start | bytes 98312 | tf_op jit(solution)/shard_map/ppermute | solution.py:540
  15.1 2.2 %shard_map.116 = (bf16[6,4,128,128]{3,2,1,0:T(8,128)(2,1)S(1)}, bf16[6,8,128,128]{3,2,1,0:T(8,128)(2,1)S(1)}) custom-call(s32[9]{0:T(128)S(1)} %stack.33.flags, bf16[6,12,128,128]{3,2,1,0:T(8,128)(2,1)} %factors.5, f32[19,4,8,128]{3,2,1,0:T(8,128)S(1)} %get-tuple-element.31.block.after), custom_call_target="tpu_custom_call" | custom-call | tf_op jit(solution)/shard_map/pallas_call | solution.py:41
  17.3 0.0 collective-permute-done.2.narrow_first
  17.3 0.0 collective-permute-done.3.narrow_second
  17.4 0.0 collective-permute-done.4.corner_first
  17.4 0.0 collective-permute-done.5.corner_second
  17.4 3.4 %shard_map.117 = (f32[18,13,8,128]{3,2,1,0:T(8,128)S(1)}, s32[14,8,128]{2,1,0:T(8,128)S(1)}, f32[3,14,8,128]{3,2,1,0:T(8,128)S(1)}, f32[32,3,4,128]{3,2,1,0:T(4,...) custom-call(s32[9]{0:T(128)S(1)} %stack.33.flags, ...), custom_call_target="tpu_custom_call" | custom-call | tf_op jit(solution)/shard_map/pallas_call | solution.py:41
  20.8 4.4 %all-to-all-start = ((f32[32,3,4,128]{3,2,1,0:T(4,128)}), f32[32,3,4,128]{3,2,1,0:T(4,128)S(1)}, u32[]{:S(2)}, u32[]{:S(2)}) async-start(f32[32,3,4,128]{3,2,1,0:T(4,128)} %get-tuple-element.47), calls=%async_computation | async-start | bytes 393216 | tf_op jit(solution)/shard_map/all_to_all | solution.py:632
  25.2 0.3 collective-permute-start.8
  25.5 1.6 %collective-permute-start.9 = (f32[3,3,8,128]{3,2,1,0:T(8,128)S(1)}, f32[3,3,8,128]{3,2,1,0:T(8,128)S(1)}, u32[]{:S(2)}, u32[]{:S(2)}) collective-permute-start(f32[3,3,8,128]{3,2,1,0:T(8,128)S(1)} %get-tuple-element.46), channel_id=1, source_target_pairs={{0,3},{1,2},{2,1},{3,0},{4,7},{5,6},{6,5},{7,4},{8,11},{9,10},{10,... | collective-permute-start | bytes 110600 | tf_op jit(solution)/shard_map/ppermute | solution.py:540
  27.1 1.5 %collective-permute-start.6 = (f32[3,2,8,128]{3,2,1,0:T(8,128)S(1)}, f32[3,2,8,128]{3,2,1,0:T(8,128)S(1)}, u32[]{:S(2)}, u32[]{:S(2)}) collective-permute-start(f32[3,2,8,128]{3,2,1,0:T(8,128)S(1)} %get-tuple-element.43), channel_id=1, source_target_pairs={{0,4},{4,0},{8,12},{12,8},{16,20},{20,16},{24,28},{28,24},{1,5},{5... | collective-permute-start | bytes 73736 | tf_op jit(solution)/shard_map/ppermute | solution.py:539
  28.6 3.3 %collective-permute-start.7 = (f32[3,2,8,128]{3,2,1,0:T(8,128)S(1)}, f32[3,2,8,128]{3,2,1,0:T(8,128)S(1)}, u32[]{:S(2)}, u32[]{:S(2)}) collective-permute-start(f32[3,2,8,128]{3,2,1,0:T(8,128)S(1)} %get-tuple-element.44), channel_id=1, source_target_pairs={{0,28},{4,8},{8,4},{12,16},{16,12},{20,24},{24,20},{28,0},{1,29},{... | collective-permute-start | bytes 73736 | tf_op jit(solution)/shard_map/ppermute | solution.py:540
  31.9 2.2 %all-to-all-done.after.slots_in = f32[32,3,4,128]{3,2,1,0:T(4,128)S(1)} async-done(((f32[32,3,4,128]{3,2,1,0:T(4,128)}), f32[32,3,4,128]{3,2,1,0:T(4,128)S(1)}, u32[]{:S(2)}, u32[]{:S(2)}) %all-to-all-start) | async-done | bytes 196640 | tf_op jit(solution)/shard_map/all_to_all | solution.py:632
  34.2 1.7 %shard_map.118.cold = bf16[6,4,128,128]{3,2,1,0:T(8,128)(2,1)S(1)} custom-call(s32[9]{0:T(128)S(1)} %stack.33.flags, bf16[6,12,128,128]{3,2,1,0:T(8,128)(2,1)} %factors.5, f32[32,3,4,128]{3,2,1,0:T(4,128)S(1)} %all-to-all-done.after.slots_in), custom_call_target="tpu_custom_call" | custom-call | tf_op jit(solution)/shard_map/pallas_call | solution.py:41
  35.8 0.0 collective-permute-done.6.got_0
  35.9 0.0 collective-permute-done.7.got_1
  35.9 0.0 collective-permute-done.8.got_2
  35.9 0.0 collective-permute-done.9.got_3
  35.9 3.4 %shard_map.119 = (f32[3,14,8,128]{3,2,1,0:T(8,128)S(1)}, f32[32,3,4,128]{3,2,1,0:T(4,128)}, f32[3,2,8,128]{3,2,1,0:T(8,128)S(1)}, f32[3,2,8,128]{3,2,1,0:T(8,128...) custom-call(s32[9]{0:T(128)S(1)} %stack.33.flags, f32[3,14,8,128]{3,2,1,0:T(8,128)S(1)} %get-tuple-element.40.current, ...), custom_call_target="tpu_custom_call" | custom-call | tf_op jit(solution)/shard_map/pallas_call | solution.py:41
  39.3 2.9 %all-to-all-start.1 = ((f32[32,3,4,128]{3,2,1,0:T(4,128)}), f32[32,3,4,128]{3,2,1,0:T(4,128)S(1)}, u32[]{:S(2)}, u32[]{:S(2)}) async-start(f32[32,3,4,128]{3,2,1,0:T(4,128)} %get-tuple-element.53), calls=%async_computation.1 | async-start | bytes 393216 | tf_op jit(solution)/shard_map/all_to_all | solution.py:632
  42.2 0.3 collective-permute-start.12
  42.5 1.6 %collective-permute-start.13 = (f32[3,3,8,128]{3,2,1,0:T(8,128)S(1)}, f32[3,3,8,128]{3,2,1,0:T(8,128)S(1)}, u32[]{:S(2)}, u32[]{:S(2)}) collective-permute-start(f32[3,3,8,128]{3,2,1,0:T(8,128)S(1)} %get-tuple-element.52), channel_id=1, source_target_pairs={{0,3},{1,2},{2,1},{3,0},{4,7},{5,6},{6,5},{7,4},{8,11},{9,10},{10,... | collective-permute-start | bytes 110600 | tf_op jit(solution)/shard_map/ppermute | solution.py:540
  44.2 1.5 %collective-permute-start.10 = (f32[3,2,8,128]{3,2,1,0:T(8,128)S(1)}, f32[3,2,8,128]{3,2,1,0:T(8,128)S(1)}, u32[]{:S(2)}, u32[]{:S(2)}) collective-permute-start(f32[3,2,8,128]{3,2,1,0:T(8,128)S(1)} %get-tuple-element.49), channel_id=1, source_target_pairs={{0,4},{4,0},{8,12},{12,8},{16,20},{20,16},{24,28},{28,24},{1,5},{5... | collective-permute-start | bytes 73736 | tf_op jit(solution)/shard_map/ppermute | solution.py:539
  45.6 3.3 %collective-permute-start.11 = (f32[3,2,8,128]{3,2,1,0:T(8,128)S(1)}, f32[3,2,8,128]{3,2,1,0:T(8,128)S(1)}, u32[]{:S(2)}, u32[]{:S(2)}) collective-permute-start(f32[3,2,8,128]{3,2,1,0:T(8,128)S(1)} %get-tuple-element.50), channel_id=1, source_target_pairs={{0,28},{4,8},{8,4},{12,16},{16,12},{20,24},{24,20},{28,0},{1,29},{... | collective-permute-start | bytes 73736 | tf_op jit(solution)/shard_map/ppermute | solution.py:540
  49.0 2.2 %all-to-all-done.1.after.slots_in = f32[32,3,4,128]{3,2,1,0:T(4,128)S(1)} async-done(((f32[32,3,4,128]{3,2,1,0:T(4,128)}), f32[32,3,4,128]{3,2,1,0:T(4,128)S(1)}, u32[]{:S(2)}, u32[]{:S(2)}) %all-to-all-start.1) | async-done | bytes 196640 | tf_op jit(solution)/shard_map/all_to_all | solution.py:632
  51.2 1.7 %shard_map.120.cold = bf16[6,4,128,128]{3,2,1,0:T(8,128)(2,1)S(1)} custom-call(s32[9]{0:T(128)S(1)} %stack.33.flags, bf16[6,12,128,128]{3,2,1,0:T(8,128)(2,1)} %factors.5, f32[32,3,4,128]{3,2,1,0:T(4,128)S(1)} %all-to-all-done.1.after.slots_in), custom_call_target="tpu_custom_call" | custom-call | tf_op jit(solution)/shard_map/pallas_call | solution.py:41
  52.9 0.0 collective-permute-done.10.got_0
  52.9 0.0 collective-permute-done.11.got_1
  52.9 3.4 %shard_map.121 = (f32[3,14,8,128]{3,2,1,0:T(8,128)S(1)}, f32[32,3,4,128]{3,2,1,0:T(4,128)}, f32[3,2,8,128]{3,2,1,0:T(8,128)S(1)}, f32[3,2,8,128]{3,2,1,0:T(8,128...) custom-call(s32[9]{0:T(128)S(1)} %stack.33.flags, f32[3,14,8,128]{3,2,1,0:T(8,128)S(1)} %get-tuple-element.48.current, ...), custom_call_target="tpu_custom_call" | custom-call | tf_op jit(solution)/shard_map/pallas_call | solution.py:41
  56.3 2.9 %all-to-all-start.2 = ((f32[32,3,4,128]{3,2,1,0:T(4,128)}), f32[32,3,4,128]{3,2,1,0:T(4,128)S(1)}, u32[]{:S(2)}, u32[]{:S(2)}) async-start(f32[32,3,4,128]{3,2,1,0:T(4,128)} %get-tuple-element.59), calls=%async_computation.2 | async-start | bytes 393216 | tf_op jit(solution)/shard_map/all_to_all | solution.py:632
  59.2 0.3 collective-permute-start.16
  59.5 1.6 %collective-permute-start.17 = (f32[3,3,8,128]{3,2,1,0:T(8,128)S(1)}, f32[3,3,8,128]{3,2,1,0:T(8,128)S(1)}, u32[]{:S(2)}, u32[]{:S(2)}) collective-permute-start(f32[3,3,8,128]{3,2,1,0:T(8,128)S(1)} %get-tuple-element.58), channel_id=1, source_target_pairs={{0,3},{1,2},{2,1},{3,0},{4,7},{5,6},{6,5},{7,4},{8,11},{9,10},{10,... | collective-permute-start | bytes 110600 | tf_op jit(solution)/shard_map/ppermute | solution.py:540
  61.2 1.5 %collective-permute-start.14 = (f32[3,2,8,128]{3,2,1,0:T(8,128)S(1)}, f32[3,2,8,128]{3,2,1,0:T(8,128)S(1)}, u32[]{:S(2)}, u32[]{:S(2)}) collective-permute-start(f32[3,2,8,128]{3,2,1,0:T(8,128)S(1)} %get-tuple-element.55), channel_id=1, source_target_pairs={{0,4},{4,0},{8,12},{12,8},{16,20},{20,16},{24,28},{28,24},{1,5},{5... | collective-permute-start | bytes 73736 | tf_op jit(solution)/shard_map/ppermute | solution.py:539
  62.6 3.3 %collective-permute-start.15 = (f32[3,2,8,128]{3,2,1,0:T(8,128)S(1)}, f32[3,2,8,128]{3,2,1,0:T(8,128)S(1)}, u32[]{:S(2)}, u32[]{:S(2)}) collective-permute-start(f32[3,2,8,128]{3,2,1,0:T(8,128)S(1)} %get-tuple-element.56), channel_id=1, source_target_pairs={{0,28},{4,8},{8,4},{12,16},{16,12},{20,24},{24,20},{28,0},{1,29},{... | collective-permute-start | bytes 73736 | tf_op jit(solution)/shard_map/ppermute | solution.py:540
  66.0 3.3 %collective-permute-done.15.got_1 = f32[3,2,8,128]{3,2,1,0:T(8,128)S(1)} collective-permute-done((f32[3,2,8,128]{3,2,1,0:T(8,128)S(1)}, f32[3,2,8,128]{3,2,1,0:T(8,128)S(1)}, u32[]{:S(2)}, u32[]{:S(2)}) %collective-permute-start.15) | collective-permute-done | bytes 24608 | tf_op jit(solution)/shard_map/ppermute | solution.py:540
  69.2 0.0 collective-permute-done.16.got_2
  69.2 1.4 %shard_map.122 = (f32[3,4,8,128]{3,2,1,0:T(8,128)}, f32[3,4,8,128]{3,2,1,0:T(8,128)}) custom-call(s32[9]{0:T(128)S(1)} %stack.33.flags, f32[3,14,8,128]{3,2,1,0:T(8,128)S(1)} %get-tuple-element.54.current, f32[18,13,8,128]{3,2,1,0:T(8,128)S(1)} %get-tuple-element.41.coeffs, s32[14,8,128]{2,1,0:T(8,128)S(1)} %get-tuple-element.42.index, ...), custom_call_target="tpu_custom_call" | custom-call | tf_op jit(solution)/shard_map/pallas_call | solution.py:41
  (7 shorter events, 0.0 us)
Async XLA Ops:
  0.6 16.7 %copy-start = (f32[32,1024]{1,0:T(8,128)S(1)}, f32[32,1024]{1,0:T(8,128)}, u32[]{:S(2)}) copy-start(f32[32,1024]{1,0:T(8,128)} %cinv.5) | copy-start | bytes 393220
  2.4 8.9 %collective-permute-start = (f32[24,8,128]{2,1,0:T(8,128)S(1)}, f32[24,8,128]{2,1,0:T(8,128)S(1)}, u32[]{:S(2)}, u32[]{:S(2)}) collective-permute-start(f32[24,8,128]{2,1,0:T(8,128)S(1)} %get-tuple-element.32), channel_id=1, source_target_pairs={{0,4},{4,0},{8,12},{12,8},{16,20},{20,16},{24,28},{28,24},{1,5},{5... | collective-permute-start | bytes 294920 | tf_op jit(solution)/shard_map/ppermute | solution.py:539
  5.5 7.3 %collective-permute-start.1 = (f32[24,8,128]{2,1,0:T(8,128)S(1)}, f32[24,8,128]{2,1,0:T(8,128)S(1)}, u32[]{:S(2)}, u32[]{:S(2)}) collective-permute-start(f32[24,8,128]{2,1,0:T(8,128)S(1)} %get-tuple-element.33), channel_id=1, source_target_pairs={{0,28},{4,8},{8,4},{12,16},{16,12},{20,24},{24,20},{28,0},{1,29},{... | collective-permute-start | bytes 294920 | tf_op jit(solution)/shard_map/ppermute | solution.py:540
  9.6 7.7 %collective-permute-start.2 = (f32[176,128]{1,0:T(8,128)S(1)}, f32[176,128]{1,0:T(8,128)S(1)}, u32[]{:S(2)}, u32[]{:S(2)}) collective-permute-start(f32[176,128]{1,0:T(8,128)S(1)} %get-tuple-element.34), channel_id=1, source_target_pairs={{0,1},{1,0},{2,3},{3,2},{4,5},{5,4},{6,7},{7,6},{8,9},{9,8},{10,11... | collective-permute-start | bytes 270344 | tf_op jit(solution)/shard_map/ppermute | solution.py:539
  9.7 7.6 %collective-permute-start.3 = (f32[176,128]{1,0:T(8,128)S(1)}, f32[176,128]{1,0:T(8,128)S(1)}, u32[]{:S(2)}, u32[]{:S(2)}) collective-permute-start(f32[176,128]{1,0:T(8,128)S(1)} %get-tuple-element.35), channel_id=1, source_target_pairs={{0,3},{1,2},{2,1},{3,0},{4,7},{5,6},{6,5},{7,4},{8,11},{9,10},{10,... | collective-permute-start | bytes 270344 | tf_op jit(solution)/shard_map/ppermute | solution.py:540
  13.4 3.9 %collective-permute-start.4 = (f32[64,128]{1,0:T(8,128)S(1)}, f32[64,128]{1,0:T(8,128)S(1)}, u32[]{:S(2)}, u32[]{:S(2)}) collective-permute-start(f32[64,128]{1,0:T(8,128)S(1)} %get-tuple-element.36), channel_id=1, source_target_pairs={{0,1},{1,0},{2,3},{3,2},{4,5},{5,4},{6,7},{7,6},{8,9},{9,8},{10,11... | collective-permute-start | bytes 98312 | tf_op jit(solution)/shard_map/ppermute | solution.py:539
  13.5 3.9 %collective-permute-start.5 = (f32[64,128]{1,0:T(8,128)S(1)}, f32[64,128]{1,0:T(8,128)S(1)}, u32[]{:S(2)}, u32[]{:S(2)}) collective-permute-start(f32[64,128]{1,0:T(8,128)S(1)} %get-tuple-element.37), channel_id=1, source_target_pairs={{0,3},{1,2},{2,1},{3,0},{4,7},{5,6},{6,5},{7,4},{8,11},{9,10},{10,... | collective-permute-start | bytes 98312 | tf_op jit(solution)/shard_map/ppermute | solution.py:540
  20.8 13.4 %all-to-all-start = ((f32[32,3,4,128]{3,2,1,0:T(4,128)}), f32[32,3,4,128]{3,2,1,0:T(4,128)S(1)}, u32[]{:S(2)}, u32[]{:S(2)}) async-start(f32[32,3,4,128]{3,2,1,0:T(4,128)} %get-tuple-element.47), calls=%async_computation | async-start | bytes 393216 | tf_op jit(solution)/shard_map/all_to_all | solution.py:632
  25.2 10.7 %collective-permute-start.8 = (f32[3,3,8,128]{3,2,1,0:T(8,128)S(1)}, f32[3,3,8,128]{3,2,1,0:T(8,128)S(1)}, u32[]{:S(2)}, u32[]{:S(2)}) collective-permute-start(f32[3,3,8,128]{3,2,1,0:T(8,128)S(1)} %get-tuple-element.45), channel_id=1, source_target_pairs={{0,1},{1,0},{2,3},{3,2},{4,5},{5,4},{6,7},{7,6},{8,9},{9,8},{10,11... | collective-permute-start | bytes 110600 | tf_op jit(solution)/shard_map/ppermute | solution.py:539
  25.5 10.4 %collective-permute-start.9 = (f32[3,3,8,128]{3,2,1,0:T(8,128)S(1)}, f32[3,3,8,128]{3,2,1,0:T(8,128)S(1)}, u32[]{:S(2)}, u32[]{:S(2)}) collective-permute-start(f32[3,3,8,128]{3,2,1,0:T(8,128)S(1)} %get-tuple-element.46), channel_id=1, source_target_pairs={{0,3},{1,2},{2,1},{3,0},{4,7},{5,6},{6,5},{7,4},{8,11},{9,10},{10,... | collective-permute-start | bytes 110600 | tf_op jit(solution)/shard_map/ppermute | solution.py:540
  27.1 8.7 %collective-permute-start.6 = (f32[3,2,8,128]{3,2,1,0:T(8,128)S(1)}, f32[3,2,8,128]{3,2,1,0:T(8,128)S(1)}, u32[]{:S(2)}, u32[]{:S(2)}) collective-permute-start(f32[3,2,8,128]{3,2,1,0:T(8,128)S(1)} %get-tuple-element.43), channel_id=1, source_target_pairs={{0,4},{4,0},{8,12},{12,8},{16,20},{20,16},{24,28},{28,24},{1,5},{5... | collective-permute-start | bytes 73736 | tf_op jit(solution)/shard_map/ppermute | solution.py:539
  28.6 7.3 %collective-permute-start.7 = (f32[3,2,8,128]{3,2,1,0:T(8,128)S(1)}, f32[3,2,8,128]{3,2,1,0:T(8,128)S(1)}, u32[]{:S(2)}, u32[]{:S(2)}) collective-permute-start(f32[3,2,8,128]{3,2,1,0:T(8,128)S(1)} %get-tuple-element.44), channel_id=1, source_target_pairs={{0,28},{4,8},{8,4},{12,16},{16,12},{20,24},{24,20},{28,0},{1,29},{... | collective-permute-start | bytes 73736 | tf_op jit(solution)/shard_map/ppermute | solution.py:540
  39.3 11.9 %all-to-all-start.1 = ((f32[32,3,4,128]{3,2,1,0:T(4,128)}), f32[32,3,4,128]{3,2,1,0:T(4,128)S(1)}, u32[]{:S(2)}, u32[]{:S(2)}) async-start(f32[32,3,4,128]{3,2,1,0:T(4,128)} %get-tuple-element.53), calls=%async_computation.1 | async-start | bytes 393216 | tf_op jit(solution)/shard_map/all_to_all | solution.py:632
  42.2 10.7 %collective-permute-start.12 = (f32[3,3,8,128]{3,2,1,0:T(8,128)S(1)}, f32[3,3,8,128]{3,2,1,0:T(8,128)S(1)}, u32[]{:S(2)}, u32[]{:S(2)}) collective-permute-start(f32[3,3,8,128]{3,2,1,0:T(8,128)S(1)} %get-tuple-element.51), channel_id=1, source_target_pairs={{0,1},{1,0},{2,3},{3,2},{4,5},{5,4},{6,7},{7,6},{8,9},{9,8},{10,11... | collective-permute-start | bytes 110600 | tf_op jit(solution)/shard_map/ppermute | solution.py:539
  42.5 10.4 %collective-permute-start.13 = (f32[3,3,8,128]{3,2,1,0:T(8,128)S(1)}, f32[3,3,8,128]{3,2,1,0:T(8,128)S(1)}, u32[]{:S(2)}, u32[]{:S(2)}) collective-permute-start(f32[3,3,8,128]{3,2,1,0:T(8,128)S(1)} %get-tuple-element.52), channel_id=1, source_target_pairs={{0,3},{1,2},{2,1},{3,0},{4,7},{5,6},{6,5},{7,4},{8,11},{9,10},{10,... | collective-permute-start | bytes 110600 | tf_op jit(solution)/shard_map/ppermute | solution.py:540
  44.2 8.7 %collective-permute-start.10 = (f32[3,2,8,128]{3,2,1,0:T(8,128)S(1)}, f32[3,2,8,128]{3,2,1,0:T(8,128)S(1)}, u32[]{:S(2)}, u32[]{:S(2)}) collective-permute-start(f32[3,2,8,128]{3,2,1,0:T(8,128)S(1)} %get-tuple-element.49), channel_id=1, source_target_pairs={{0,4},{4,0},{8,12},{12,8},{16,20},{20,16},{24,28},{28,24},{1,5},{5... | collective-permute-start | bytes 73736 | tf_op jit(solution)/shard_map/ppermute | solution.py:539
  45.6 7.3 %collective-permute-start.11 = (f32[3,2,8,128]{3,2,1,0:T(8,128)S(1)}, f32[3,2,8,128]{3,2,1,0:T(8,128)S(1)}, u32[]{:S(2)}, u32[]{:S(2)}) collective-permute-start(f32[3,2,8,128]{3,2,1,0:T(8,128)S(1)} %get-tuple-element.50), channel_id=1, source_target_pairs={{0,28},{4,8},{8,4},{12,16},{16,12},{20,24},{24,20},{28,0},{1,29},{... | collective-permute-start | bytes 73736 | tf_op jit(solution)/shard_map/ppermute | solution.py:540
  56.3 13.0 %all-to-all-start.2 = ((f32[32,3,4,128]{3,2,1,0:T(4,128)}), f32[32,3,4,128]{3,2,1,0:T(4,128)S(1)}, u32[]{:S(2)}, u32[]{:S(2)}) async-start(f32[32,3,4,128]{3,2,1,0:T(4,128)} %get-tuple-element.59), calls=%async_computation.2 | async-start | bytes 393216 | tf_op jit(solution)/shard_map/all_to_all | solution.py:632
  59.2 10.0 %collective-permute-start.16 = (f32[3,3,8,128]{3,2,1,0:T(8,128)S(1)}, f32[3,3,8,128]{3,2,1,0:T(8,128)S(1)}, u32[]{:S(2)}, u32[]{:S(2)}) collective-permute-start(f32[3,3,8,128]{3,2,1,0:T(8,128)S(1)} %get-tuple-element.57), channel_id=1, source_target_pairs={{0,1},{1,0},{2,3},{3,2},{4,5},{5,4},{6,7},{7,6},{8,9},{9,8},{10,11... | collective-permute-start | bytes 110600 | tf_op jit(solution)/shard_map/ppermute | solution.py:539
  59.5 9.7 %collective-permute-start.17 = (f32[3,3,8,128]{3,2,1,0:T(8,128)S(1)}, f32[3,3,8,128]{3,2,1,0:T(8,128)S(1)}, u32[]{:S(2)}, u32[]{:S(2)}) collective-permute-start(f32[3,3,8,128]{3,2,1,0:T(8,128)S(1)} %get-tuple-element.58), channel_id=1, source_target_pairs={{0,3},{1,2},{2,1},{3,0},{4,7},{5,6},{6,5},{7,4},{8,11},{9,10},{10,... | collective-permute-start | bytes 110600 | tf_op jit(solution)/shard_map/ppermute | solution.py:540
  61.2 4.8 %collective-permute-start.14 = (f32[3,2,8,128]{3,2,1,0:T(8,128)S(1)}, f32[3,2,8,128]{3,2,1,0:T(8,128)S(1)}, u32[]{:S(2)}, u32[]{:S(2)}) collective-permute-start(f32[3,2,8,128]{3,2,1,0:T(8,128)S(1)} %get-tuple-element.55), channel_id=1, source_target_pairs={{0,4},{4,0},{8,12},{12,8},{16,20},{20,16},{24,28},{28,24},{1,5},{5... | collective-permute-start | bytes 73736 | tf_op jit(solution)/shard_map/ppermute | solution.py:539
  62.6 6.6 %collective-permute-start.15 = (f32[3,2,8,128]{3,2,1,0:T(8,128)S(1)}, f32[3,2,8,128]{3,2,1,0:T(8,128)S(1)}, u32[]{:S(2)}, u32[]{:S(2)}) collective-permute-start(f32[3,2,8,128]{3,2,1,0:T(8,128)S(1)} %get-tuple-element.56), channel_id=1, source_target_pairs={{0,28},{4,8},{8,4},{12,16},{16,12},{20,24},{24,20},{28,0},{1,29},{... | collective-permute-start | bytes 73736 | tf_op jit(solution)/shard_map/ppermute | solution.py:540

commit v5 on v4

--- a/solution.py
+++ b/solution.py
@@ -81,21 +81,48 @@
     return lax.dot_general(left, right, (((1,), (1,)), ((), ())), preferred_element_type=jnp.float32)
 
 
-def fetch(flags, factors, after, *refs):
-    *near, sems = refs
-    cold = near[0]
-    side = cold.shape[1] // 2
-    inside = factors.shape[1] - 2 * side
-    copies = [
-        (factors.at[:, pl.ds(0, side)], cold.at[:, pl.ds(0, side)]),
-        (factors.at[:, pl.ds(side + inside, side)], cold.at[:, pl.ds(side, side)]),
-    ]
-    copies += [(factors.at[:, pl.ds(side, inside)], hot) for hot in near[1:]]
-    copies = [pltpu.make_async_copy(source, target, sems.at[k]) for k, (source, target) in enumerate(copies)]
-    for copy in copies:
-        copy.start()
-    for copy in copies:
-        copy.wait()
+def turn(flags, factors, after, cold, hot, kept, raw, sems):
+    boxes, count, tile, _ = factors.shape
+    side = cold.shape[0] // 2
+    inside = hot.shape[0]
+    order = sorted(range(count // 2), key=lambda group: side <= group < side + inside)
+    loads = {}
+    for group in order:
+        some = pl.ds(2 * group, 2)
+        loads[group] = pltpu.make_async_copy(factors.at[:, some], raw.at[:, some], sems.at[group])
+        loads[group].start()
+    save = pltpu.make_async_copy(cold, kept, sems.at[count // 2])
+    row_no = lax.broadcasted_iota(jnp.int32, (tile, tile), 0)
+    unit = jnp.where(row_no == lax.broadcasted_iota(jnp.int32, (tile, tile), 1), 1.0, 0.0).astype(factors.dtype)
+    for number, group in enumerate(order):
+        if number == 2 * side:
+            save.start()
+        loads[group].wait()
+        if group < side:
+            target = cold.at[group]
+        elif group < side + inside:
+            target = hot.at[group - side]
+        else:
+            target = cold.at[group - inside]
+        for place in range(2):
+            stacked = jnp.concatenate([raw[a, 2 * group + place] for a in range(boxes)], axis=0)
+            turned = nt_dot(unit, stacked).astype(factors.dtype)
+            for a in range(boxes):
+                spot = (pl.ds(a * tile, tile), pl.ds(place * tile, tile))
+                target[spot] = turned[:, a * tile : (a + 1) * tile]
+    save.wait()
+
+
+def fetch(flags, kept, after, cold, sems):
+    rows = cold.shape[1] // (sems.shape[0] // cold.shape[0])
+    loads = []
+    for number in range(sems.shape[0]):
+        spot = (number % cold.shape[0], pl.ds(number // cold.shape[0] * rows, rows))
+        loads.append(pltpu.make_async_copy(kept.at[spot], cold.at[spot], sems.at[number]))
+    for load in loads:
+        load.start()
+    for load in loads:
+        load.wait()
 
 
 def pack_wide(flags, trans, accum, coupling, rhs, start, agg, far_cells, far_index, block, first, second, groups, near_accum, cells, index, sems):
@@ -389,64 +416,77 @@
             coeffs[GR + c, column] = field[RHS + c, column]
 
 
-def tile_apply(values, coeffs, tiles, column, first, last):
-    scaled = [coeffs[GI + c, column] * values[c] for c in range(3)]
-    stacked = jnp.concatenate(scaled, axis=0)
-    width = scaled[0].shape[0]
+def tile_apply(values, coeffs, tiles, columns, first, last):
+    stacked = [coeffs[GI + c, column] * value[c] for column, value in zip(columns, values) for c in range(3)]
+    width, tile = stacked[0].shape
+    stacked = jnp.concatenate(stacked, axis=0)
     pair_no = lax.broadcasted_iota(jnp.int32, stacked.shape, 0) % width
     left = [jnp.where(pair_no == a + HX - 1, stacked, 0.0).astype(jnp.bfloat16) for a in range(first, last)]
-    right = [tiles(a, column - 1) for a in range(first, last)]
-    result = nt_dot(jnp.concatenate(left, axis=1), jnp.concatenate(right, axis=1))
-    return [result[c * width : (c + 1) * width] for c in range(3)]
+    right = tiles[first * tile : last * tile, :]
+    result = jnp.dot(jnp.concatenate(left, axis=1), right, preferred_element_type=jnp.float32)
+    return [
+        [result[(place * 3 + c) * width : (place * 3 + c + 1) * width, place * tile : (place + 1) * tile] for c in range(3)]
+        for place in range(2)
+    ]
 
 
 def solve(flags, misfit, coeffs, hot, cold, update, first, second, third, fourth, work, hold, send_shares, send_corners):
     phases, columns = work.shape[:2]
     cy = columns - 2 * HY
-    boxes, inside = hot.shape[:2]
-    width = work.shape[2]
+    inside = hot.shape[0]
+    width, tile = work.shape[2:]
+    boxes = hot.shape[1] // tile
     px = width - 2 * HX
     half = lane_half(work.shape[2:])
-    side = cold.shape[1] // 2
-
-    def tiles(a, b):
-        if b < side:
-            return cold[a, b]
-        return hot[a, b - side] if b < side + inside else cold[a, b - inside]
+    side = cold.shape[0] // 2
+    groups = 2 * side + inside
+    empty = jnp.zeros((width, tile), jnp.float32)
+
+    def tiles(group):
+        if group < side:
+            return cold.at[group]
+        return hot.at[group - side] if group < side + inside else cold.at[group - inside]
 
     for c in range(phases):
-        work[c, 0] = jnp.zeros(work.shape[2:], jnp.float32)
-        work[c, columns - 1] = jnp.zeros(work.shape[2:], jnp.float32)
-
-    def start(column):
-        new = tile_apply([misfit[c, column] for c in range(phases)], coeffs, tiles, column, 0, boxes)
-        for c in range(phases):
-            work[c, column] = new[c]
-
-    def step(source, target, shift, column, first_box, last_box):
-        applied = operate(lambda c, y: source[c, y], coeffs, column, half)
-        left = [misfit[c, column] - applied[c] for c in range(phases)]
-        new = tile_apply(left, coeffs, tiles, column, first_box, last_box)
-        for c in range(phases):
-            target[c, column - shift] = source[c, column] + new[c]
-
-    for column in range(1, columns - 1):
-        start(column)
+        work[c, 0] = empty
+        work[c, columns - 1] = empty
+
+    def pair_of(group):
+        return (1 + 2 * group, 2 + 2 * group)
+
+    def start(group):
+        values = [[misfit[c, column] for c in range(phases)] for column in pair_of(group)]
+        new = tile_apply(values, coeffs, tiles(group), pair_of(group), 0, boxes)
+        for column, value in zip(pair_of(group), new):
+            for c in range(phases):
+                work[c, column] = value[c]
+
+    def step(source, target, shift, group, first_box, last_box):
+        needed = [1 < column < columns - 2 for column in pair_of(group)]
+        values = []
+        for column, want in zip(pair_of(group), needed):
+            if want:
+                applied = operate(lambda c, y: source[c, y], coeffs, column, half)
+                values.append([misfit[c, column] - applied[c] for c in range(phases)])
+            else:
+                values.append([empty] * phases)
+        new = tile_apply(values, coeffs, tiles(group), pair_of(group), first_box, last_box)
+        for column, want, value in zip(pair_of(group), needed, new):
+            for c in range(phases):
+                if want:
+                    target[c, column - shift] = source[c, column] + value[c]
+
+    for group in range(groups):
+        start(group)
     send_shares()
-    edge = 2 * (HY - 1)
-    middle = range(2 + edge, columns - 2 - edge)
-    for column in range(2, columns - 2):
-        if column not in middle:
-            step(work, hold, 0, column, 0, boxes)
-    ends = [column for column in range(HY, HY + cy) if min(column - HY, HY + cy - 1 - column) < HY - 1]
-    for column in ends:
-        step(hold, update, HY, column, 1, boxes - 1)
+    for group in range(groups):
+        step(work, hold, 0, group, 0, boxes)
+    ends = (side, groups - side - 1)
+    for group in ends:
+        step(hold, update, HY, group, 1, boxes - 1)
     send_corners()
-    for column in middle:
-        step(work, hold, 0, column, 0, boxes)
-    for column in range(HY, HY + cy):
-        if column not in ends:
-            step(hold, update, HY, column, 1, boxes - 1)
+    for group in range(side + 1, groups - side - 1):
+        step(hold, update, HY, group, 1, boxes - 1)
     rows = rows_of(update)
     for c in range(phases):
         for pair in range(HX):
@@ -575,12 +615,11 @@
     if min(wide, narrow) < 3 or lanes != tile:
         raise ValueError("unsupported mesh")
 
-    boxes = tile_factors.shape
-    cold = ((boxes[0], 2 * COLD) + boxes[2:], tile_factors.dtype)
-    hot = ((boxes[0], boxes[1] - 2 * COLD) + boxes[2:], tile_factors.dtype)
-
-    def tiles_after(value, outs):
-        return call(fetch, outs, [pltpu.SemaphoreType.DMA((3,))], far=(0,))(flags, tile_factors, value)
+    boxes, count = tile_factors.shape[:2]
+    if HY != 3 or COLD != 2 or cy % 2:
+        raise ValueError("unsupported sizes")
+    cold = ((COLD, boxes * tile, 2 * tile), tile_factors.dtype)
+    hot = ((count // 2 - COLD, boxes * tile, 2 * tile), tile_factors.dtype)
 
     face = ((FIELDS + len(OUTER_X), cy, tile), f32)
     block, first, second = call(
@@ -598,7 +637,13 @@
     got = swap(first, second, "wide")
     face = ((narrow_rows(px), tile), f32)
     got += swap(*call(pack_narrow, [face, face])(flags, block), "narrow")
-    cold_tiles, hot_tiles = tiles_after(block, [cold, hot])
+    cold_tiles, hot_tiles, kept = call(
+        turn,
+        [cold, hot, cold],
+        [pltpu.VMEM(tile_factors.shape, tile_factors.dtype), pltpu.SemaphoreType.DMA((count // 2 + 1,))],
+        far=(0,),
+        far_outs=(2,),
+    )(flags, tile_factors, block)
     face = ((CORNER_ROWS, tile), f32)
     got += swap(*call(pack_corners, [face, face])(flags, *got[:2]), "narrow")
 
@@ -632,7 +677,7 @@
         gathered = lax.all_to_all(slots, ("wide", "narrow"), 0, 0, tiled=True)
         got = swap(*sends[:2], "wide") + swap(*sends[2:], "narrow")
         if sweep < SWEEPS - 1:
-            (cold_tiles,) = tiles_after(gathered, [cold])
+            (cold_tiles,) = call(fetch, [cold], [pltpu.SemaphoreType.DMA((COLD,))], far=(0,))(flags, kept, gathered)
         if sweep < SWEEPS - 1:
             current, slots, *sends = call(
                 functools.partial(next_sweep, px=px, narrow=narrow),

time: 71.1 us -> 69.4 us (0.976)
  Pallas kernels: 20 us -> 18.7 us
    pallas_call x10, Pallas kernels: 20 us -> 18.7 us  [run(): pl.pallas_call(body, out_shape=tuple(((pltpu.HBM if number in far_outs el...]
  transfers between devices with their start and end apart: 21 -> 21, of which waited for: 4 -> 4; matrix products, arithmetic and copies ran while one was open for 0% -> 0% of each run, Pallas kernels for 10% -> 11%
where the time goes in v5:
time: 69.4 us; the launch traced here: 69 us
  starting transfers between devices  40 us (58%)
  Pallas kernels  18.7 us (27%)
  waiting for transfers between devices  9.25 us (13%)
  between operations  0.94 us (1%)
    ppermute x9, starting transfers between devices, swap(): second = lax.ppermute(second, axis, pairs[1])  21.6 us
    pallas_call x10, Pallas kernels, run(): pl.pallas_call(body, out_shape=tuple(((pltpu.HBM if number in far_outs el...  18.7 us
    all_to_all x3, starting transfers between devices, per_device(): gathered = lax.all_to_all(slots, ('wide', 'narrow'), 0, 0, tiled=True)  9.82 us
    ppermute x9, starting transfers between devices, swap(): first = lax.ppermute(first, axis, pairs[0])  8.55 us
    ppermute x9, waiting for transfers between devices, swap(): second = lax.ppermute(second, axis, pairs[1])  4.78 us
    all_to_all x3, waiting for transfers between devices, per_device(): gathered = lax.all_to_all(slots, ('wide', 'narrow'), 0, 0, tiled=True)  4.45 us
  transfers between devices with their start and end apart: 21, of which 4 were waited for; matrix products, arithmetic and copies ran while one was open for 0% of the time, Pallas kernels for 11%

profile of v5, /device:TPU:0, one launch (start us, length us, event | category | flops | bytes accessed | tf_op | source)
XLA Modules:
  0.0 69.0 jit_solution(1943620767707545324)
XLA Ops:
  0.7 0.1 stack.33.flags
  0.8 1.6 %shard_map.113 = (f32[19,4,8,128]{3,2,1,0:T(8,128)S(1)}, f32[24,8,128]{2,1,0:T(8,128)S(1)}, f32[24,8,128]{2,1,0:T(8,128)S(1)}) custom-call(s32[9]{0:T(128)S(1)} %stack.33.flags, f32[3,4,8,128]{3,2,1,0:T(8,128)} %trans.1, f32[4,8,128]{2,1,0:T(8,128)} %accum.1, f32[3,3,4,8,128]{4,3,2,1,0:T(8,128)} %coupling.1, f32[3,4,8,128]{3,2,1,0:T(8,128)} %rhs.1, ...), custom_call_target="tpu_custom_call" | custom-call | tf_op jit(solution)/shard_map/pallas_call | solution.py:41
  2.4 3.1 %collective-permute-start = (f32[24,8,128]{2,1,0:T(8,128)S(1)}, f32[24,8,128]{2,1,0:T(8,128)S(1)}, u32[]{:S(2)}, u32[]{:S(2)}) collective-permute-start(f32[24,8,128]{2,1,0:T(8,128)S(1)} %get-tuple-element.33), channel_id=1, source_target_pairs={{0,4},{4,0},{8,12},{12,8},{16,20},{20,16},{24,28},{28,24},{1,5},{5... | collective-permute-start | bytes 294920 | tf_op jit(solution)/shard_map/ppermute | solution.py:579
  5.5 3.5 %collective-permute-start.1 = (f32[24,8,128]{2,1,0:T(8,128)S(1)}, f32[24,8,128]{2,1,0:T(8,128)S(1)}, u32[]{:S(2)}, u32[]{:S(2)}) collective-permute-start(f32[24,8,128]{2,1,0:T(8,128)S(1)} %get-tuple-element.34), channel_id=1, source_target_pairs={{0,28},{4,8},{8,4},{12,16},{16,12},{20,24},{24,20},{28,0},{1,29},{... | collective-permute-start | bytes 294920 | tf_op jit(solution)/shard_map/ppermute | solution.py:580
  9.0 0.6 shard_map.114
  9.6 0.1 collective-permute-start.2
  9.7 1.6 %collective-permute-start.3 = (f32[176,128]{1,0:T(8,128)S(1)}, f32[176,128]{1,0:T(8,128)S(1)}, u32[]{:S(2)}, u32[]{:S(2)}) collective-permute-start(f32[176,128]{1,0:T(8,128)S(1)} %get-tuple-element.36), channel_id=1, source_target_pairs={{0,3},{1,2},{2,1},{3,0},{4,7},{5,6},{6,5},{7,4},{8,11},{9,10},{10,... | collective-permute-start | bytes 270344 | tf_op jit(solution)/shard_map/ppermute | solution.py:580
  11.3 0.0 collective-permute-done.got_first.wide_first
  11.3 1.5 %collective-permute-done.1.got_second.wide_second = f32[24,8,128]{2,1,0:T(8,128)S(1)} collective-permute-done((f32[24,8,128]{2,1,0:T(8,128)S(1)}, f32[24,8,128]{2,1,0:T(8,128)S(1)}, u32[]{:S(2)}, u32[]{:S(2)}) %collective-permute-start.1) | collective-permute-done | bytes 98336 | tf_op jit(solution)/shard_map/ppermute | solution.py:580
  12.8 0.6 shard_map.115
  13.4 0.1 collective-permute-start.4
  13.5 1.6 %collective-permute-start.5 = (f32[64,128]{1,0:T(8,128)S(1)}, f32[64,128]{1,0:T(8,128)S(1)}, u32[]{:S(2)}, u32[]{:S(2)}) collective-permute-start(f32[64,128]{1,0:T(8,128)S(1)} %get-tuple-element.38), channel_id=1, source_target_pairs={{0,3},{1,2},{2,1},{3,0},{4,7},{5,6},{6,5},{7,4},{8,11},{9,10},{10,... | collective-permute-start | bytes 98312 | tf_op jit(solution)/shard_map/ppermute | solution.py:580
  15.1 3.2 %shard_map.116 = (bf16[2,768,256]{2,1,0:T(8,128)(2,1)S(1)}, bf16[4,768,256]{2,1,0:T(8,128)(2,1)S(1)}, bf16[2,768,256]{2,1,0:T(8,128)(2,1)}) custom-call(s32[9]{0:T(128)S(1)} %stack.33.flags, bf16[6,12,128,128]{3,2,1,0:T(8,128)(2,1)} %factors.1, f32[19,4,8,128]{3,2,1,0:T(8,128)S(1)} %get-tuple-element.32.block.after), custom_call_target="tpu_custom_call" | custom-call | tf_op jit(solution)/shard_map/pallas_call | solution.py:41
  18.3 0.0 collective-permute-done.2.narrow_first
  18.3 0.0 collective-permute-done.3.narrow_second
  18.3 0.0 collective-permute-done.4.corner_first
  18.3 0.0 collective-permute-done.5.corner_second
  18.4 2.7 %shard_map.117 = (f32[18,13,8,128]{3,2,1,0:T(8,128)S(1)}, s32[14,8,128]{2,1,0:T(8,128)S(1)}, f32[3,14,8,128]{3,2,1,0:T(8,128)S(1)}, f32[32,3,4,128]{3,2,1,0:T(4,...) custom-call(s32[9]{0:T(128)S(1)} %stack.33.flags, ...), custom_call_target="tpu_custom_call" | custom-call | tf_op jit(solution)/shard_map/pallas_call | solution.py:41
  21.0 3.9 %all-to-all-start = ((f32[32,3,4,128]{3,2,1,0:T(4,128)}), f32[32,3,4,128]{3,2,1,0:T(4,128)S(1)}, u32[]{:S(2)}, u32[]{:S(2)}) async-start(f32[32,3,4,128]{3,2,1,0:T(4,128)} %get-tuple-element.48), calls=%async_computation | async-start | bytes 393216 | tf_op jit(solution)/shard_map/all_to_all | solution.py:677
  25.0 0.3 collective-permute-start.8
  25.3 1.6 %collective-permute-start.9 = (f32[3,3,8,128]{3,2,1,0:T(8,128)S(1)}, f32[3,3,8,128]{3,2,1,0:T(8,128)S(1)}, u32[]{:S(2)}, u32[]{:S(2)}) collective-permute-start(f32[3,3,8,128]{3,2,1,0:T(8,128)S(1)} %get-tuple-element.47), channel_id=1, source_target_pairs={{0,3},{1,2},{2,1},{3,0},{4,7},{5,6},{6,5},{7,4},{8,11},{9,10},{10,... | collective-permute-start | bytes 110600 | tf_op jit(solution)/shard_map/ppermute | solution.py:580
  26.9 1.5 %collective-permute-start.6 = (f32[3,2,8,128]{3,2,1,0:T(8,128)S(1)}, f32[3,2,8,128]{3,2,1,0:T(8,128)S(1)}, u32[]{:S(2)}, u32[]{:S(2)}) collective-permute-start(f32[3,2,8,128]{3,2,1,0:T(8,128)S(1)} %get-tuple-element.44), channel_id=1, source_target_pairs={{0,4},{4,0},{8,12},{12,8},{16,20},{20,16},{24,28},{28,24},{1,5},{5... | collective-permute-start | bytes 73736 | tf_op jit(solution)/shard_map/ppermute | solution.py:579
  28.4 3.3 %collective-permute-start.7 = (f32[3,2,8,128]{3,2,1,0:T(8,128)S(1)}, f32[3,2,8,128]{3,2,1,0:T(8,128)S(1)}, u32[]{:S(2)}, u32[]{:S(2)}) collective-permute-start(f32[3,2,8,128]{3,2,1,0:T(8,128)S(1)} %get-tuple-element.45), channel_id=1, source_target_pairs={{0,28},{4,8},{8,4},{12,16},{16,12},{20,24},{24,20},{28,0},{1,29},{... | collective-permute-start | bytes 73736 | tf_op jit(solution)/shard_map/ppermute | solution.py:580
  31.7 2.2 %all-to-all-done.after.slots_in = f32[32,3,4,128]{3,2,1,0:T(4,128)S(1)} async-done(((f32[32,3,4,128]{3,2,1,0:T(4,128)}), f32[32,3,4,128]{3,2,1,0:T(4,128)S(1)}, u32[]{:S(2)}, u32[]{:S(2)}) %all-to-all-start) | async-done | bytes 196640 | tf_op jit(solution)/shard_map/all_to_all | solution.py:677
  33.9 1.7 %shard_map.118.cold = bf16[2,768,256]{2,1,0:T(8,128)(2,1)S(1)} custom-call(s32[9]{0:T(128)S(1)} %stack.33.flags, bf16[2,768,256]{2,1,0:T(8,128)(2,1)} %get-tuple-element.49.kept, f32[32,3,4,128]{3,2,1,0:T(4,128)S(1)} %all-to-all-done.after.slots_in), custom_call_target="tpu_custom_call" | custom-call | tf_op jit(solution)/shard_map/pallas_call | solution.py:41
  35.6 0.0 collective-permute-done.6.got_0
  35.6 0.0 collective-permute-done.7.got_1
  35.6 0.0 collective-permute-done.8.got_2
  35.7 0.0 collective-permute-done.9.got_3
  35.7 2.6 %shard_map.119 = (f32[3,14,8,128]{3,2,1,0:T(8,128)S(1)}, f32[32,3,4,128]{3,2,1,0:T(4,128)}, f32[3,2,8,128]{3,2,1,0:T(8,128)S(1)}, f32[3,2,8,128]{3,2,1,0:T(8,128...) custom-call(s32[9]{0:T(128)S(1)} %stack.33.flags, f32[3,14,8,128]{3,2,1,0:T(8,128)S(1)} %get-tuple-element.41.current, ...), custom_call_target="tpu_custom_call" | custom-call | tf_op jit(solution)/shard_map/pallas_call | solution.py:41
  38.3 2.9 %all-to-all-start.1 = ((f32[32,3,4,128]{3,2,1,0:T(4,128)}), f32[32,3,4,128]{3,2,1,0:T(4,128)S(1)}, u32[]{:S(2)}, u32[]{:S(2)}) async-start(f32[32,3,4,128]{3,2,1,0:T(4,128)} %get-tuple-element.55), calls=%async_computation.1 | async-start | bytes 393216 | tf_op jit(solution)/shard_map/all_to_all | solution.py:677
  41.3 0.3 collective-permute-start.12
  41.6 1.6 %collective-permute-start.13 = (f32[3,3,8,128]{3,2,1,0:T(8,128)S(1)}, f32[3,3,8,128]{3,2,1,0:T(8,128)S(1)}, u32[]{:S(2)}, u32[]{:S(2)}) collective-permute-start(f32[3,3,8,128]{3,2,1,0:T(8,128)S(1)} %get-tuple-element.54), channel_id=1, source_target_pairs={{0,3},{1,2},{2,1},{3,0},{4,7},{5,6},{6,5},{7,4},{8,11},{9,10},{10,... | collective-permute-start | bytes 110600 | tf_op jit(solution)/shard_map/ppermute | solution.py:580
  43.2 1.5 %collective-permute-start.10 = (f32[3,2,8,128]{3,2,1,0:T(8,128)S(1)}, f32[3,2,8,128]{3,2,1,0:T(8,128)S(1)}, u32[]{:S(2)}, u32[]{:S(2)}) collective-permute-start(f32[3,2,8,128]{3,2,1,0:T(8,128)S(1)} %get-tuple-element.51), channel_id=1, source_target_pairs={{0,4},{4,0},{8,12},{12,8},{16,20},{20,16},{24,28},{28,24},{1,5},{5... | collective-permute-start | bytes 73736 | tf_op jit(solution)/shard_map/ppermute | solution.py:579
  44.7 3.3 %collective-permute-start.11 = (f32[3,2,8,128]{3,2,1,0:T(8,128)S(1)}, f32[3,2,8,128]{3,2,1,0:T(8,128)S(1)}, u32[]{:S(2)}, u32[]{:S(2)}) collective-permute-start(f32[3,2,8,128]{3,2,1,0:T(8,128)S(1)} %get-tuple-element.52), channel_id=1, source_target_pairs={{0,28},{4,8},{8,4},{12,16},{16,12},{20,24},{24,20},{28,0},{1,29},{... | collective-permute-start | bytes 73736 | tf_op jit(solution)/shard_map/ppermute | solution.py:580
  48.0 2.2 %all-to-all-done.1.after.slots_in = f32[32,3,4,128]{3,2,1,0:T(4,128)S(1)} async-done(((f32[32,3,4,128]{3,2,1,0:T(4,128)}), f32[32,3,4,128]{3,2,1,0:T(4,128)S(1)}, u32[]{:S(2)}, u32[]{:S(2)}) %all-to-all-start.1) | async-done | bytes 196640 | tf_op jit(solution)/shard_map/all_to_all | solution.py:677
  50.2 1.7 %shard_map.120.cold = bf16[2,768,256]{2,1,0:T(8,128)(2,1)S(1)} custom-call(s32[9]{0:T(128)S(1)} %stack.33.flags, bf16[2,768,256]{2,1,0:T(8,128)(2,1)} %get-tuple-element.49.kept, f32[32,3,4,128]{3,2,1,0:T(4,128)S(1)} %all-to-all-done.1.after.slots_in), custom_call_target="tpu_custom_call" | custom-call | tf_op jit(solution)/shard_map/pallas_call | solution.py:41
  51.9 0.0 collective-permute-done.10.got_0
  51.9 0.0 collective-permute-done.11.got_1
  51.9 0.0 collective-permute-done.13.got_3
  51.9 2.6 %shard_map.121 = (f32[3,14,8,128]{3,2,1,0:T(8,128)S(1)}, f32[32,3,4,128]{3,2,1,0:T(4,128)}, f32[3,2,8,128]{3,2,1,0:T(8,128)S(1)}, f32[3,2,8,128]{3,2,1,0:T(8,128...) custom-call(s32[9]{0:T(128)S(1)} %stack.33.flags, f32[3,14,8,128]{3,2,1,0:T(8,128)S(1)} %get-tuple-element.50.current, ...), custom_call_target="tpu_custom_call" | custom-call | tf_op jit(solution)/shard_map/pallas_call | solution.py:41
  54.6 2.9 %all-to-all-start.2 = ((f32[32,3,4,128]{3,2,1,0:T(4,128)}), f32[32,3,4,128]{3,2,1,0:T(4,128)S(1)}, u32[]{:S(2)}, u32[]{:S(2)}) async-start(f32[32,3,4,128]{3,2,1,0:T(4,128)} %get-tuple-element.61), calls=%async_computation.2 | async-start | bytes 393216 | tf_op jit(solution)/shard_map/all_to_all | solution.py:677
  57.5 0.3 collective-permute-start.16
  57.8 1.6 %collective-permute-start.17 = (f32[3,3,8,128]{3,2,1,0:T(8,128)S(1)}, f32[3,3,8,128]{3,2,1,0:T(8,128)S(1)}, u32[]{:S(2)}, u32[]{:S(2)}) collective-permute-start(f32[3,3,8,128]{3,2,1,0:T(8,128)S(1)} %get-tuple-element.60), channel_id=1, source_target_pairs={{0,3},{1,2},{2,1},{3,0},{4,7},{5,6},{6,5},{7,4},{8,11},{9,10},{10,... | collective-permute-start | bytes 110600 | tf_op jit(solution)/shard_map/ppermute | solution.py:580
  59.5 1.5 %collective-permute-start.14 = (f32[3,2,8,128]{3,2,1,0:T(8,128)S(1)}, f32[3,2,8,128]{3,2,1,0:T(8,128)S(1)}, u32[]{:S(2)}, u32[]{:S(2)}) collective-permute-start(f32[3,2,8,128]{3,2,1,0:T(8,128)S(1)} %get-tuple-element.57), channel_id=1, source_target_pairs={{0,4},{4,0},{8,12},{12,8},{16,20},{20,16},{24,28},{28,24},{1,5},{5... | collective-permute-start | bytes 73736 | tf_op jit(solution)/shard_map/ppermute | solution.py:579
  60.9 3.3 %collective-permute-start.15 = (f32[3,2,8,128]{3,2,1,0:T(8,128)S(1)}, f32[3,2,8,128]{3,2,1,0:T(8,128)S(1)}, u32[]{:S(2)}, u32[]{:S(2)}) collective-permute-start(f32[3,2,8,128]{3,2,1,0:T(8,128)S(1)} %get-tuple-element.58), channel_id=1, source_target_pairs={{0,28},{4,8},{8,4},{12,16},{16,12},{20,24},{24,20},{28,0},{1,29},{... | collective-permute-start | bytes 73736 | tf_op jit(solution)/shard_map/ppermute | solution.py:580
  64.3 3.3 %collective-permute-done.15.got_1 = f32[3,2,8,128]{3,2,1,0:T(8,128)S(1)} collective-permute-done((f32[3,2,8,128]{3,2,1,0:T(8,128)S(1)}, f32[3,2,8,128]{3,2,1,0:T(8,128)S(1)}, u32[]{:S(2)}, u32[]{:S(2)}) %collective-permute-start.15) | collective-permute-done | bytes 24608 | tf_op jit(solution)/shard_map/ppermute | solution.py:580
  67.5 1.4 %shard_map.122 = (f32[3,4,8,128]{3,2,1,0:T(8,128)}, f32[3,4,8,128]{3,2,1,0:T(8,128)}) custom-call(s32[9]{0:T(128)S(1)} %stack.33.flags, f32[3,14,8,128]{3,2,1,0:T(8,128)S(1)} %get-tuple-element.56.current, f32[18,13,8,128]{3,2,1,0:T(8,128)S(1)} %get-tuple-element.42.coeffs, s32[14,8,128]{2,1,0:T(8,128)S(1)} %get-tuple-element.43.index, ...), custom_call_target="tpu_custom_call" | custom-call | tf_op jit(solution)/shard_map/pallas_call | solution.py:41
  (7 shorter events, 0.0 us)
Async XLA Ops:
  0.6 17.7 %copy-start = (f32[32,1024]{1,0:T(8,128)S(1)}, f32[32,1024]{1,0:T(8,128)}, u32[]{:S(2)}) copy-start(f32[32,1024]{1,0:T(8,128)} %cinv.5) | copy-start | bytes 393220
  2.4 8.9 %collective-permute-start = (f32[24,8,128]{2,1,0:T(8,128)S(1)}, f32[24,8,128]{2,1,0:T(8,128)S(1)}, u32[]{:S(2)}, u32[]{:S(2)}) collective-permute-start(f32[24,8,128]{2,1,0:T(8,128)S(1)} %get-tuple-element.33), channel_id=1, source_target_pairs={{0,4},{4,0},{8,12},{12,8},{16,20},{20,16},{24,28},{28,24},{1,5},{5... | collective-permute-start | bytes 294920 | tf_op jit(solution)/shard_map/ppermute | solution.py:579
  5.5 7.3 %collective-permute-start.1 = (f32[24,8,128]{2,1,0:T(8,128)S(1)}, f32[24,8,128]{2,1,0:T(8,128)S(1)}, u32[]{:S(2)}, u32[]{:S(2)}) collective-permute-start(f32[24,8,128]{2,1,0:T(8,128)S(1)} %get-tuple-element.34), channel_id=1, source_target_pairs={{0,28},{4,8},{8,4},{12,16},{16,12},{20,24},{24,20},{28,0},{1,29},{... | collective-permute-start | bytes 294920 | tf_op jit(solution)/shard_map/ppermute | solution.py:580
  9.6 8.7 %collective-permute-start.2 = (f32[176,128]{1,0:T(8,128)S(1)}, f32[176,128]{1,0:T(8,128)S(1)}, u32[]{:S(2)}, u32[]{:S(2)}) collective-permute-start(f32[176,128]{1,0:T(8,128)S(1)} %get-tuple-element.35), channel_id=1, source_target_pairs={{0,1},{1,0},{2,3},{3,2},{4,5},{5,4},{6,7},{7,6},{8,9},{9,8},{10,11... | collective-permute-start | bytes 270344 | tf_op jit(solution)/shard_map/ppermute | solution.py:579
  9.7 8.6 %collective-permute-start.3 = (f32[176,128]{1,0:T(8,128)S(1)}, f32[176,128]{1,0:T(8,128)S(1)}, u32[]{:S(2)}, u32[]{:S(2)}) collective-permute-start(f32[176,128]{1,0:T(8,128)S(1)} %get-tuple-element.36), channel_id=1, source_target_pairs={{0,3},{1,2},{2,1},{3,0},{4,7},{5,6},{6,5},{7,4},{8,11},{9,10},{10,... | collective-permute-start | bytes 270344 | tf_op jit(solution)/shard_map/ppermute | solution.py:580
  13.4 4.9 %collective-permute-start.4 = (f32[64,128]{1,0:T(8,128)S(1)}, f32[64,128]{1,0:T(8,128)S(1)}, u32[]{:S(2)}, u32[]{:S(2)}) collective-permute-start(f32[64,128]{1,0:T(8,128)S(1)} %get-tuple-element.37), channel_id=1, source_target_pairs={{0,1},{1,0},{2,3},{3,2},{4,5},{5,4},{6,7},{7,6},{8,9},{9,8},{10,11... | collective-permute-start | bytes 98312 | tf_op jit(solution)/shard_map/ppermute | solution.py:579
  13.5 4.8 %collective-permute-start.5 = (f32[64,128]{1,0:T(8,128)S(1)}, f32[64,128]{1,0:T(8,128)S(1)}, u32[]{:S(2)}, u32[]{:S(2)}) collective-permute-start(f32[64,128]{1,0:T(8,128)S(1)} %get-tuple-element.38), channel_id=1, source_target_pairs={{0,3},{1,2},{2,1},{3,0},{4,7},{5,6},{6,5},{7,4},{8,11},{9,10},{10,... | collective-permute-start | bytes 98312 | tf_op jit(solution)/shard_map/ppermute | solution.py:580
  21.0 12.9 %all-to-all-start = ((f32[32,3,4,128]{3,2,1,0:T(4,128)}), f32[32,3,4,128]{3,2,1,0:T(4,128)S(1)}, u32[]{:S(2)}, u32[]{:S(2)}) async-start(f32[32,3,4,128]{3,2,1,0:T(4,128)} %get-tuple-element.48), calls=%async_computation | async-start | bytes 393216 | tf_op jit(solution)/shard_map/all_to_all | solution.py:677
  25.0 10.7 %collective-permute-start.8 = (f32[3,3,8,128]{3,2,1,0:T(8,128)S(1)}, f32[3,3,8,128]{3,2,1,0:T(8,128)S(1)}, u32[]{:S(2)}, u32[]{:S(2)}) collective-permute-start(f32[3,3,8,128]{3,2,1,0:T(8,128)S(1)} %get-tuple-element.46), channel_id=1, source_target_pairs={{0,1},{1,0},{2,3},{3,2},{4,5},{5,4},{6,7},{7,6},{8,9},{9,8},{10,11... | collective-permute-start | bytes 110600 | tf_op jit(solution)/shard_map/ppermute | solution.py:579
  25.3 10.4 %collective-permute-start.9 = (f32[3,3,8,128]{3,2,1,0:T(8,128)S(1)}, f32[3,3,8,128]{3,2,1,0:T(8,128)S(1)}, u32[]{:S(2)}, u32[]{:S(2)}) collective-permute-start(f32[3,3,8,128]{3,2,1,0:T(8,128)S(1)} %get-tuple-element.47), channel_id=1, source_target_pairs={{0,3},{1,2},{2,1},{3,0},{4,7},{5,6},{6,5},{7,4},{8,11},{9,10},{10,... | collective-permute-start | bytes 110600 | tf_op jit(solution)/shard_map/ppermute | solution.py:580
  26.9 8.7 %collective-permute-start.6 = (f32[3,2,8,128]{3,2,1,0:T(8,128)S(1)}, f32[3,2,8,128]{3,2,1,0:T(8,128)S(1)}, u32[]{:S(2)}, u32[]{:S(2)}) collective-permute-start(f32[3,2,8,128]{3,2,1,0:T(8,128)S(1)} %get-tuple-element.44), channel_id=1, source_target_pairs={{0,4},{4,0},{8,12},{12,8},{16,20},{20,16},{24,28},{28,24},{1,5},{5... | collective-permute-start | bytes 73736 | tf_op jit(solution)/shard_map/ppermute | solution.py:579
  28.4 7.2 %collective-permute-start.7 = (f32[3,2,8,128]{3,2,1,0:T(8,128)S(1)}, f32[3,2,8,128]{3,2,1,0:T(8,128)S(1)}, u32[]{:S(2)}, u32[]{:S(2)}) collective-permute-start(f32[3,2,8,128]{3,2,1,0:T(8,128)S(1)} %get-tuple-element.45), channel_id=1, source_target_pairs={{0,28},{4,8},{8,4},{12,16},{16,12},{20,24},{24,20},{28,0},{1,29},{... | collective-permute-start | bytes 73736 | tf_op jit(solution)/shard_map/ppermute | solution.py:580
  38.3 11.9 %all-to-all-start.1 = ((f32[32,3,4,128]{3,2,1,0:T(4,128)}), f32[32,3,4,128]{3,2,1,0:T(4,128)S(1)}, u32[]{:S(2)}, u32[]{:S(2)}) async-start(f32[32,3,4,128]{3,2,1,0:T(4,128)} %get-tuple-element.55), calls=%async_computation.1 | async-start | bytes 393216 | tf_op jit(solution)/shard_map/all_to_all | solution.py:677
  41.3 10.7 %collective-permute-start.12 = (f32[3,3,8,128]{3,2,1,0:T(8,128)S(1)}, f32[3,3,8,128]{3,2,1,0:T(8,128)S(1)}, u32[]{:S(2)}, u32[]{:S(2)}) collective-permute-start(f32[3,3,8,128]{3,2,1,0:T(8,128)S(1)} %get-tuple-element.53), channel_id=1, source_target_pairs={{0,1},{1,0},{2,3},{3,2},{4,5},{5,4},{6,7},{7,6},{8,9},{9,8},{10,11... | collective-permute-start | bytes 110600 | tf_op jit(solution)/shard_map/ppermute | solution.py:579
  41.6 10.4 %collective-permute-start.13 = (f32[3,3,8,128]{3,2,1,0:T(8,128)S(1)}, f32[3,3,8,128]{3,2,1,0:T(8,128)S(1)}, u32[]{:S(2)}, u32[]{:S(2)}) collective-permute-start(f32[3,3,8,128]{3,2,1,0:T(8,128)S(1)} %get-tuple-element.54), channel_id=1, source_target_pairs={{0,3},{1,2},{2,1},{3,0},{4,7},{5,6},{6,5},{7,4},{8,11},{9,10},{10,... | collective-permute-start | bytes 110600 | tf_op jit(solution)/shard_map/ppermute | solution.py:580
  43.2 8.7 %collective-permute-start.10 = (f32[3,2,8,128]{3,2,1,0:T(8,128)S(1)}, f32[3,2,8,128]{3,2,1,0:T(8,128)S(1)}, u32[]{:S(2)}, u32[]{:S(2)}) collective-permute-start(f32[3,2,8,128]{3,2,1,0:T(8,128)S(1)} %get-tuple-element.51), channel_id=1, source_target_pairs={{0,4},{4,0},{8,12},{12,8},{16,20},{20,16},{24,28},{28,24},{1,5},{5... | collective-permute-start | bytes 73736 | tf_op jit(solution)/shard_map/ppermute | solution.py:579
  44.7 7.2 %collective-permute-start.11 = (f32[3,2,8,128]{3,2,1,0:T(8,128)S(1)}, f32[3,2,8,128]{3,2,1,0:T(8,128)S(1)}, u32[]{:S(2)}, u32[]{:S(2)}) collective-permute-start(f32[3,2,8,128]{3,2,1,0:T(8,128)S(1)} %get-tuple-element.52), channel_id=1, source_target_pairs={{0,28},{4,8},{8,4},{12,16},{16,12},{20,24},{24,20},{28,0},{1,29},{... | collective-permute-start | bytes 73736 | tf_op jit(solution)/shard_map/ppermute | solution.py:580
  54.6 13.0 %all-to-all-start.2 = ((f32[32,3,4,128]{3,2,1,0:T(4,128)}), f32[32,3,4,128]{3,2,1,0:T(4,128)S(1)}, u32[]{:S(2)}, u32[]{:S(2)}) async-start(f32[32,3,4,128]{3,2,1,0:T(4,128)} %get-tuple-element.61), calls=%async_computation.2 | async-start | bytes 393216 | tf_op jit(solution)/shard_map/all_to_all | solution.py:677
  57.5 10.0 %collective-permute-start.16 = (f32[3,3,8,128]{3,2,1,0:T(8,128)S(1)}, f32[3,3,8,128]{3,2,1,0:T(8,128)S(1)}, u32[]{:S(2)}, u32[]{:S(2)}) collective-permute-start(f32[3,3,8,128]{3,2,1,0:T(8,128)S(1)} %get-tuple-element.59), channel_id=1, source_target_pairs={{0,1},{1,0},{2,3},{3,2},{4,5},{5,4},{6,7},{7,6},{8,9},{9,8},{10,11... | collective-permute-start | bytes 110600 | tf_op jit(solution)/shard_map/ppermute | solution.py:579
  57.8 9.7 %collective-permute-start.17 = (f32[3,3,8,128]{3,2,1,0:T(8,128)S(1)}, f32[3,3,8,128]{3,2,1,0:T(8,128)S(1)}, u32[]{:S(2)}, u32[]{:S(2)}) collective-permute-start(f32[3,3,8,128]{3,2,1,0:T(8,128)S(1)} %get-tuple-element.60), channel_id=1, source_target_pairs={{0,3},{1,2},{2,1},{3,0},{4,7},{5,6},{6,5},{7,4},{8,11},{9,10},{10,... | collective-permute-start | bytes 110600 | tf_op jit(solution)/shard_map/ppermute | solution.py:580
  59.5 4.8 %collective-permute-start.14 = (f32[3,2,8,128]{3,2,1,0:T(8,128)S(1)}, f32[3,2,8,128]{3,2,1,0:T(8,128)S(1)}, u32[]{:S(2)}, u32[]{:S(2)}) collective-permute-start(f32[3,2,8,128]{3,2,1,0:T(8,128)S(1)} %get-tuple-element.57), channel_id=1, source_target_pairs={{0,4},{4,0},{8,12},{12,8},{16,20},{20,16},{24,28},{28,24},{1,5},{5... | collective-permute-start | bytes 73736 | tf_op jit(solution)/shard_map/ppermute | solution.py:579
  60.9 6.6 %collective-permute-start.15 = (f32[3,2,8,128]{3,2,1,0:T(8,128)S(1)}, f32[3,2,8,128]{3,2,1,0:T(8,128)S(1)}, u32[]{:S(2)}, u32[]{:S(2)}) collective-permute-start(f32[3,2,8,128]{3,2,1,0:T(8,128)S(1)} %get-tuple-element.58), channel_id=1, source_target_pairs={{0,28},{4,8},{8,4},{12,16},{16,12},{20,24},{24,20},{28,0},{1,29},{... | collective-permute-start | bytes 73736 | tf_op jit(solution)/shard_map/ppermute | solution.py:580

commit v6 on v5

--- a/solution.py
+++ b/solution.py
@@ -352,6 +352,8 @@
     sends = []
 
     def send_corners():
+        if slots.shape[1] == 1:
+            return
         near = lane_half(update.shape[2:])
         for number, (x, y) in enumerate(CORNERS):
             rows = []
@@ -521,7 +523,7 @@
                 place = column if y < 0 else column - HY - cy
                 away = HY - column if y < 0 else place + 1
                 change = jnp.where(owned, received(flags, 1, got[2][c, place], got[3][c, place])[(y + 1) // 2], 0.0)
-                for number, (x, side) in enumerate(CORNERS):
+                for number, (x, side) in enumerate(CORNERS if slots_in.shape[1] > 1 else ()):
                     for tile_no, (pairs, distance) in enumerate(CORNER_TILES):
                         if side == y and distance == away:
                             pair = HX - pairs if x < 0 else HX + px + pairs - 1
@@ -651,6 +653,7 @@
     field = ((phases, columns) + vec, f32)
     inner = ((phases, columns - 1) + vec, f32)
     slot = ((wide * narrow,) + SLOT + (lanes,), f32)
+    last_slot = ((wide * narrow, 1) + SLOT[1:] + (lanes,), f32)
     part = ((phases, cy) + vec, f32)
     face = ((phases, HX, cy, tile), f32)
     edge_face = ((phases, HY) + vec, f32)
@@ -681,7 +684,7 @@
         if sweep < SWEEPS - 1:
             current, slots, *sends = call(
                 functools.partial(next_sweep, px=px, narrow=narrow),
-                [field, slot] + faces,
+                [field, slot if sweep < SWEEPS - 2 else last_slot] + faces,
                 scratch,
                 far_outs=(1,),
             )(flags, current, coeffs, index, *got, gathered, coarse_inverse, hot_tiles, cold_tiles)

time: 69.4 us -> 69.2 us (level)
  no operation moved by 1% of the time
where the time goes in v6:
time: 69.2 us; the launch traced here: 68.9 us
  starting transfers between devices  40 us (58%)
  Pallas kernels  18.7 us (27%)
  waiting for transfers between devices  9.18 us (13%)
  between operations  0.94 us (1%)
    ppermute x9, starting transfers between devices, swap(): second = lax.ppermute(second, axis, pairs[1])  21.6 us
    pallas_call x10, Pallas kernels, run(): pl.pallas_call(body, out_shape=tuple(((pltpu.HBM if number in far_outs el...  18.7 us
    all_to_all x3, starting transfers between devices, per_device(): gathered = lax.all_to_all(slots, ('wide', 'narrow'), 0, 0, tiled=True)  9.82 us
    ppermute x9, starting transfers between devices, swap(): first = lax.ppermute(first, axis, pairs[0])  8.55 us
    ppermute x9, waiting for transfers between devices, swap(): second = lax.ppermute(second, axis, pairs[1])  4.71 us
    all_to_all x3, waiting for transfers between devices, per_device(): gathered = lax.all_to_all(slots, ('wide', 'narrow'), 0, 0, tiled=True)  4.45 us
  transfers between devices with their start and end apart: 21, of which 4 were waited for; matrix products, arithmetic and copies ran while one was open for 0% of the time, Pallas kernels for 11%

profile of v6, /device:TPU:0, one launch (start us, length us, event | category | flops | bytes accessed | tf_op | source)
XLA Modules:
  0.0 68.9 jit_solution(1611757125310708764)
XLA Ops:
  0.7 0.1 stack.33.flags
  0.8 1.6 %shard_map.113 = (f32[19,4,8,128]{3,2,1,0:T(8,128)S(1)}, f32[24,8,128]{2,1,0:T(8,128)S(1)}, f32[24,8,128]{2,1,0:T(8,128)S(1)}) custom-call(s32[9]{0:T(128)S(1)} %stack.33.flags, f32[3,4,8,128]{3,2,1,0:T(8,128)} %trans.1, f32[4,8,128]{2,1,0:T(8,128)} %accum.1, f32[3,3,4,8,128]{4,3,2,1,0:T(8,128)} %coupling.1, f32[3,4,8,128]{3,2,1,0:T(8,128)} %rhs.1, ...), custom_call_target="tpu_custom_call" | custom-call | tf_op jit(solution)/shard_map/pallas_call | solution.py:41
  2.4 3.1 %collective-permute-start = (f32[24,8,128]{2,1,0:T(8,128)S(1)}, f32[24,8,128]{2,1,0:T(8,128)S(1)}, u32[]{:S(2)}, u32[]{:S(2)}) collective-permute-start(f32[24,8,128]{2,1,0:T(8,128)S(1)} %get-tuple-element.33), channel_id=1, source_target_pairs={{0,4},{4,0},{8,12},{12,8},{16,20},{20,16},{24,28},{28,24},{1,5},{5... | collective-permute-start | bytes 294920 | tf_op jit(solution)/shard_map/ppermute | solution.py:581
  5.5 3.5 %collective-permute-start.1 = (f32[24,8,128]{2,1,0:T(8,128)S(1)}, f32[24,8,128]{2,1,0:T(8,128)S(1)}, u32[]{:S(2)}, u32[]{:S(2)}) collective-permute-start(f32[24,8,128]{2,1,0:T(8,128)S(1)} %get-tuple-element.34), channel_id=1, source_target_pairs={{0,28},{4,8},{8,4},{12,16},{16,12},{20,24},{24,20},{28,0},{1,29},{... | collective-permute-start | bytes 294920 | tf_op jit(solution)/shard_map/ppermute | solution.py:582
  9.0 0.6 shard_map.114
  9.6 0.1 collective-permute-start.2
  9.7 1.6 %collective-permute-start.3 = (f32[176,128]{1,0:T(8,128)S(1)}, f32[176,128]{1,0:T(8,128)S(1)}, u32[]{:S(2)}, u32[]{:S(2)}) collective-permute-start(f32[176,128]{1,0:T(8,128)S(1)} %get-tuple-element.36), channel_id=1, source_target_pairs={{0,3},{1,2},{2,1},{3,0},{4,7},{5,6},{6,5},{7,4},{8,11},{9,10},{10,... | collective-permute-start | bytes 270344 | tf_op jit(solution)/shard_map/ppermute | solution.py:582
  11.3 0.0 collective-permute-done.got_first.wide_first
  11.3 1.5 %collective-permute-done.1.got_second.wide_second = f32[24,8,128]{2,1,0:T(8,128)S(1)} collective-permute-done((f32[24,8,128]{2,1,0:T(8,128)S(1)}, f32[24,8,128]{2,1,0:T(8,128)S(1)}, u32[]{:S(2)}, u32[]{:S(2)}) %collective-permute-start.1) | collective-permute-done | bytes 98336 | tf_op jit(solution)/shard_map/ppermute | solution.py:582
  12.8 0.6 shard_map.115
  13.4 0.1 collective-permute-start.4
  13.5 1.6 %collective-permute-start.5 = (f32[64,128]{1,0:T(8,128)S(1)}, f32[64,128]{1,0:T(8,128)S(1)}, u32[]{:S(2)}, u32[]{:S(2)}) collective-permute-start(f32[64,128]{1,0:T(8,128)S(1)} %get-tuple-element.38), channel_id=1, source_target_pairs={{0,3},{1,2},{2,1},{3,0},{4,7},{5,6},{6,5},{7,4},{8,11},{9,10},{10,... | collective-permute-start | bytes 98312 | tf_op jit(solution)/shard_map/ppermute | solution.py:582
  15.1 3.2 %shard_map.116 = (bf16[2,768,256]{2,1,0:T(8,128)(2,1)S(1)}, bf16[4,768,256]{2,1,0:T(8,128)(2,1)S(1)}, bf16[2,768,256]{2,1,0:T(8,128)(2,1)}) custom-call(s32[9]{0:T(128)S(1)} %stack.33.flags, bf16[6,12,128,128]{3,2,1,0:T(8,128)(2,1)} %factors.1, f32[19,4,8,128]{3,2,1,0:T(8,128)S(1)} %get-tuple-element.32.block.after), custom_call_target="tpu_custom_call" | custom-call | tf_op jit(solution)/shard_map/pallas_call | solution.py:41
  18.3 0.0 collective-permute-done.2.narrow_first
  18.3 0.0 collective-permute-done.3.narrow_second
  18.3 0.0 collective-permute-done.4.corner_first
  18.3 0.0 collective-permute-done.5.corner_second
  18.4 2.7 %shard_map.117 = (f32[18,13,8,128]{3,2,1,0:T(8,128)S(1)}, s32[14,8,128]{2,1,0:T(8,128)S(1)}, f32[3,14,8,128]{3,2,1,0:T(8,128)S(1)}, f32[32,3,4,128]{3,2,1,0:T(4,...) custom-call(s32[9]{0:T(128)S(1)} %stack.33.flags, ...), custom_call_target="tpu_custom_call" | custom-call | tf_op jit(solution)/shard_map/pallas_call | solution.py:41
  21.0 3.9 %all-to-all-start = ((f32[32,3,4,128]{3,2,1,0:T(4,128)}), f32[32,3,4,128]{3,2,1,0:T(4,128)S(1)}, u32[]{:S(2)}, u32[]{:S(2)}) async-start(f32[32,3,4,128]{3,2,1,0:T(4,128)} %get-tuple-element.48), calls=%async_computation | async-start | bytes 393216 | tf_op jit(solution)/shard_map/all_to_all | solution.py:680
  25.0 0.3 collective-permute-start.8
  25.3 1.6 %collective-permute-start.9 = (f32[3,3,8,128]{3,2,1,0:T(8,128)S(1)}, f32[3,3,8,128]{3,2,1,0:T(8,128)S(1)}, u32[]{:S(2)}, u32[]{:S(2)}) collective-permute-start(f32[3,3,8,128]{3,2,1,0:T(8,128)S(1)} %get-tuple-element.47), channel_id=1, source_target_pairs={{0,3},{1,2},{2,1},{3,0},{4,7},{5,6},{6,5},{7,4},{8,11},{9,10},{10,... | collective-permute-start | bytes 110600 | tf_op jit(solution)/shard_map/ppermute | solution.py:582
  26.9 1.5 %collective-permute-start.6 = (f32[3,2,8,128]{3,2,1,0:T(8,128)S(1)}, f32[3,2,8,128]{3,2,1,0:T(8,128)S(1)}, u32[]{:S(2)}, u32[]{:S(2)}) collective-permute-start(f32[3,2,8,128]{3,2,1,0:T(8,128)S(1)} %get-tuple-element.44), channel_id=1, source_target_pairs={{0,4},{4,0},{8,12},{12,8},{16,20},{20,16},{24,28},{28,24},{1,5},{5... | collective-permute-start | bytes 73736 | tf_op jit(solution)/shard_map/ppermute | solution.py:581
  28.4 3.3 %collective-permute-start.7 = (f32[3,2,8,128]{3,2,1,0:T(8,128)S(1)}, f32[3,2,8,128]{3,2,1,0:T(8,128)S(1)}, u32[]{:S(2)}, u32[]{:S(2)}) collective-permute-start(f32[3,2,8,128]{3,2,1,0:T(8,128)S(1)} %get-tuple-element.45), channel_id=1, source_target_pairs={{0,28},{4,8},{8,4},{12,16},{16,12},{20,24},{24,20},{28,0},{1,29},{... | collective-permute-start | bytes 73736 | tf_op jit(solution)/shard_map/ppermute | solution.py:582
  31.7 2.2 %all-to-all-done.after.slots_in = f32[32,3,4,128]{3,2,1,0:T(4,128)S(1)} async-done(((f32[32,3,4,128]{3,2,1,0:T(4,128)}), f32[32,3,4,128]{3,2,1,0:T(4,128)S(1)}, u32[]{:S(2)}, u32[]{:S(2)}) %all-to-all-start) | async-done | bytes 196640 | tf_op jit(solution)/shard_map/all_to_all | solution.py:680
  33.9 1.7 %shard_map.118.cold = bf16[2,768,256]{2,1,0:T(8,128)(2,1)S(1)} custom-call(s32[9]{0:T(128)S(1)} %stack.33.flags, bf16[2,768,256]{2,1,0:T(8,128)(2,1)} %get-tuple-element.49.kept, f32[32,3,4,128]{3,2,1,0:T(4,128)S(1)} %all-to-all-done.after.slots_in), custom_call_target="tpu_custom_call" | custom-call | tf_op jit(solution)/shard_map/pallas_call | solution.py:41
  35.6 0.0 collective-permute-done.6.got_0
  35.6 0.0 collective-permute-done.7.got_1
  35.6 0.0 collective-permute-done.8.got_2
  35.7 0.0 collective-permute-done.9.got_3
  35.7 2.6 %shard_map.119 = (f32[3,14,8,128]{3,2,1,0:T(8,128)S(1)}, f32[32,3,4,128]{3,2,1,0:T(4,128)}, f32[3,2,8,128]{3,2,1,0:T(8,128)S(1)}, f32[3,2,8,128]{3,2,1,0:T(8,128...) custom-call(s32[9]{0:T(128)S(1)} %stack.33.flags, f32[3,14,8,128]{3,2,1,0:T(8,128)S(1)} %get-tuple-element.41.current, ...), custom_call_target="tpu_custom_call" | custom-call | tf_op jit(solution)/shard_map/pallas_call | solution.py:41
  38.3 2.9 %all-to-all-start.1 = ((f32[32,3,4,128]{3,2,1,0:T(4,128)}), f32[32,3,4,128]{3,2,1,0:T(4,128)S(1)}, u32[]{:S(2)}, u32[]{:S(2)}) async-start(f32[32,3,4,128]{3,2,1,0:T(4,128)} %get-tuple-element.55), calls=%async_computation.1 | async-start | bytes 393216 | tf_op jit(solution)/shard_map/all_to_all | solution.py:680
  41.3 0.3 collective-permute-start.12
  41.6 1.6 %collective-permute-start.13 = (f32[3,3,8,128]{3,2,1,0:T(8,128)S(1)}, f32[3,3,8,128]{3,2,1,0:T(8,128)S(1)}, u32[]{:S(2)}, u32[]{:S(2)}) collective-permute-start(f32[3,3,8,128]{3,2,1,0:T(8,128)S(1)} %get-tuple-element.54), channel_id=1, source_target_pairs={{0,3},{1,2},{2,1},{3,0},{4,7},{5,6},{6,5},{7,4},{8,11},{9,10},{10,... | collective-permute-start | bytes 110600 | tf_op jit(solution)/shard_map/ppermute | solution.py:582
  43.2 1.5 %collective-permute-start.10 = (f32[3,2,8,128]{3,2,1,0:T(8,128)S(1)}, f32[3,2,8,128]{3,2,1,0:T(8,128)S(1)}, u32[]{:S(2)}, u32[]{:S(2)}) collective-permute-start(f32[3,2,8,128]{3,2,1,0:T(8,128)S(1)} %get-tuple-element.51), channel_id=1, source_target_pairs={{0,4},{4,0},{8,12},{12,8},{16,20},{20,16},{24,28},{28,24},{1,5},{5... | collective-permute-start | bytes 73736 | tf_op jit(solution)/shard_map/ppermute | solution.py:581
  44.7 3.3 %collective-permute-start.11 = (f32[3,2,8,128]{3,2,1,0:T(8,128)S(1)}, f32[3,2,8,128]{3,2,1,0:T(8,128)S(1)}, u32[]{:S(2)}, u32[]{:S(2)}) collective-permute-start(f32[3,2,8,128]{3,2,1,0:T(8,128)S(1)} %get-tuple-element.52), channel_id=1, source_target_pairs={{0,28},{4,8},{8,4},{12,16},{16,12},{20,24},{24,20},{28,0},{1,29},{... | collective-permute-start | bytes 73736 | tf_op jit(solution)/shard_map/ppermute | solution.py:582
  48.0 2.2 %all-to-all-done.1.after.slots_in = f32[32,3,4,128]{3,2,1,0:T(4,128)S(1)} async-done(((f32[32,3,4,128]{3,2,1,0:T(4,128)}), f32[32,3,4,128]{3,2,1,0:T(4,128)S(1)}, u32[]{:S(2)}, u32[]{:S(2)}) %all-to-all-start.1) | async-done | bytes 196640 | tf_op jit(solution)/shard_map/all_to_all | solution.py:680
  50.2 1.7 %shard_map.120.cold = bf16[2,768,256]{2,1,0:T(8,128)(2,1)S(1)} custom-call(s32[9]{0:T(128)S(1)} %stack.33.flags, bf16[2,768,256]{2,1,0:T(8,128)(2,1)} %get-tuple-element.49.kept, f32[32,3,4,128]{3,2,1,0:T(4,128)S(1)} %all-to-all-done.1.after.slots_in), custom_call_target="tpu_custom_call" | custom-call | tf_op jit(solution)/shard_map/pallas_call | solution.py:41
  51.9 0.0 collective-permute-done.10.got_0
  51.9 0.0 collective-permute-done.13.got_3
  51.9 2.6 %shard_map.121 = (f32[3,14,8,128]{3,2,1,0:T(8,128)S(1)}, f32[32,1,4,128]{3,2,1,0:T(4,128)}, f32[3,2,8,128]{3,2,1,0:T(8,128)S(1)}, f32[3,2,8,128]{3,2,1,0:T(8,128...) custom-call(s32[9]{0:T(128)S(1)} %stack.33.flags, f32[3,14,8,128]{3,2,1,0:T(8,128)S(1)} %get-tuple-element.50.current, ...), custom_call_target="tpu_custom_call" | custom-call | tf_op jit(solution)/shard_map/pallas_call | solution.py:41
  54.5 3.0 %all-to-all-start.2 = ((f32[32,1,4,128]{3,2,1,0:T(4,128)}), f32[32,1,4,128]{3,2,1,0:T(4,128)S(1)}, u32[]{:S(2)}, u32[]{:S(2)}) async-start(f32[32,1,4,128]{3,2,1,0:T(4,128)} %get-tuple-element.61), calls=%async_computation.2 | async-start | bytes 131072 | tf_op jit(solution)/shard_map/all_to_all | solution.py:680
  57.5 0.3 collective-permute-start.16
  57.8 1.6 %collective-permute-start.17 = (f32[3,3,8,128]{3,2,1,0:T(8,128)S(1)}, f32[3,3,8,128]{3,2,1,0:T(8,128)S(1)}, u32[]{:S(2)}, u32[]{:S(2)}) collective-permute-start(f32[3,3,8,128]{3,2,1,0:T(8,128)S(1)} %get-tuple-element.60), channel_id=1, source_target_pairs={{0,3},{1,2},{2,1},{3,0},{4,7},{5,6},{6,5},{7,4},{8,11},{9,10},{10,... | collective-permute-start | bytes 110600 | tf_op jit(solution)/shard_map/ppermute | solution.py:582
  59.4 1.5 %collective-permute-start.14 = (f32[3,2,8,128]{3,2,1,0:T(8,128)S(1)}, f32[3,2,8,128]{3,2,1,0:T(8,128)S(1)}, u32[]{:S(2)}, u32[]{:S(2)}) collective-permute-start(f32[3,2,8,128]{3,2,1,0:T(8,128)S(1)} %get-tuple-element.57), channel_id=1, source_target_pairs={{0,4},{4,0},{8,12},{12,8},{16,20},{20,16},{24,28},{28,24},{1,5},{5... | collective-permute-start | bytes 73736 | tf_op jit(solution)/shard_map/ppermute | solution.py:581
  60.9 3.3 %collective-permute-start.15 = (f32[3,2,8,128]{3,2,1,0:T(8,128)S(1)}, f32[3,2,8,128]{3,2,1,0:T(8,128)S(1)}, u32[]{:S(2)}, u32[]{:S(2)}) collective-permute-start(f32[3,2,8,128]{3,2,1,0:T(8,128)S(1)} %get-tuple-element.58), channel_id=1, source_target_pairs={{0,28},{4,8},{8,4},{12,16},{16,12},{20,24},{24,20},{28,0},{1,29},{... | collective-permute-start | bytes 73736 | tf_op jit(solution)/shard_map/ppermute | solution.py:582
  64.2 0.0 collective-permute-done.14.got_0
  64.2 3.2 %collective-permute-done.15.got_1 = f32[3,2,8,128]{3,2,1,0:T(8,128)S(1)} collective-permute-done((f32[3,2,8,128]{3,2,1,0:T(8,128)S(1)}, f32[3,2,8,128]{3,2,1,0:T(8,128)S(1)}, u32[]{:S(2)}, u32[]{:S(2)}) %collective-permute-start.15) | collective-permute-done | bytes 24608 | tf_op jit(solution)/shard_map/ppermute | solution.py:582
  67.4 1.4 %shard_map.122 = (f32[3,4,8,128]{3,2,1,0:T(8,128)}, f32[3,4,8,128]{3,2,1,0:T(8,128)}) custom-call(s32[9]{0:T(128)S(1)} %stack.33.flags, f32[3,14,8,128]{3,2,1,0:T(8,128)S(1)} %get-tuple-element.56.current, f32[18,13,8,128]{3,2,1,0:T(8,128)S(1)} %get-tuple-element.42.coeffs, s32[14,8,128]{2,1,0:T(8,128)S(1)} %get-tuple-element.43.index, ...), custom_call_target="tpu_custom_call" | custom-call | tf_op jit(solution)/shard_map/pallas_call | solution.py:41
  (7 shorter events, 0.0 us)
Async XLA Ops:
  0.6 17.7 %copy-start = (f32[32,1024]{1,0:T(8,128)S(1)}, f32[32,1024]{1,0:T(8,128)}, u32[]{:S(2)}) copy-start(f32[32,1024]{1,0:T(8,128)} %cinv.5) | copy-start | bytes 393220
  2.4 8.9 %collective-permute-start = (f32[24,8,128]{2,1,0:T(8,128)S(1)}, f32[24,8,128]{2,1,0:T(8,128)S(1)}, u32[]{:S(2)}, u32[]{:S(2)}) collective-permute-start(f32[24,8,128]{2,1,0:T(8,128)S(1)} %get-tuple-element.33), channel_id=1, source_target_pairs={{0,4},{4,0},{8,12},{12,8},{16,20},{20,16},{24,28},{28,24},{1,5},{5... | collective-permute-start | bytes 294920 | tf_op jit(solution)/shard_map/ppermute | solution.py:581
  5.5 7.3 %collective-permute-start.1 = (f32[24,8,128]{2,1,0:T(8,128)S(1)}, f32[24,8,128]{2,1,0:T(8,128)S(1)}, u32[]{:S(2)}, u32[]{:S(2)}) collective-permute-start(f32[24,8,128]{2,1,0:T(8,128)S(1)} %get-tuple-element.34), channel_id=1, source_target_pairs={{0,28},{4,8},{8,4},{12,16},{16,12},{20,24},{24,20},{28,0},{1,29},{... | collective-permute-start | bytes 294920 | tf_op jit(solution)/shard_map/ppermute | solution.py:582
  9.6 8.7 %collective-permute-start.2 = (f32[176,128]{1,0:T(8,128)S(1)}, f32[176,128]{1,0:T(8,128)S(1)}, u32[]{:S(2)}, u32[]{:S(2)}) collective-permute-start(f32[176,128]{1,0:T(8,128)S(1)} %get-tuple-element.35), channel_id=1, source_target_pairs={{0,1},{1,0},{2,3},{3,2},{4,5},{5,4},{6,7},{7,6},{8,9},{9,8},{10,11... | collective-permute-start | bytes 270344 | tf_op jit(solution)/shard_map/ppermute | solution.py:581
  9.7 8.6 %collective-permute-start.3 = (f32[176,128]{1,0:T(8,128)S(1)}, f32[176,128]{1,0:T(8,128)S(1)}, u32[]{:S(2)}, u32[]{:S(2)}) collective-permute-start(f32[176,128]{1,0:T(8,128)S(1)} %get-tuple-element.36), channel_id=1, source_target_pairs={{0,3},{1,2},{2,1},{3,0},{4,7},{5,6},{6,5},{7,4},{8,11},{9,10},{10,... | collective-permute-start | bytes 270344 | tf_op jit(solution)/shard_map/ppermute | solution.py:582
  13.4 4.9 %collective-permute-start.4 = (f32[64,128]{1,0:T(8,128)S(1)}, f32[64,128]{1,0:T(8,128)S(1)}, u32[]{:S(2)}, u32[]{:S(2)}) collective-permute-start(f32[64,128]{1,0:T(8,128)S(1)} %get-tuple-element.37), channel_id=1, source_target_pairs={{0,1},{1,0},{2,3},{3,2},{4,5},{5,4},{6,7},{7,6},{8,9},{9,8},{10,11... | collective-permute-start | bytes 98312 | tf_op jit(solution)/shard_map/ppermute | solution.py:581
  13.5 4.8 %collective-permute-start.5 = (f32[64,128]{1,0:T(8,128)S(1)}, f32[64,128]{1,0:T(8,128)S(1)}, u32[]{:S(2)}, u32[]{:S(2)}) collective-permute-start(f32[64,128]{1,0:T(8,128)S(1)} %get-tuple-element.38), channel_id=1, source_target_pairs={{0,3},{1,2},{2,1},{3,0},{4,7},{5,6},{6,5},{7,4},{8,11},{9,10},{10,... | collective-permute-start | bytes 98312 | tf_op jit(solution)/shard_map/ppermute | solution.py:582
  21.0 12.9 %all-to-all-start = ((f32[32,3,4,128]{3,2,1,0:T(4,128)}), f32[32,3,4,128]{3,2,1,0:T(4,128)S(1)}, u32[]{:S(2)}, u32[]{:S(2)}) async-start(f32[32,3,4,128]{3,2,1,0:T(4,128)} %get-tuple-element.48), calls=%async_computation | async-start | bytes 393216 | tf_op jit(solution)/shard_map/all_to_all | solution.py:680
  25.0 10.7 %collective-permute-start.8 = (f32[3,3,8,128]{3,2,1,0:T(8,128)S(1)}, f32[3,3,8,128]{3,2,1,0:T(8,128)S(1)}, u32[]{:S(2)}, u32[]{:S(2)}) collective-permute-start(f32[3,3,8,128]{3,2,1,0:T(8,128)S(1)} %get-tuple-element.46), channel_id=1, source_target_pairs={{0,1},{1,0},{2,3},{3,2},{4,5},{5,4},{6,7},{7,6},{8,9},{9,8},{10,11... | collective-permute-start | bytes 110600 | tf_op jit(solution)/shard_map/ppermute | solution.py:581
  25.3 10.4 %collective-permute-start.9 = (f32[3,3,8,128]{3,2,1,0:T(8,128)S(1)}, f32[3,3,8,128]{3,2,1,0:T(8,128)S(1)}, u32[]{:S(2)}, u32[]{:S(2)}) collective-permute-start(f32[3,3,8,128]{3,2,1,0:T(8,128)S(1)} %get-tuple-element.47), channel_id=1, source_target_pairs={{0,3},{1,2},{2,1},{3,0},{4,7},{5,6},{6,5},{7,4},{8,11},{9,10},{10,... | collective-permute-start | bytes 110600 | tf_op jit(solution)/shard_map/ppermute | solution.py:582
  26.9 8.7 %collective-permute-start.6 = (f32[3,2,8,128]{3,2,1,0:T(8,128)S(1)}, f32[3,2,8,128]{3,2,1,0:T(8,128)S(1)}, u32[]{:S(2)}, u32[]{:S(2)}) collective-permute-start(f32[3,2,8,128]{3,2,1,0:T(8,128)S(1)} %get-tuple-element.44), channel_id=1, source_target_pairs={{0,4},{4,0},{8,12},{12,8},{16,20},{20,16},{24,28},{28,24},{1,5},{5... | collective-permute-start | bytes 73736 | tf_op jit(solution)/shard_map/ppermute | solution.py:581
  28.4 7.2 %collective-permute-start.7 = (f32[3,2,8,128]{3,2,1,0:T(8,128)S(1)}, f32[3,2,8,128]{3,2,1,0:T(8,128)S(1)}, u32[]{:S(2)}, u32[]{:S(2)}) collective-permute-start(f32[3,2,8,128]{3,2,1,0:T(8,128)S(1)} %get-tuple-element.45), channel_id=1, source_target_pairs={{0,28},{4,8},{8,4},{12,16},{16,12},{20,24},{24,20},{28,0},{1,29},{... | collective-permute-start | bytes 73736 | tf_op jit(solution)/shard_map/ppermute | solution.py:582
  38.3 11.9 %all-to-all-start.1 = ((f32[32,3,4,128]{3,2,1,0:T(4,128)}), f32[32,3,4,128]{3,2,1,0:T(4,128)S(1)}, u32[]{:S(2)}, u32[]{:S(2)}) async-start(f32[32,3,4,128]{3,2,1,0:T(4,128)} %get-tuple-element.55), calls=%async_computation.1 | async-start | bytes 393216 | tf_op jit(solution)/shard_map/all_to_all | solution.py:680
  41.3 10.7 %collective-permute-start.12 = (f32[3,3,8,128]{3,2,1,0:T(8,128)S(1)}, f32[3,3,8,128]{3,2,1,0:T(8,128)S(1)}, u32[]{:S(2)}, u32[]{:S(2)}) collective-permute-start(f32[3,3,8,128]{3,2,1,0:T(8,128)S(1)} %get-tuple-element.53), channel_id=1, source_target_pairs={{0,1},{1,0},{2,3},{3,2},{4,5},{5,4},{6,7},{7,6},{8,9},{9,8},{10,11... | collective-permute-start | bytes 110600 | tf_op jit(solution)/shard_map/ppermute | solution.py:581
  41.6 10.4 %collective-permute-start.13 = (f32[3,3,8,128]{3,2,1,0:T(8,128)S(1)}, f32[3,3,8,128]{3,2,1,0:T(8,128)S(1)}, u32[]{:S(2)}, u32[]{:S(2)}) collective-permute-start(f32[3,3,8,128]{3,2,1,0:T(8,128)S(1)} %get-tuple-element.54), channel_id=1, source_target_pairs={{0,3},{1,2},{2,1},{3,0},{4,7},{5,6},{6,5},{7,4},{8,11},{9,10},{10,... | collective-permute-start | bytes 110600 | tf_op jit(solution)/shard_map/ppermute | solution.py:582
  43.2 8.7 %collective-permute-start.10 = (f32[3,2,8,128]{3,2,1,0:T(8,128)S(1)}, f32[3,2,8,128]{3,2,1,0:T(8,128)S(1)}, u32[]{:S(2)}, u32[]{:S(2)}) collective-permute-start(f32[3,2,8,128]{3,2,1,0:T(8,128)S(1)} %get-tuple-element.51), channel_id=1, source_target_pairs={{0,4},{4,0},{8,12},{12,8},{16,20},{20,16},{24,28},{28,24},{1,5},{5... | collective-permute-start | bytes 73736 | tf_op jit(solution)/shard_map/ppermute | solution.py:581
  44.7 7.2 %collective-permute-start.11 = (f32[3,2,8,128]{3,2,1,0:T(8,128)S(1)}, f32[3,2,8,128]{3,2,1,0:T(8,128)S(1)}, u32[]{:S(2)}, u32[]{:S(2)}) collective-permute-start(f32[3,2,8,128]{3,2,1,0:T(8,128)S(1)} %get-tuple-element.52), channel_id=1, source_target_pairs={{0,28},{4,8},{8,4},{12,16},{16,12},{20,24},{24,20},{28,0},{1,29},{... | collective-permute-start | bytes 73736 | tf_op jit(solution)/shard_map/ppermute | solution.py:582
  54.5 12.9 %all-to-all-start.2 = ((f32[32,1,4,128]{3,2,1,0:T(4,128)}), f32[32,1,4,128]{3,2,1,0:T(4,128)S(1)}, u32[]{:S(2)}, u32[]{:S(2)}) async-start(f32[32,1,4,128]{3,2,1,0:T(4,128)} %get-tuple-element.61), calls=%async_computation.2 | async-start | bytes 131072 | tf_op jit(solution)/shard_map/all_to_all | solution.py:680
  57.5 9.9 %collective-permute-start.16 = (f32[3,3,8,128]{3,2,1,0:T(8,128)S(1)}, f32[3,3,8,128]{3,2,1,0:T(8,128)S(1)}, u32[]{:S(2)}, u32[]{:S(2)}) collective-permute-start(f32[3,3,8,128]{3,2,1,0:T(8,128)S(1)} %get-tuple-element.59), channel_id=1, source_target_pairs={{0,1},{1,0},{2,3},{3,2},{4,5},{5,4},{6,7},{7,6},{8,9},{9,8},{10,11... | collective-permute-start | bytes 110600 | tf_op jit(solution)/shard_map/ppermute | solution.py:581
  57.8 9.6 %collective-permute-start.17 = (f32[3,3,8,128]{3,2,1,0:T(8,128)S(1)}, f32[3,3,8,128]{3,2,1,0:T(8,128)S(1)}, u32[]{:S(2)}, u32[]{:S(2)}) collective-permute-start(f32[3,3,8,128]{3,2,1,0:T(8,128)S(1)} %get-tuple-element.60), channel_id=1, source_target_pairs={{0,3},{1,2},{2,1},{3,0},{4,7},{5,6},{6,5},{7,4},{8,11},{9,10},{10,... | collective-permute-start | bytes 110600 | tf_op jit(solution)/shard_map/ppermute | solution.py:582
  59.4 4.8 %collective-permute-start.14 = (f32[3,2,8,128]{3,2,1,0:T(8,128)S(1)}, f32[3,2,8,128]{3,2,1,0:T(8,128)S(1)}, u32[]{:S(2)}, u32[]{:S(2)}) collective-permute-start(f32[3,2,8,128]{3,2,1,0:T(8,128)S(1)} %get-tuple-element.57), channel_id=1, source_target_pairs={{0,4},{4,0},{8,12},{12,8},{16,20},{20,16},{24,28},{28,24},{1,5},{5... | collective-permute-start | bytes 73736 | tf_op jit(solution)/shard_map/ppermute | solution.py:581
  60.9 6.5 %collective-permute-start.15 = (f32[3,2,8,128]{3,2,1,0:T(8,128)S(1)}, f32[3,2,8,128]{3,2,1,0:T(8,128)S(1)}, u32[]{:S(2)}, u32[]{:S(2)}) collective-permute-start(f32[3,2,8,128]{3,2,1,0:T(8,128)S(1)} %get-tuple-element.58), channel_id=1, source_target_pairs={{0,28},{4,8},{8,4},{12,16},{16,12},{20,24},{24,20},{28,0},{1,29},{... | collective-permute-start | bytes 73736 | tf_op jit(solution)/shard_map/ppermute | solution.py:582
